TPU v7x, 32 devices: a whole 2x2x4 slice. The times are simulated.
32 devices in a mesh: dp: 8 (over z, x), mp: 4 (over y, core).
Axes of the slice: x: 2, y: 2, z: 4, core: 2. Of those that a mesh axis runs over, the one named last changes fastest.
Arguments:
- patches: bfloat16 [16384, 768], P(('dp', 'mp')), may hold values from -6 to 6
- segment_ids: int32 [16, 1024], P('dp'), may hold values from 0 to 7, never falling along the last dimension, each value on 1 to 256 neighbouring positions
- fill_counts: int32 [16], P('dp'), may hold values from 512 to 1024, as said below
- attn_gain: float32 [768], replicated, may hold values from 0.1 to 1.9
- attn_shift: float32 [768], replicated, may hold values from -3 to 3
- qkv_weight: bfloat16 [3, 768, 768], P(None, None, 'mp'), may hold values from -0.21875 to 0.21875
- qv_bias: bfloat16 [2, 768], P(None, 'mp'), may hold values from -3 to 3
- rel_table: bfloat16 [12, 1024, 1024], P('mp'), may hold values from -4 to 4
- proj_weight: bfloat16 [768, 768], P('mp'), may hold values from -1.5 to 1.5
- proj_bias: bfloat16 [768], replicated, may hold values from -3 to 3
- attn_scale: float32 [768], replicated, may hold values from 0.5 to 2
- mlp_gain: float32 [768], replicated, may hold values from 0.1 to 1.9
- mlp_shift: float32 [768], replicated, may hold values from -3 to 3
- up_weight: bfloat16 [768, 3072], P(None, 'mp'), may hold values from -0.21875 to 0.21875
- up_bias: bfloat16 [3072], P('mp'), may hold values from -3 to 3
- down_weight: bfloat16 [3072, 768], P('mp'), may hold values from -0.109375 to 0.109375
- down_bias: bfloat16 [768], replicated, may hold values from -3 to 3
- mlp_scale: float32 [768], replicated, may hold values from 0.5 to 2
- cotangent: bfloat16 [16384, 768], P(('dp', 'mp')), may hold values from -6 to 6
Outputs:
- layer_out: bfloat16 [16384, 768], P(('dp', 'mp'))
- patch_grad: float32 [16384, 768], P(('dp', 'mp'))
- attn_gain_grad: float32 [768], replicated
- attn_shift_grad: float32 [768], replicated
- qkv_grad: float32 [3, 768, 768], P(None, 'dp', 'mp')
- qv_bias_grad: float32 [2, 768], P(None, 'mp')
- table_grad: float32 [12, 1024, 1024], P('mp', 'dp')
- proj_grad: float32 [768, 768], P('mp', 'dp')
- proj_bias_grad: float32 [768], replicated
- attn_scale_grad: float32 [768], replicated
- mlp_gain_grad: float32 [768], replicated
- mlp_shift_grad: float32 [768], replicated
- up_grad: float32 [768, 3072], P('dp', 'mp')
- up_bias_grad: float32 [3072], P('mp')
- down_grad: float32 [3072, 768], P('mp', 'dp')
- down_bias_grad: float32 [768], replicated
- mlp_scale_grad: float32 [768], replicated
Inputs may be any that keep to these rules, and one draw needn't show every extreme that they name: `segment_ids`: within each sequence the page numbers never fall, and each page holds 1 to 256 patches. `fill_counts`: positions at or past a sequence's count are padding; some sequence is full and some is half full.
All inputs are finite; a program needn't handle non-finite values.
Results may differ from a plain program's by a relative error of at most 0.012.
Values may be sent and summed in bfloat16 or wider, within the bound.
A program may use at most 192 MiB of HBM per device.

v0:
```python
from functools import partial

import jax
import jax.numpy as jnp
from jax import lax
from jax.sharding import PartitionSpec as P

HEAD_DIM = 64


def norm_rows(rows, gain, shift):
    centre = rows - jnp.mean(rows, axis=-1, keepdims=True)
    inv_std = lax.rsqrt(jnp.mean(centre * centre, axis=-1, keepdims=True) + 1e-06)
    normed = centre * inv_std
    return (normed * gain + shift, normed, inv_std)


def norm_back(grad_out, normed, inv_std, gain):
    scaled = grad_out * gain
    inner = (
        scaled
        - jnp.mean(scaled, axis=-1, keepdims=True)
        - normed * jnp.mean(scaled * normed, axis=-1, keepdims=True)
    )
    return (inv_std * inner, jnp.sum(grad_out * normed, axis=0), jnp.sum(grad_out, axis=0))


def gelu_back(pre_act, grad):
    _, pullback = jax.vjp(partial(jax.nn.gelu, approximate=True), pre_act)
    return pullback(grad)[0]


def block_mask(seg_row, fill_one, start, count):
    length = seg_row.shape[0]
    query_pos = start + jnp.arange(count, dtype=jnp.int32)
    key_pos = jnp.arange(length, dtype=jnp.int32)
    seg_query = seg_row[start : start + count]
    valid_query = query_pos < fill_one
    valid_key = key_pos < fill_one
    same = (seg_query[:, None] == seg_row[None, :]) & valid_query[:, None] & valid_key[None, :]
    return same | (query_pos[:, None] == key_pos[None, :])


def block_scores(query_blk, keys_seq, table, start, count):
    raw = jnp.einsum("qhd,khd->hqk", query_blk, keys_seq, preferred_element_type=jnp.float32)
    return raw * 0.125 + table[:, start : start + count, :].astype(jnp.float32)


def attend_sequence(table, items):
    query_seq, keys_seq, values_seq, seg_row, fill_one = items
    length = query_seq.shape[0]
    block = min(512, length)
    contexts = []
    sums = []
    for start in range(0, length, block):
        scores = block_scores(query_seq[start : start + block], keys_seq, table, start, block)
        scores = jnp.where(block_mask(seg_row, fill_one, start, block)[None], scores, -1e30)
        peak = jnp.max(scores, axis=-1, keepdims=True)
        expo = jnp.exp(scores - peak)
        total = jnp.sum(expo, axis=-1, keepdims=True)
        probs = (expo / total).astype(jnp.bfloat16)
        context = jnp.einsum("hqk,khd->qhd", probs, values_seq, preferred_element_type=jnp.float32)
        contexts.append(context.astype(jnp.bfloat16))
        sums.append((peak + jnp.log(total))[..., 0])
    return (jnp.concatenate(contexts, axis=0), jnp.concatenate(sums, axis=1))


def attend_back(table, carry, items):
    query_seq, keys_seq, values_seq, grad_ctx, log_sums, seg_row, fill_one = items
    length = query_seq.shape[0]
    block = min(512, length)
    key_total = jnp.zeros(keys_seq.shape, jnp.float32)
    value_total = jnp.zeros(values_seq.shape, jnp.float32)
    query_grads = []
    for start in range(0, length, block):
        query_blk = query_seq[start : start + block]
        grad_blk = grad_ctx[start : start + block]
        scores = block_scores(query_blk, keys_seq, table, start, block)
        allowed = block_mask(seg_row, fill_one, start, block)[None]
        probs = jnp.where(allowed, jnp.exp(scores - log_sums[:, start : start + block, None]), 0.0)
        grad_probs = jnp.einsum(
            "qhd,khd->hqk", grad_blk, values_seq, preferred_element_type=jnp.float32
        )
        centre = jnp.sum(grad_probs * probs, axis=-1, keepdims=True)
        grad_scores = (probs * (grad_probs - centre)).astype(jnp.bfloat16)
        query_grad = (
            jnp.einsum("hqk,khd->qhd", grad_scores, keys_seq, preferred_element_type=jnp.float32)
            * 0.125
        )
        query_grads.append(query_grad.astype(jnp.bfloat16))
        key_total = (
            key_total
            + jnp.einsum("hqk,qhd->khd", grad_scores, query_blk, preferred_element_type=jnp.float32)
            * 0.125
        )
        value_total = value_total + jnp.einsum(
            "hqk,qhd->khd", probs.astype(jnp.bfloat16), grad_blk, preferred_element_type=jnp.float32
        )
        carry = carry.at[:, start : start + block, :].add(grad_scores.astype(jnp.float32))
    return (
        carry,
        (
            jnp.concatenate(query_grads, axis=0),
            key_total.astype(jnp.bfloat16),
            value_total.astype(jnp.bfloat16),
        ),
    )


def local(
    patches,
    segment_ids,
    fill_counts,
    attn_gain,
    attn_shift,
    qkv_weight,
    qv_bias,
    rel_table,
    proj_weight,
    proj_bias,
    attn_scale,
    mlp_gain,
    mlp_shift,
    up_weight,
    up_bias,
    down_weight,
    down_bias,
    mlp_scale,
    cotangent,
):
    rows_own = patches.shape[0]
    seqs = segment_ids.shape[0]
    length = segment_ids.shape[1]
    local_cols = qkv_weight.shape[2]
    heads_here = local_cols // HEAD_DIM
    shaped = (seqs, length, heads_here, HEAD_DIM)
    inputs = patches.astype(jnp.float32)
    normed_one, hat_one, inv_one = norm_rows(inputs, attn_gain, attn_shift)
    rows_one = lax.all_gather(normed_one.astype(jnp.bfloat16), "mp", axis=0, tiled=True)
    queries = (
        jnp.dot(rows_one, qkv_weight[0], preferred_element_type=jnp.float32)
        + qv_bias[0].astype(jnp.float32)
    ).astype(jnp.bfloat16)
    keys_all = jnp.dot(rows_one, qkv_weight[1], preferred_element_type=jnp.float32).astype(
        jnp.bfloat16
    )
    values_all = (
        jnp.dot(rows_one, qkv_weight[2], preferred_element_type=jnp.float32)
        + qv_bias[1].astype(jnp.float32)
    ).astype(jnp.bfloat16)
    query_four = queries.reshape(shaped)
    keys_four = keys_all.reshape(shaped)
    values_four = values_all.reshape(shaped)
    contexts, log_sums = lax.map(
        partial(attend_sequence, rel_table),
        (query_four, keys_four, values_four, segment_ids, fill_counts),
    )
    context = contexts.reshape(seqs * length, local_cols)
    attn_out = lax.psum_scatter(
        jnp.dot(
            lax.slice_in_dim(context, 0, rows_own * lax.axis_size("mp"), axis=0),
            proj_weight,
            preferred_element_type=jnp.float32,
        ),
        "mp",
        scatter_dimension=0,
        tiled=True,
    ) + proj_bias.astype(jnp.float32)
    middle = inputs + attn_scale * attn_out
    normed_two, hat_two, inv_two = norm_rows(middle, mlp_gain, mlp_shift)
    normed_low = normed_two.astype(jnp.bfloat16)
    grad_top = cotangent.astype(jnp.float32)
    rows_two = lax.all_gather(normed_low, "mp", axis=0, tiled=True)
    pre_act = jnp.dot(rows_two, up_weight, preferred_element_type=jnp.float32) + up_bias.astype(
        jnp.float32
    )
    hidden = jax.nn.gelu(pre_act, approximate=True).astype(jnp.bfloat16)
    mlp_out = lax.psum_scatter(
        jnp.dot(
            lax.slice_in_dim(hidden, 0, lax.axis_size("mp") * rows_own, axis=0),
            down_weight,
            preferred_element_type=jnp.float32,
        ).astype(jnp.bfloat16),
        "mp",
        scatter_dimension=0,
        tiled=True,
    ).astype(jnp.float32) + down_bias.astype(jnp.float32)
    layer_out = (middle + mlp_scale * mlp_out).astype(jnp.bfloat16)
    grad_mlp = (grad_top * mlp_scale).astype(jnp.bfloat16)
    grad_rows = lax.all_gather(grad_mlp, "mp", axis=0, tiled=True)
    grad_hidden = jnp.dot(grad_rows, down_weight.T, preferred_element_type=jnp.float32)
    grad_pre = gelu_back(pre_act, grad_hidden).astype(jnp.bfloat16)
    up_local = jnp.dot(rows_two.T, grad_pre, preferred_element_type=jnp.float32)
    down_local = jnp.dot(hidden.T, grad_rows, preferred_element_type=jnp.float32)
    up_bias_local = jnp.sum(grad_pre.astype(jnp.float32), axis=0)
    grad_norm_two = lax.psum_scatter(
        jnp.dot(
            lax.slice_in_dim(grad_pre, 0, rows_own * lax.axis_size("mp"), axis=0),
            up_weight.T,
            preferred_element_type=jnp.float32,
        ),
        "mp",
        scatter_dimension=0,
        tiled=True,
    )
    scale_two_grad = jnp.sum(grad_top * mlp_out, axis=0)
    down_bias_grad = jnp.sum(grad_mlp.astype(jnp.float32), axis=0)
    back_two, gain_two_grad, shift_two_grad = norm_back(grad_norm_two, hat_two, inv_two, mlp_gain)
    grad_middle = grad_top + back_two
    grad_attn = (grad_middle * attn_scale).astype(jnp.bfloat16)
    scale_one_grad = jnp.sum(grad_middle * attn_out, axis=0)
    proj_bias_grad = jnp.sum(grad_attn.astype(jnp.float32), axis=0)
    attn_grad_rows = lax.all_gather(grad_attn, "mp", axis=0, tiled=True)
    proj_local = jnp.dot(context.T, attn_grad_rows, preferred_element_type=jnp.float32)
    grad_context = jnp.dot(
        attn_grad_rows, proj_weight.T, preferred_element_type=jnp.float32
    ).astype(jnp.bfloat16)
    table_zero = jnp.zeros(rel_table.shape, jnp.float32)
    table_local, (grad_q, grad_k, grad_v) = lax.scan(
        partial(attend_back, rel_table),
        table_zero,
        (
            query_four,
            keys_four,
            values_four,
            grad_context.reshape(shaped),
            log_sums,
            segment_ids,
            fill_counts,
        ),
    )
    grad_q = grad_q.reshape(seqs * length, local_cols)
    grad_k = grad_k.reshape(seqs * length, local_cols)
    grad_v = grad_v.reshape(seqs * length, local_cols)
    qkv_local = jnp.stack(
        [
            jnp.dot(rows_one.T, grad_q, preferred_element_type=jnp.float32),
            jnp.dot(rows_one.T, grad_k, preferred_element_type=jnp.float32),
            jnp.dot(rows_one.T, grad_v, preferred_element_type=jnp.float32),
        ]
    )
    qv_bias_local = jnp.stack(
        [jnp.sum(grad_q.astype(jnp.float32), axis=0), jnp.sum(grad_v.astype(jnp.float32), axis=0)]
    )
    total = jnp.dot(
        lax.slice_in_dim(grad_q, 0, rows_own * lax.axis_size("mp"), axis=0),
        qkv_weight[0].T,
        preferred_element_type=jnp.float32,
    )
    total = total + jnp.dot(
        lax.slice_in_dim(grad_k, 0, rows_own * lax.axis_size("mp"), axis=0),
        qkv_weight[1].T,
        preferred_element_type=jnp.float32,
    )
    grad_norm_one = lax.psum_scatter(
        total
        + jnp.dot(
            lax.slice_in_dim(grad_v, 0, rows_own * lax.axis_size("mp"), axis=0),
            qkv_weight[2].T,
            preferred_element_type=jnp.float32,
        ),
        "mp",
        scatter_dimension=0,
        tiled=True,
    )
    back_one, gain_one_grad, shift_one_grad = norm_back(grad_norm_one, hat_one, inv_one, attn_gain)
    patch_grad = grad_middle + back_one
    qkv_grad, proj_grad, up_grad, down_grad, table_grad = (
        lax.psum_scatter(qkv_local, "dp", scatter_dimension=1, tiled=True),
        lax.psum_scatter(proj_local, "dp", scatter_dimension=1, tiled=True),
        lax.psum_scatter(up_local, "dp", scatter_dimension=0, tiled=True),
        lax.psum_scatter(down_local, "dp", scatter_dimension=1, tiled=True),
        lax.psum_scatter(table_local, "dp", scatter_dimension=1, tiled=True),
    )
    small = lax.psum(
        jnp.stack(
            [
                gain_one_grad,
                shift_one_grad,
                proj_bias_grad,
                scale_one_grad,
                gain_two_grad,
                shift_two_grad,
                down_bias_grad,
                scale_two_grad,
            ]
        ),
        ("dp", "mp"),
    )
    qv_bias_grad, up_bias_grad = lax.psum((qv_bias_local, up_bias_local), "dp")
    return (
        layer_out,
        patch_grad,
        small[0],
        small[1],
        qkv_grad,
        qv_bias_grad,
        table_grad,
        proj_grad,
        small[2],
        small[3],
        small[4],
        small[5],
        up_grad,
        up_bias_grad,
        down_grad,
        small[6],
        small[7],
    )


def solution(mesh):
    placed = (
        P(("dp", "mp"), None),
        P("dp", None),
        P("dp"),
        P(),
        P(),
        P(None, None, "mp"),
        P(None, "mp"),
        P("mp", None, None),
        P("mp", None),
        P(),
        P(),
        P(),
        P(),
        P(None, "mp"),
        P("mp"),
        P("mp", None),
        P(),
        P(),
        P(("dp", "mp"), None),
    )
    return jax.shard_map(
        local,
        mesh=mesh,
        in_specs=placed,
        out_specs=(
            P(("dp", "mp"), None),
            P(("dp", "mp"), None),
            P(),
            P(),
            P(None, "dp", "mp"),
            P(None, "mp"),
            P("mp", "dp", None),
            P("mp", "dp"),
            P(),
            P(),
            P(),
            P(),
            P("dp", "mp"),
            P("mp"),
            P("mp", "dp"),
            P(),
            P(),
        ),
        check_vma=False,
    )
```

profile of v0, /device:TPU:0, one launch (start us, length us, event | category | flops | bytes accessed | tf_op | source)
XLA Modules:
  0.0 977.0 jit_solution(12218697017338891953)
XLA Ops:
  12.7 31.3 %all-gather.5.cloned.1.call-done = bf16[2048,768]{1,0:T(8,128)(2,1)} async-done(((bf16[512,768]{1,0:T(8,128)(2,1)}), bf16[2048,768]{1,0:T(8,128)(2,1)}) %all-gather.5.cloned.1.call-update) | async-done | bytes 3145744 | tf_op jit(solution)/shard_map/all_gather | solution.py:139
  44.0 3.1 fusion.85
  47.9 3.1 fusion.84
  51.8 3.1 convolution_convert_fusion.2
  58.7 34.6 %while.32 = (s32[]{:T(128)}, bf16[2,1024,3,64]{1,3,2,0:T(8,128)(2,1)}, f32[2,3,1024]{2,1,0:T(4,128)}, bf16[2,1024,3,64]{1,3,2,0:T(8,128)(2,1)S(1)}, s32[2,1024]{...) while((s32[]{:T(128)}, ...), condition=%wide.region_7.8_spmd, body=%wide.region_2.7_spmd.sunk | while | flops 842992640 | bytes 74619672 | solution.py:154
  62.4 3.7 fusion.197
  79.6 3.7 fusion.197
  93.3 2.5 copy.59
  97.0 3.7 fusion.123
  101.4 58.3 %reduce-scatter.14.cloned.1.call-done = f32[512,768]{1,0:T(8,128)} async-done(((f32[2048,768]{1,0:T(8,128)}), f32[512,768]{1,0:T(8,128)}) %reduce-scatter.14.cloned.1.call-update) | async-done | bytes 1572880 | tf_op jit(solution)/shard_map/reduce_scatter | solution.py:159
  164.5 2.8 convert_reduce_fusion.4
  169.1 24.1 %all-gather.7.cloned.1.call-done = bf16[2048,768]{1,0:T(8,128)(2,1)} async-done(((bf16[512,768]{1,0:T(8,128)(2,1)}), bf16[2048,768]{1,0:T(8,128)(2,1)}) %all-gather.7.cloned.1.call-update) | async-done | bytes 3145744 | tf_op jit(solution)/shard_map/all_gather | solution.py:173
  193.1 7.5 fusion.124
  200.6 23.0 %all-gather.9.cloned.1.call-done = bf16[2048,768]{1,0:T(8,128)(2,1)} async-done(((bf16[512,768]{1,0:T(8,128)(2,1)}), bf16[2048,768]{1,0:T(8,128)(2,1)}) %all-gather.9.cloned.1.call-update) | async-done | bytes 3145744 | tf_op jit(solution)/shard_map/all_gather | solution.py:190
  223.7 12.4 %convert_reduce_fusion = (f32[768]{0:T(1024)}, bf16[2048,768]{1,0:T(8,128)(2,1)S(1)}, bf16[2048,768]{1,0:T(8,128)(2,1)}) fusion(f32[2048,768]{1,0:T(8,128)} %fusion.124, f32[768]{0:T(1024)} %convert_element_type.190, bf16[2048,768]{1,0:T(8,128)(2,1)} %all-gather.9.cloned.1.call-done, bf16[768,768]{1,0:T(8,128)(2,1)S(1)} %copy-done), kind=kOutput, calls=%fused_computation.123 | convolution fusion | flops 2455239936 | bytes 16914432 | tf_op jit(solution)/shard_map/dot_general | solution.py:191
  237.8 4.6 fusion.125
  242.4 6.5 convolution_convert_fusion
  249.6 51.7 %reduce-scatter.18.cloned.1.call-done = f32[512,768]{1,0:T(8,128)} async-done(((f32[2048,768]{1,0:T(8,128)}), f32[512,768]{1,0:T(8,128)}) %reduce-scatter.18.cloned.1.call-update) | async-done | bytes 1572880 | tf_op jit(solution)/shard_map/reduce_scatter | solution.py:196
  301.4 2.7 multiply_reduce_fusion.2
  304.1 37.6 %reduce-scatter.16.cloned.1.call-done = bf16[512,768]{1,0:T(8,128)(2,1)} async-done(((bf16[2048,768]{1,0:T(8,128)(2,1)}), bf16[512,768]{1,0:T(8,128)(2,1)}) %reduce-scatter.16.cloned.1.call-update) | async-done | bytes 786448 | tf_op jit(solution)/shard_map/reduce_scatter | solution.py:178
  341.7 4.1 multiply_reduce_fusion.3
  348.6 28.6 %all-gather.11.cloned.1.call-done = bf16[2048,768]{1,0:T(8,128)(2,1)} async-done(((bf16[512,768]{1,0:T(8,128)(2,1)}), bf16[2048,768]{1,0:T(8,128)(2,1)}) %all-gather.11.cloned.1.call-update) | async-done | bytes 3145744 | tf_op jit(solution)/shard_map/all_gather | solution.py:213
  377.2 3.1 convolution_convert_fusion.1
  381.1 4.1 convolution_bitcast_fusion
  388.2 6.2 broadcast_in_dim.135
  394.4 72.5 %while.33 = (s32[]{:T(128)}, f32[3,1024,1024]{2,1,0:T(8,128)}, bf16[2,1024,3,64]{1,3,2,0:T(8,128)(2,1)}, bf16[2,1024,3,64]{1,3,2,0:T(8,128)(2,1)}, bf16[2,1024,3...) while((s32[]{:T(128)}, f32[3,1024,1024]{2,1,0:T(8,128)}, ...), condition=%wide.region_18.19_spmd, body=%wide.region_15.18_spmd.sunk | while | flops 2061565952 | bytes 177995760 | solution.py:219
  398.9 4.2 exponential_select_fusion.4
  408.1 3.6 multiply_reduce_fusion.10
  411.7 7.7 add_dynamic-update-slice_fusion.2
  419.5 5.1 fusion.218
  435.1 4.2 exponential_select_fusion.4
  444.3 3.6 multiply_reduce_fusion.10
  448.0 7.5 add_dynamic-update-slice_fusion.2
  455.5 5.0 fusion.218
  475.1 4.2 copy.68
  479.3 4.7 reshape.571
  487.2 3.7 add_add_fusion
  491.0 7.1 fusion.126
  498.4 7.0 fusion.127
  510.9 22.3 %all-reduce = (f32[2,192]{1,0:T(2,128)}, f32[768]{0:T(1024)}) all-reduce(f32[2,192]{1,0:T(2,128)S(1)} %pad_maximum_fusion.1, f32[768]{0:T(1024)S(1)} %copy-done.46), channel_id=1, replica_groups=mesh['dp'=8,'mp'=4] {'dp'}, use_global_device_ids=true, to_apply=%region_34.35 | all-reduce | flops 1152 | bytes 9216 | tf_op jit(solution)/shard_map/psum | solution.py:290
  534.8 16.9 %reduce-scatter.28.cloned.1.call-done = f32[96,576]{1,0:T(8,128)} async-done(((f32[768,576]{1,0:T(8,128)}), f32[96,576]{1,0:T(8,128)}) %reduce-scatter.28.cloned.1.call-update) | async-done | bytes 221200
  553.6 58.4 %reduce-scatter.20.cloned.1.call-done = f32[512,768]{1,0:T(8,128)} async-done(((f32[2048,768]{1,0:T(8,128)}), f32[512,768]{1,0:T(8,128)}) %reduce-scatter.20.cloned.1.call-update) | async-done | bytes 1572880 | tf_op jit(solution)/shard_map/reduce_scatter | solution.py:255
  612.0 2.8 fusion.98
  617.4 40.7 %psum.21 = f32[8,768]{1,0:T(8,128)} all-reduce(f32[8,768]{1,0:T(8,128)} %stack.56), channel_id=1, replica_groups=mesh['dp'=8,'mp'=4] {'dp','mp'}, use_global_device_ids=true, to_apply=%region_30.31 | all-reduce | flops 6144 | bytes 49152 | tf_op jit(solution)/shard_map/psum | solution.py:275
  661.2 3.1 fusion.97
  664.3 21.9 %reduce-scatter.24.cloned.1.call-done = f32[96,768]{1,0:T(8,128)} async-done(((f32[768,768]{1,0:T(8,128)}), f32[96,768]{1,0:T(8,128)}) %reduce-scatter.24.cloned.1.call-update) | async-done | bytes 294928 | tf_op jit(solution)/shard_map/reduce_scatter | solution.py:271
  686.2 72.7 %reduce-scatter.26.cloned.1.call-done = f32[768,96]{0,1:T(8,128)} async-done(((f32[768,768]{0,1:T(8,128)}), f32[768,96]{0,1:T(8,128)}) %reduce-scatter.26.cloned.1.call-update) | async-done | bytes 294928 | tf_op jit(solution)/shard_map/reduce_scatter | solution.py:272
  758.9 211.3 %reduce-scatter.22.cloned.1.call-done = f32[3,128,1024]{2,1,0:T(8,128)} async-done(((f32[3,1024,1024]{2,1,0:T(8,128)}), f32[3,128,1024]{2,1,0:T(8,128)}) %reduce-scatter.22.cloned.1.call-update) | async-done | bytes 1572880 | tf_op jit(solution)/shard_map/reduce_scatter | solution.py:273
  (303 shorter events, 111.8 us)
Async XLA Ops:
  7.2 216.5 %copy-start = (bf16[768,768]{1,0:T(8,128)(2,1)S(1)}, bf16[768,768]{1,0:T(8,128)(2,1)}, u32[]{:S(2)}) copy-start(bf16[768,768]{1,0:T(8,128)(2,1)} %param.42) | copy-start | bytes 3538948
  7.2 5.5 copy-start.47
  7.2 36.8 %all-gather.5.cloned.1.call-start = ((), (), s32[]{:S(2)}) async-start(), calls=%async_computation.9 | async-start | bytes 3932160 | tf_op jit(solution)/shard_map/all_gather | solution.py:139
  8.7 35.3 %copy-start.28 = (f32[512]{0:T(512)}, f32[512]{0:T(512)S(1)}, u32[]{:S(2)}) copy-start(f32[512]{0:T(512)S(1)} %broadcast_multiply_fusion.5) | copy-start | bytes 6148
  10.2 33.8 %copy-start.34 = (f32[512]{0:T(512)}, f32[512]{0:T(512)S(1)}, u32[]{:S(2)}) copy-start(f32[512]{0:T(512)S(1)} %add_rsqrt_fusion.1) | copy-start | bytes 6148
  12.6 147.1 %reduce-scatter.14.cloned.1.call-start = ((), (), s32[]{:S(2)}) async-start(), calls=%async_computation.10 | async-start | bytes 7864320 | tf_op jit(solution)/shard_map/reduce_scatter | solution.py:159
  54.9 3.8 copy-start.25
  54.9 3.8 copy-start.51
  93.3 7.4 copy-start.4
  93.3 7.4 copy-start.8
  93.3 3.7 copy-start.26
  100.7 61.9 %copy-start.30 = (f32[768]{0:T(1024)S(1)}, f32[768]{0:T(1024)}, u32[]{:S(2)}) copy-start(f32[768]{0:T(1024)} %param.38) | copy-start | bytes 9220
  100.7 92.4 %all-gather.7.cloned.1.call-start = ((), (), s32[]{:S(2)}) async-start(), calls=%async_computation.11 | async-start | bytes 3932160 | tf_op jit(solution)/shard_map/all_gather | solution.py:173
  101.4 60.3 %copy-start.32 = (f32[768]{0:T(1024)}, f32[768]{0:T(1024)S(1)}, u32[]{:S(2)}) copy-start(f32[768]{0:T(1024)S(1)} %convert_element_type.188) | copy-start | bytes 9220
  164.5 59.2 %all-gather.9.cloned.1.call-start = ((), (), s32[]{:S(2)}) async-start(), calls=%async_computation.13 | async-start | bytes 3932160 | tf_op jit(solution)/shard_map/all_gather | solution.py:190
  167.4 134.0 %reduce-scatter.18.cloned.1.call-start = ((), (), s32[]{:S(2)}) async-start(), calls=%async_computation.14 | async-start | bytes 7864320 | tf_op jit(solution)/shard_map/reduce_scatter | solution.py:196
  223.7 14.1 %copy-start.50 = (bf16[768,768]{1,0:T(8,128)(2,1)S(1)}, bf16[768,768]{1,0:T(8,128)(2,1)}, u32[]{:S(2)}) copy-start(bf16[768,768]{1,0:T(8,128)(2,1)} %param.40) | copy-start | bytes 3538948
  242.4 99.3 %reduce-scatter.16.cloned.1.call-start = ((), (), s32[]{:S(2)}) async-start(), calls=%async_computation.12 | async-start | bytes 3932160 | tf_op jit(solution)/shard_map/reduce_scatter | solution.py:178
  248.9 52.4 %copy-start.37 = (f32[512]{0:T(512)S(1)}, f32[512]{0:T(512)}, u32[]{:S(2)}) copy-start(f32[512]{0:T(512)} %copy-done.36) | copy-start | bytes 6148
  249.0 92.7 %copy-start.18 = (bf16[512,768]{1,0:T(8,128)(2,1)S(1)}, bf16[512,768]{1,0:T(8,128)(2,1)}, u32[]{:S(2)}) copy-start(bf16[512,768]{1,0:T(8,128)(2,1)} %param.45) | copy-start | bytes 2359300
  249.0 92.7 %copy-start.33 = (f32[768]{0:T(1024)S(1)}, f32[768]{0:T(1024)}, u32[]{:S(2)}) copy-start(f32[768]{0:T(1024)} %copy-done.32) | copy-start | bytes 9220
  249.0 92.7 %copy-start.38 = (f32[768]{0:T(1024)S(1)}, f32[768]{0:T(1024)}, u32[]{:S(2)}) copy-start(f32[768]{0:T(1024)} %param.44) | copy-start | bytes 9220
  249.0 128.2 %all-gather.11.cloned.1.call-start = ((), (), s32[]{:S(2)}) async-start(), calls=%async_computation.15 | async-start | bytes 3932160 | tf_op jit(solution)/shard_map/all_gather | solution.py:213
  341.7 5.2 copy-start.39
  345.7 31.5 %copy-start.27 = (bf16[192,768]{1,0:T(8,128)(2,1)S(1)}, bf16[192,768]{1,0:T(8,128)(2,1)}, u32[]{:S(2)}) copy-start(bf16[192,768]{1,0:T(8,128)(2,1)} %param.35) | copy-start | bytes 884740
  348.5 184.6 %reduce-scatter.30.cloned.1.call-start = ((), (), s32[]{:S(2)}) async-start(), calls=%async_computation.21 | async-start | bytes 884736
  348.6 32.5 %copy-start.17 = (bf16[24,8,2,1024]{3,1,2,0:T(8,128)(2,1)S(1)}, bf16[24,8,2,1024]{3,1,2,0:T(8,128)(2,1)}, u32[]{:S(2)}) copy-start(bf16[24,8,2,1024]{3,1,2,0:T(8,128)(2,1)} %copy-done.16) | copy-start | bytes 2359300
  385.2 166.5 %reduce-scatter.28.cloned.1.call-start = ((), (), s32[]{:S(2)}) async-start(), calls=%async_computation.20 | async-start | bytes 2211840
  388.2 6.2 copy-start.5
  388.2 6.2 copy-start.52
  397.3 5.8 slice-start.2
  398.9 4.2 copy-start.9
  398.9 4.2 slice-start.3
  433.5 5.8 slice-start.2
  435.1 4.2 copy-start.9
  435.1 4.2 slice-start.3
  484.0 128.0 %reduce-scatter.20.cloned.1.call-start = ((), (), s32[]{:S(2)}) async-start(), calls=%async_computation.16 | async-start | bytes 7864320 | tf_op jit(solution)/shard_map/reduce_scatter | solution.py:255
  490.9 195.3 %reduce-scatter.24.cloned.1.call-start = ((), (), s32[]{:S(2)}) async-start(), calls=%async_computation.18 | async-start | bytes 2654208 | tf_op jit(solution)/shard_map/reduce_scatter | solution.py:271
  498.1 260.9 %reduce-scatter.26.cloned.1.call-start = ((), (), s32[]{:S(2)}) async-start(), calls=%async_computation.19 | async-start | bytes 2654208 | tf_op jit(solution)/shard_map/reduce_scatter | solution.py:272
  505.4 464.8 %reduce-scatter.22.cloned.1.call-start = ((), (), s32[]{:S(2)}) async-start(), calls=%async_computation.17 | async-start | bytes 14155776 | tf_op jit(solution)/shard_map/reduce_scatter | solution.py:273
  505.5 3.6 copy-start.12
  505.5 5.3 copy-start.46
  506.1 105.8 %copy-start.3 = (bf16[512,768]{1,0:T(8,128)(2,1)S(1)}, bf16[512,768]{1,0:T(8,128)(2,1)}, u32[]{:S(2)}) copy-start(bf16[512,768]{1,0:T(8,128)(2,1)} %param.27) | copy-start | bytes 2359300
  506.2 105.8 %copy-start.29 = (f32[512]{0:T(512)S(1)}, f32[512]{0:T(512)}, u32[]{:S(2)}) copy-start(f32[512]{0:T(512)} %copy-done.28) | copy-start | bytes 6148
  506.2 105.8 %copy-start.31 = (f32[768]{0:T(1024)S(1)}, f32[768]{0:T(1024)}, u32[]{:S(2)}) copy-start(f32[768]{0:T(1024)} %param.30) | copy-start | bytes 9220
  506.2 105.8 %copy-start.35 = (f32[512]{0:T(512)S(1)}, f32[512]{0:T(512)}, u32[]{:S(2)}) copy-start(f32[512]{0:T(512)} %copy-done.34) | copy-start | bytes 6148
  506.2 155.0 %copy-start.7 = (f32[512,768]{1,0:T(8,128)S(1)}, f32[512,768]{1,0:T(8,128)}, u32[]{:S(2)}) copy-start(f32[512,768]{1,0:T(8,128)} %copy-done.6) | copy-start | bytes 4718596
  612.0 358.2 %copy-start.1 = (bf16[768,768]{1,0:T(8,128)(2,1)S(1)}, bf16[768,768]{1,0:T(8,128)(2,1)}, u32[]{:S(2)}) copy-start(bf16[768,768]{1,0:T(8,128)(2,1)} %param.42) | copy-start | bytes 3538948
  (36 other events, 54.9 us)
Sparse Core Ops, SparseCore 0:
  12.7 31.2 all-gather.4
  100.8 58.8 reduce-scatter.13
  164.6 28.4 all-gather.6
  195.1 28.4 all-gather.8
  242.5 58.8 reduce-scatter.17
  303.7 37.8 reduce-scatter.15
  348.7 28.4 all-gather.10
  385.3 63.2 reduce-scatter.29
  484.1 67.5 reduce-scatter.27
  554.1 57.8 reduce-scatter.19
  616.0 70.1 reduce-scatter.23
  690.1 68.7 reduce-scatter.25
  763.1 207.0 reduce-scatter.21
where the time goes:
time: 983 us; the launch traced here: 977 us
  waiting for transfers between devices  637 us (65%)
  matrix products  124 us (13%)
  other arithmetic  76.2 us (8%)
  blocking collectives  63 us (6%)
  local copies, waits for them, and re-layouts  60 us (6%)
  between operations  14.8 us (2%)
    reduce_scatter x1, waiting for transfers between devices, local(): lax.psum_scatter(table_local, 'dp', scatter_dimension=1, tiled=True)  211 us
    reduce_scatter x1, waiting for transfers between devices, local(): lax.psum_scatter(down_local, 'dp', scatter_dimension=1, tiled=True)  72.7 us
    reduce_scatter x1, waiting for transfers between devices, local(): lax.psum_scatter(total + jnp.dot(lax.slice_in_dim(grad_v, 0, rows_own * l...  58.4 us
    reduce_scatter x1, waiting for transfers between devices, local(): lax.psum_scatter(jnp.dot(lax.slice_in_dim(context, 0, rows_own * lax.axis...  58.3 us
    reduce_scatter x1, waiting for transfers between devices, local(): lax.psum_scatter(jnp.dot(lax.slice_in_dim(grad_pre, 0, rows_own * lax.axi...  51.7 us
    psum x1, blocking collectives, local(): lax.psum(jnp.stack([gain_one_grad, shift_one_grad, proj_bias_grad, scale_...  40.7 us
    reduce_scatter x1, waiting for transfers between devices, local(): lax.psum_scatter(jnp.dot(lax.slice_in_dim(hidden, 0, lax.axis_size('mp')...  37.6 us
    all_gather x1, waiting for transfers between devices, local(): lax.all_gather(normed_one.astype(jnp.bfloat16), 'mp', axis=0, tiled=True)  31.3 us
  transfers between devices with their start and end apart: 13, of which 12 were waited for; matrix products, arithmetic and copies ran while one was open for 16% of the time, Pallas kernels for 0%

commit v1 on v0

v1 whole, which is shorter than its diff:
```python
from functools import partial

import jax
import jax.numpy as jnp
from jax import lax
from jax.experimental import pallas as pl
from jax.experimental.pallas import tpu as pltpu
from jax.sharding import PartitionSpec as P

HEAD_DIM = 64
BLOCK = 256
GROUP = 128
PAGE_MOST = 256
BF = jnp.bfloat16
F32 = jnp.float32
MESH = pl.DeviceIdType.MESH
VMEM_MOST = 60 * 1024 * 1024
NT = (((1,), (1,)), ((), ()))
TN = (((0,), (0,)), ((), ()))


def vmem():
    return pl.BlockSpec(memory_space=pltpu.VMEM)


def dot(a, b):
    return jnp.dot(a, b, preferred_element_type=F32)


def dot_nt(a, b):
    return lax.dot_general(a, b, NT, preferred_element_type=F32)


def dot_tn(a, b):
    return lax.dot_general(a, b, TN, preferred_element_type=F32)


def norm_rows(rows, gain, shift):
    centre = rows - jnp.mean(rows, axis=-1, keepdims=True)
    inv_std = lax.rsqrt(jnp.mean(centre * centre, axis=-1, keepdims=True) + 1e-06)
    normed = centre * inv_std
    return (normed * gain + shift, normed, inv_std)


def norm_back(grad_out, normed, inv_std, gain):
    scaled = grad_out * gain
    inner = (
        scaled
        - jnp.mean(scaled, axis=-1, keepdims=True)
        - normed * jnp.mean(scaled * normed, axis=-1, keepdims=True)
    )
    return (inv_std * inner, jnp.sum(grad_out * normed, axis=0), jnp.sum(grad_out, axis=0))


def gelu_back(pre_act, grad):
    _, pullback = jax.vjp(partial(jax.nn.gelu, approximate=True), pre_act)
    return pullback(grad)[0]


def window(index, length):
    width = min(length, BLOCK + 2 * PAGE_MOST)
    start = jnp.clip(index * BLOCK - PAGE_MOST, 0, length - width)
    return pl.multiple_of(start, 128), width


def band_window(group, length):
    wide = min(length, GROUP + 2 * PAGE_MOST)
    start = jnp.clip(group * GROUP - PAGE_MOST, 0, length - wide)
    return pl.multiple_of(start, 128), wide


def head_lanes(head, cols):
    return lax.broadcasted_iota(jnp.int32, (1, cols), 1) // HEAD_DIM == head


def id_columns(ids_ref, cols_ref, seqs, length):
    for s in range(seqs):
        wide = jnp.broadcast_to(ids_ref[s : s + 1, :], (128, length))
        cols_ref[s * length : (s + 1) * length, :] = wide.T


def attend_body(q_ref, k_ref, v_ref, table_ref, ids_ref, cols_ref, ctx_ref, lse_ref, length, step, heads):
    cols = q_ref.shape[1]
    blocks = length // BLOCK
    seq, index = step // blocks, step % blocks
    base = seq * length
    start, width = window(index, length)
    rows = pl.ds(pl.multiple_of(base + index * BLOCK, BLOCK), BLOCK)
    keys_at = pl.ds(pl.multiple_of(base + start, 128), width)
    query = q_ref[rows, :]
    keys = k_ref[keys_at, :]
    values = v_ref[keys_at, :]
    same = cols_ref[rows, 0:1] == ids_ref[pl.ds(seq, 1), pl.ds(start, width)]
    context = jnp.zeros((BLOCK, cols), F32)
    sums = jnp.zeros((BLOCK, 128), F32)
    lane = lax.broadcasted_iota(jnp.int32, (1, 128), 1)
    for head in range(heads):
        mine = head_lanes(head, cols)
        scores = dot_nt(jnp.where(mine, query, 0), keys)
        bias = table_ref[head, pl.ds(pl.multiple_of(index * BLOCK, BLOCK), BLOCK), pl.ds(start, width)]
        scores = jnp.where(same, scores + bias.astype(F32), -1e30)
        peak = jnp.max(scores, axis=-1, keepdims=True)
        expo = jnp.exp(scores - peak)
        total = jnp.sum(expo, axis=-1, keepdims=True)
        part = dot(expo.astype(BF), values) * (1.0 / total)
        context = jnp.where(mine, part, context)
        sums = jnp.where(lane == head, peak + jnp.log(total), sums)
    ctx_ref[rows, :] = context.astype(BF)
    lse_ref[rows, :] = sums


def attend_kernel(seqs, length, heads, q_ref, k_ref, v_ref, table_ref, ids_ref, ctx_ref, lse_ref, cols_ref):
    id_columns(ids_ref, cols_ref, seqs, length)

    def step(i, _):
        attend_body(q_ref, k_ref, v_ref, table_ref, ids_ref, cols_ref, ctx_ref, lse_ref, length, i, heads)
        return 0

    lax.fori_loop(0, seqs * (length // BLOCK), step, 0)


def attend(q, k, v, table, ids):
    seqs, length = ids.shape
    rows, cols = q.shape
    heads = cols // HEAD_DIM
    return pl.pallas_call(
        partial(attend_kernel, seqs, length, heads),
        out_shape=(jax.ShapeDtypeStruct((rows, cols), BF), jax.ShapeDtypeStruct((rows, 128), F32)),
        in_specs=[vmem()] * 5,
        out_specs=(vmem(), vmem()),
        scratch_shapes=[pltpu.VMEM((rows, 128), F32)],
        compiler_params=pltpu.CompilerParams(vmem_limit_bytes=VMEM_MOST),
        name="attend",
    )(q, k, v, table, ids)


def attend_back_kernel(
    seqs, length, heads,
    q_ref, k_ref, v_ref, g_ref, lse_ref, table_ref, ids_ref,
    dq_ref, dk_ref, dv_ref, band_ref,
    cols_ref, qt_ref, gt_ref, dkt_ref, dvt_ref, total_ref,
):
    cols = q_ref.shape[1]
    blocks = length // BLOCK
    id_columns(ids_ref, cols_ref, seqs, length)
    lane = lax.broadcasted_iota(jnp.int32, (1, 128), 1)

    def flip(i, _):
        at = pl.ds(pl.multiple_of(i * BLOCK, BLOCK), BLOCK)
        qt_ref[:, at] = q_ref[at, :].T
        gt_ref[:, at] = g_ref[at, :].T
        return 0

    lax.fori_loop(0, seqs * blocks, flip, 0)
    dkt_ref[...] = jnp.zeros_like(dkt_ref)
    dvt_ref[...] = jnp.zeros_like(dvt_ref)

    def step(i, _):
        head, index = i // blocks, i % blocks
        start, width = window(index, length)
        mine = head_lanes(head, cols)
        feats = pl.ds(pl.multiple_of(head * HEAD_DIM, HEAD_DIM), HEAD_DIM)
        bias = table_ref[head, pl.ds(pl.multiple_of(index * BLOCK, BLOCK), BLOCK), pl.ds(start, width)].astype(F32)
        for seq in range(seqs):
            base = seq * length
            rows = pl.ds(pl.multiple_of(base + index * BLOCK, BLOCK), BLOCK)
            keys_at = pl.ds(pl.multiple_of(base + start, 128), width)
            keys = k_ref[keys_at, :]
            same = cols_ref[rows, 0:1] == ids_ref[seq : seq + 1, pl.ds(start, width)]
            sums = jnp.sum(jnp.where(lane == head, lse_ref[rows, :], 0.0), axis=-1, keepdims=True)
            scores = dot_nt(jnp.where(mine, q_ref[rows, :], 0), keys) + bias
            probs = jnp.where(same, jnp.exp(scores - sums), 0.0)
            grad_probs = dot_nt(jnp.where(mine, g_ref[rows, :], 0), v_ref[keys_at, :])
            centre = jnp.sum(grad_probs * probs, axis=-1, keepdims=True)
            grad_scores = (probs * (grad_probs - centre)).astype(BF)
            dvt_ref[feats, keys_at] += dot(gt_ref[feats, rows], probs.astype(BF))
            dkt_ref[feats, keys_at] += dot(qt_ref[feats, rows], grad_scores)
            grad_q = (dot(grad_scores, keys) * 0.125).astype(BF)
            dq_ref[rows, :] = jnp.where(mine, grad_q, dq_ref[rows, :])
            if seq == 0:
                total_ref[:, 0:width] = grad_scores.astype(F32)
            else:
                total_ref[:, 0:width] += grad_scores.astype(F32)
        for part in range(BLOCK // GROUP):
            owner = index * (BLOCK // GROUP) + part
            first, wide = band_window(owner, length)
            offset = pl.multiple_of(first - start, 128)
            band_ref[owner, head, :, :] = total_ref[part * GROUP : (part + 1) * GROUP, pl.ds(offset, wide)].astype(BF)
        return 0

    dq_ref[...] = jnp.zeros_like(dq_ref)
    total_ref[...] = jnp.zeros_like(total_ref)
    lax.fori_loop(0, heads * blocks, step, 0)

    def finish(i, _):
        at = pl.ds(pl.multiple_of(i * BLOCK, BLOCK), BLOCK)
        dk_ref[at, :] = dkt_ref[:, at].T.astype(BF)
        dv_ref[at, :] = dvt_ref[:, at].T.astype(BF)
        return 0

    lax.fori_loop(0, seqs * blocks, finish, 0)


def attend_back(q, k, v, g, lse, table, ids):
    seqs, length = ids.shape
    rows, cols = q.shape
    heads = cols // HEAD_DIM
    wide = band_window(0, length)[1]
    width = min(length, BLOCK + 2 * PAGE_MOST)
    one = jax.ShapeDtypeStruct((rows, cols), BF)
    return pl.pallas_call(
        partial(attend_back_kernel, seqs, length, heads),
        out_shape=(one, one, one, jax.ShapeDtypeStruct((length // GROUP, heads, GROUP, wide), BF)),
        in_specs=[vmem()] * 7,
        out_specs=(vmem(),) * 4,
        scratch_shapes=[
            pltpu.VMEM((rows, 128), F32),
            pltpu.VMEM((cols, rows), BF),
            pltpu.VMEM((cols, rows), BF),
            pltpu.VMEM((cols, rows), F32),
            pltpu.VMEM((cols, rows), F32),
            pltpu.VMEM((BLOCK, width), F32),
        ],
        compiler_params=pltpu.CompilerParams(vmem_limit_bytes=VMEM_MOST),
        name="attend_back",
    )(q, k, v, g, lse, table, ids)


def scatter_dp(x):
    return lax.psum_scatter(x, "dp", scatter_dimension=0, tiled=True).astype(F32)


def scatter_mp(x):
    return lax.psum_scatter(x.astype(BF), "mp", scatter_dimension=0, tiled=True).astype(F32)


def reduce_table(band, length, n_dp):
    groups, heads, _, wide = band.shape
    shard = length // n_dp
    send = band.reshape(groups, heads, GROUP // shard, shard, wide).swapaxes(1, 2)
    part = scatter_dp(send.reshape(n_dp * heads * shard, wide)).reshape(heads, shard, wide)
    first = band_window(lax.axis_index("dp") * shard // GROUP, length)[0]
    return lax.dynamic_update_slice(jnp.zeros((heads, shard, length), F32), part, (0, 0, first))


def local(
    patches, segment_ids, fill_counts, attn_gain, attn_shift, qkv_weight, qv_bias, rel_table, proj_weight,
    proj_bias, attn_scale, mlp_gain, mlp_shift, up_weight, up_bias, down_weight, down_bias, mlp_scale, cotangent,
):
    n_dp = lax.axis_size("dp")
    seqs, length = segment_ids.shape
    cols = qkv_weight.shape[2]
    heads = cols // HEAD_DIM
    places = jnp.arange(length, dtype=jnp.int32)[None]
    ids = jnp.where(places < fill_counts[:, None], segment_ids, -1 - places).astype(F32)
    inputs = patches.astype(F32)
    grad_top = cotangent.astype(F32)
    normed_one, hat_one, inv_one = norm_rows(inputs, attn_gain, attn_shift)
    rows_one = lax.all_gather(normed_one.astype(BF), "mp", axis=0, tiled=True)
    grad_mlp = (grad_top * mlp_scale).astype(BF)
    grad_rows = lax.all_gather(grad_mlp, "mp", axis=0, tiled=True)
    queries = ((dot(rows_one, qkv_weight[0]) + qv_bias[0].astype(F32)).astype(BF) * 0.125).astype(BF)
    keys = dot(rows_one, qkv_weight[1]).astype(BF)
    values = (dot(rows_one, qkv_weight[2]) + qv_bias[1].astype(F32)).astype(BF)
    context, lse = attend(queries, keys, values, rel_table, ids)
    attn_out = scatter_mp(dot(context, proj_weight)) + proj_bias.astype(F32)
    middle = inputs + attn_scale * attn_out
    normed_two, hat_two, inv_two = norm_rows(middle, mlp_gain, mlp_shift)
    rows_two = lax.all_gather(normed_two.astype(BF), "mp", axis=0, tiled=True)
    pre_act = dot(rows_two, up_weight) + up_bias.astype(F32)
    hidden = jax.nn.gelu(pre_act, approximate=True).astype(BF)
    grad_hidden = dot_nt(grad_rows, down_weight)
    grad_pre = gelu_back(pre_act, grad_hidden).astype(BF)
    grad_norm_two = scatter_mp(dot_nt(grad_pre, up_weight))
    mlp_out = scatter_mp(dot(hidden, down_weight)) + down_bias.astype(F32)
    layer_out = (middle + mlp_scale * mlp_out).astype(BF)
    up_local = dot_tn(rows_two, grad_pre).astype(BF)
    down_local = dot_tn(grad_rows, hidden).astype(BF)
    up_grad = scatter_dp(up_local)
    down_grad = scatter_dp(down_local).T
    up_bias_local = jnp.sum(grad_pre.astype(F32), axis=0)
    scale_two_grad = jnp.sum(grad_top * mlp_out, axis=0)
    down_bias_grad = jnp.sum(grad_mlp.astype(F32), axis=0)
    back_two, gain_two_grad, shift_two_grad = norm_back(grad_norm_two, hat_two, inv_two, mlp_gain)
    grad_middle = grad_top + back_two
    grad_attn = (grad_middle * attn_scale).astype(BF)
    scale_one_grad = jnp.sum(grad_middle * attn_out, axis=0)
    proj_bias_grad = jnp.sum(grad_attn.astype(F32), axis=0)
    attn_grad_rows = lax.all_gather(grad_attn, "mp", axis=0, tiled=True)
    grad_context = dot_nt(attn_grad_rows, proj_weight).astype(BF)
    grad_q, grad_k, grad_v, band = attend_back(queries, keys, values, grad_context, lse, rel_table, ids)
    total = dot_nt(grad_q, qkv_weight[0]) + dot_nt(grad_k, qkv_weight[1]) + dot_nt(grad_v, qkv_weight[2])
    grad_norm_one = scatter_mp(total)
    table_grad = reduce_table(band, length, n_dp)
    mixed = jnp.concatenate(
        [dot_tn(rows_one, grad_q), dot_tn(rows_one, grad_k), dot_tn(rows_one, grad_v), dot_tn(attn_grad_rows, context)],
        axis=1,
    ).astype(BF)
    mixed = scatter_dp(mixed)
    qkv_grad = mixed[:, : 3 * cols].reshape(-1, 3, cols).swapaxes(0, 1)
    proj_grad = mixed[:, 3 * cols :].T
    qv_bias_local = jnp.stack([jnp.sum(grad_q.astype(F32), axis=0), jnp.sum(grad_v.astype(F32), axis=0)])
    back_one, gain_one_grad, shift_one_grad = norm_back(grad_norm_one, hat_one, inv_one, attn_gain)
    patch_grad = grad_middle + back_one
    small = lax.psum(
        jnp.stack(
            [
                gain_one_grad, shift_one_grad, proj_bias_grad, scale_one_grad,
                gain_two_grad, shift_two_grad, down_bias_grad, scale_two_grad,
            ]
        ),
        ("dp", "mp"),
    )
    qv_bias_grad, up_bias_grad = lax.psum((qv_bias_local, up_bias_local), "dp")
    return (
        layer_out, patch_grad, small[0], small[1], qkv_grad, qv_bias_grad, table_grad, proj_grad, small[2], small[3],
        small[4], small[5], up_grad, up_bias_grad, down_grad, small[6], small[7],
    )


def solution(mesh):
    rows, split = P(("dp", "mp"), None), P("mp", None)
    placed = (
        rows, P("dp", None), P("dp"), P(), P(), P(None, None, "mp"), P(None, "mp"), P("mp", None, None), split,
        P(), P(), P(), P(), P(None, "mp"), P("mp"), split, P(), P(), rows,
    )
    given = (
        rows, rows, P(), P(), P(None, "dp", "mp"), P(None, "mp"), P("mp", "dp", None), P("mp", "dp"), P(), P(),
        P(), P(), P("dp", "mp"), P("mp"), P("mp", "dp"), P(), P(),
    )
    return jax.shard_map(local, mesh=mesh, in_specs=placed, out_specs=given, check_vma=False)
```

time: 983 us -> 660 us (0.67)
  waiting for transfers between devices: 637 us -> 404 us
  matrix products: 124 us -> 72.1 us
  Pallas kernels: 0 us -> 48.8 us
  other arithmetic: 76.2 us -> 28.8 us
  local copies, waits for them, and re-layouts: 60 us -> 20.8 us
    reduce_scatter x7, waiting for transfers between devices: 512 us -> 267 us  [the longest x4 141 us: scatter_mp(): lax.psum_scatter(x.astype(BF), 'mp', scatter_dimension=0, tiled=True)]
    pallas_call x0 -> x2, Pallas kernels: none -> 48.8 us  [the longest x1 32 us: attend_back(): pl.pallas_call(partial(attend_back_kernel, seqs, length, heads), out_shap...]
    dot_general x45 -> x18, matrix products: 120 us -> 72.1 us  [the longest x6 28 us: dot(): return jnp.dot(a, b, preferred_element_type=F32)]
    unnamed x15 -> x13, waiting for transfers between devices: 17.7 us -> 45.7 us
    scatter-add x4 -> x0, other arithmetic: 25.4 us -> none  [attend_back(): carry.at[:, start:start + block, :].add(grad_scores.astype(jnp.float32))]
    while x60 -> x0, local copies, waits for them, and re-layouts: 16.2 us -> none
    all_gather x1, waiting for transfers between devices: 28.6 us -> 13.3 us  [local(): attn_grad_rows = lax.all_gather(grad_attn, 'mp', axis=0, tiled=True)]
    unnamed x99 -> x80, local copies, waits for them, and re-layouts: 18.8 us -> 8.38 us
  transfers between devices with their start and end apart: 13 -> 12, of which waited for: 12 -> 12; matrix products, arithmetic and copies ran while one was open for 16% -> 10% of each run, Pallas kernels for 0% -> 5%
where the time goes in v1:
time: 660 us; the launch traced here: 653 us
  waiting for transfers between devices  404 us (61%)
  matrix products  72.1 us (11%)
  blocking collectives  62.2 us (9%)
  Pallas kernels  48.8 us (7%)
  other arithmetic  28.8 us (4%)
  local copies, waits for them, and re-layouts  20.8 us (3%)
  between operations  15.1 us (2%)
    reduce_scatter x4, waiting for transfers between devices, scatter_mp(): lax.psum_scatter(x.astype(BF), 'mp', scatter_dimension=0, tiled=True)  141 us
    reduce_scatter x3, waiting for transfers between devices, scatter_dp(): lax.psum_scatter(x, 'dp', scatter_dimension=0, tiled=True).astype(F32)  126 us
    unnamed x13, waiting for transfers between devices  45.7 us
    psum x1, blocking collectives, local(): lax.psum(jnp.stack([gain_one_grad, shift_one_grad, proj_bias_grad, scale_...  41.9 us
    pallas_call x1, Pallas kernels, attend_back(): pl.pallas_call(partial(attend_back_kernel, seqs, length, heads), out_shap...  32 us
    all_gather x1, waiting for transfers between devices, local(): rows_one = lax.all_gather(normed_one.astype(BF), 'mp', axis=0, tiled=True)  30.6 us
    dot_general x6, matrix products, dot(): return jnp.dot(a, b, preferred_element_type=F32)  28 us
    all_gather x1, waiting for transfers between devices, local(): rows_two = lax.all_gather(normed_two.astype(BF), 'mp', axis=0, tiled=True)  24.7 us
  transfers between devices with their start and end apart: 12, of which 12 were waited for; matrix products, arithmetic and copies ran while one was open for 10% of the time, Pallas kernels for 5%

profile of v1, /device:TPU:0, one launch (start us, length us, event | category | flops | bytes accessed | tf_op | source)
XLA Modules:
  0.0 653.1 jit_solution(17326716485955189815)
XLA Ops:
  7.3 1.5 convert_reduce_fusion.3
  8.8 1.5 fusion.25
  10.3 1.9 fusion.21
  13.0 30.6 %all-gather.5.cloned.1.call-done = bf16[2048,768]{1,0:T(8,128)(2,1)} async-done(((bf16[512,768]{1,0:T(8,128)(2,1)}), bf16[2048,768]{1,0:T(8,128)(2,1)}) %all-gather.5.cloned.1.call-update) | async-done | bytes 3145744 | tf_op jit(solution)/shard_map/all_gather | solution.py:259
  43.7 4.0 convolution_convert_fusion.3.k_ref
  47.7 2.0 fusion.8.v_ref
  49.7 2.0 fusion.9.q_ref
  51.7 16.8 %attend.1 = (bf16[2048,192]{1,0:T(8,128)(2,1)}, f32[2048,128]{1,0:T(8,128)}) custom-call(bf16[2048,192]{1,0:T(8,128)(2,1)} %fusion.9.q_ref, bf16[2048,192]{1,0:T(8,128)(2,1)} %convolution_convert_fusion.3.k_ref, bf16[2048,192]{1,0:T(8,128)(2,1)} %fusion.8.v_ref, bf16[3,1024,1024]{2,1,0:T(8,128)(2,1)} %table_ref.3, f32[2,1024]{1,0:T(2,128)} %fusion.48.ids_ref), custom_call_target="tpu_custom_call" | custom-call | tf_op jit(solution)/shard_map/attend/pallas_call | solution.py:126
  68.5 3.9 convolution_convert_fusion.2
  73.1 37.4 %reduce-scatter.11.cloned.1.call-done = bf16[512,768]{1,0:T(8,128)(2,1)} async-done(((bf16[2048,768]{1,0:T(8,128)(2,1)}), bf16[512,768]{1,0:T(8,128)(2,1)}) %reduce-scatter.11.cloned.1.call-update) | async-done | bytes 786448 | tf_op jit(solution)/shard_map/reduce_scatter | solution.py:234
  110.5 1.6 fusion.49
  113.2 2.1 add_convert_fusion.2
  115.3 2.3 convert_reduce_fusion.6
  117.9 1.3 convert_element_type.119
  119.2 24.7 %all-gather.7.cloned.1.call-done = bf16[2048,768]{1,0:T(8,128)(2,1)} async-done(((bf16[512,768]{1,0:T(8,128)(2,1)}), bf16[2048,768]{1,0:T(8,128)(2,1)}) %all-gather.7.cloned.1.call-update) | async-done | bytes 3145744 | tf_op jit(solution)/shard_map/all_gather | solution.py:269
  143.9 7.5 %fusion.52 = f32[2048,768]{1,0:T(8,128)} fusion(bf16[2048,768]{1,0:T(8,128)(2,1)} %all-gather.7.cloned.1.call-done, bf16[768,768]{1,0:T(8,128)(2,1)} %param.32), kind=kOutput, calls=%fused_computation.116 | convolution fusion | flops 2415919104 | bytes 10616832 | tf_op jit(solution)/shard_map/dot_general | solution.py:27
  151.4 23.0 %all-gather.9.cloned.1.call-done = bf16[2048,768]{1,0:T(8,128)(2,1)} async-done(((bf16[512,768]{1,0:T(8,128)(2,1)}), bf16[2048,768]{1,0:T(8,128)(2,1)}) %all-gather.9.cloned.1.call-update) | async-done | bytes 3145744 | tf_op jit(solution)/shard_map/all_gather | solution.py:261
  174.5 10.9 %convert_reduce_fusion = (f32[768]{0:T(1024)}, bf16[2048,768]{1,0:T(8,128)(2,1)S(1)}) fusion(f32[2048,768]{1,0:T(8,128)} %fusion.52, f32[768]{0:T(1024)} %convert_element_type.119, bf16[2048,768]{1,0:T(8,128)(2,1)} %all-gather.9.cloned.1.call-done, bf16[768,768]{1,0:T(8,128)(2,1)S(1)} %copy-done), kind=kOutput, calls=%fused_computation.9 | convolution fusion | flops 2452094208 | bytes 13768704 | tf_op jit(solution)/shard_map/dot_general | solution.py:31
  185.4 1.7 copy-done.38
  187.1 4.0 convolution_convert_fusion
  191.2 8.6 %convolution_convert_fusion.1 = bf16[2048,768]{1,0:T(8,128)(2,1)} fusion(bf16[768,768]{1,0:T(8,128)(2,1)S(1)} %copy-done, f32[2048,768]{1,0:T(8,128)} %fusion.52, f32[768]{0:T(1024)} %convert_element_type.119), kind=kOutput, calls=%fused_computation.13 | convolution fusion | flops 2433220608 | bytes 10619904 | tf_op jit(solution)/shard_map/dot_general | solution.py:27
  200.4 28.7 %reduce-scatter.15.cloned.1.call-done = bf16[512,768]{1,0:T(8,128)(2,1)} async-done(((bf16[2048,768]{1,0:T(8,128)(2,1)}), bf16[512,768]{1,0:T(8,128)(2,1)}) %reduce-scatter.15.cloned.1.call-update) | async-done | bytes 786448 | tf_op jit(solution)/shard_map/reduce_scatter | solution.py:234
  229.2 2.2 fusion.32
  231.4 38.1 %reduce-scatter.13.cloned.1.call-done = bf16[512,768]{1,0:T(8,128)(2,1)} async-done(((bf16[2048,768]{1,0:T(8,128)(2,1)}), bf16[512,768]{1,0:T(8,128)(2,1)}) %reduce-scatter.13.cloned.1.call-update) | async-done | bytes 786448 | tf_op jit(solution)/shard_map/reduce_scatter | solution.py:234
  269.5 3.2 multiply_reduce_fusion
  275.0 6.6 %convolution_convert_fusion.6 = bf16[768,768]{1,0:T(8,128)(2,1)} fusion(bf16[2048,768]{1,0:T(8,128)(2,1)} %all-gather.7.cloned.1.call-done, bf16[2048,768]{1,0:T(8,128)(2,1)} %copy-done.38), kind=kOutput, calls=%fused_computation.70 | convolution fusion | flops 2416508928 | bytes 7471104 | tf_op jit(solution)/shard_map/dot_general | solution.py:35
  281.7 8.4 %convolution_convert_fusion.5 = bf16[768,768]{1,0:T(8,128)(2,1)} fusion(bf16[2048,768]{1,0:T(8,128)(2,1)} %all-gather.9.cloned.1.call-done, f32[2048,768]{1,0:T(8,128)} %fusion.52, f32[768]{0:T(1024)S(1)} %copy-done.30), kind=kOutput, calls=%fused_computation.69 | convolution fusion | flops 2432237568 | bytes 10619904 | tf_op jit(solution)/shard_map/dot_general | solution.py:35
  290.3 13.3 %all-gather.11.cloned.1.call-done = bf16[2048,768]{1,0:T(8,128)(2,1)} async-done(((bf16[512,768]{1,0:T(8,128)(2,1)}), bf16[2048,768]{1,0:T(8,128)(2,1)}) %all-gather.11.cloned.1.call-update) | async-done | bytes 3145744 | tf_op jit(solution)/shard_map/all_gather | solution.py:289
  303.6 3.1 convolution_convert_fusion.4
  306.7 1.3 copy.49.g_ref
  308.0 32.0 %attend_back.1 = (bf16[2048,192]{1,0:T(8,128)(2,1)}, bf16[2048,192]{1,0:T(8,128)(2,1)}, bf16[2048,192]{1,0:T(8,128)(2,1)}, bf16[8,3,128,640]{3,2,1,0:T(8,128)(2,1)}) custom-call(bf16[2048,192]{1,0:T(8,128)(2,1)} %fusion.9.q_ref, bf16[2048,192]{1,0:T(8,128)(2,1)} %convolution_convert_fusion.3.k_ref, bf16[2048,192]{1,0:T(8,128)(2,1)} %fusion.8.v_ref, ...), custom_call_target="tpu_custom_call" | custom-call | tf_op jit(solution)/shard_map/attend_back/pallas_call | solution.py:211
  340.0 2.9 convolution_convert_fusion.7
  346.6 1.5 copy.54
  348.2 2.1 fusion.39
  351.5 2.8 add_convert_fusion
  354.9 16.8 %reduce-scatter.21.cloned.1.call-done = bf16[96,768]{1,0:T(8,128)(2,1)} async-done(((bf16[768,768]{1,0:T(8,128)(2,1)}), bf16[96,768]{1,0:T(8,128)(2,1)}) %reduce-scatter.21.cloned.1.call-update) | async-done | bytes 147472 | tf_op jit(solution)/shard_map/reduce_scatter | solution.py:230
  371.7 1.6 convert_element_type.140
  373.3 65.6 %reduce-scatter.23.cloned.1.call-done = bf16[96,768]{1,0:T(8,128)(2,1)} async-done(((bf16[768,768]{1,0:T(8,128)(2,1)}), bf16[96,768]{1,0:T(8,128)(2,1)}) %reduce-scatter.23.cloned.1.call-update) | async-done | bytes 147472 | tf_op jit(solution)/shard_map/reduce_scatter | solution.py:230
  439.0 1.6 convert_bitcast_fusion
  441.3 20.3 %all-reduce = (f32[2,192]{1,0:T(2,128)}, f32[768]{0:T(1024)}) all-reduce(f32[2,192]{1,0:T(2,128)S(1)} %pad_maximum_fusion.1, f32[768]{0:T(1024)S(1)} %copy-done.29), channel_id=1, replica_groups=mesh['dp'=8,'mp'=4] {'dp'}, use_global_device_ids=true, to_apply=%region_24.25 | all-reduce | flops 1152 | bytes 9216 | tf_op jit(solution)/shard_map/psum | solution.py:314
  461.6 45.0 %reduce-scatter.25.cloned.1.call-done = bf16[96,768]{1,0:T(8,128)(2,1)} async-done(((bf16[768,768]{1,0:T(8,128)(2,1)}), bf16[96,768]{1,0:T(8,128)(2,1)}) %reduce-scatter.25.cloned.1.call-update) | async-done | bytes 147472
  509.3 36.8 %reduce-scatter.17.cloned.1.call-done = bf16[512,768]{1,0:T(8,128)(2,1)} async-done(((bf16[2048,768]{1,0:T(8,128)(2,1)}), bf16[512,768]{1,0:T(8,128)(2,1)}) %reduce-scatter.17.cloned.1.call-update) | async-done | bytes 786448 | tf_op jit(solution)/shard_map/reduce_scatter | solution.py:234
  546.1 2.0 fusion.33
  548.2 41.9 %psum.21 = f32[8,768]{1,0:T(8,128)S(1)} all-reduce(f32[8,768]{1,0:T(8,128)S(1)} %stack.44), channel_id=1, replica_groups=mesh['dp'=8,'mp'=4] {'dp','mp'}, use_global_device_ids=true, to_apply=%region_20.21 | all-reduce | flops 6144 | bytes 49152 | tf_op jit(solution)/shard_map/psum | solution.py:305
  590.8 1.7 fusion.24
  592.5 43.3 %reduce-scatter.19.cloned.1.call-done = bf16[384,640]{1,0:T(8,128)(2,1)} async-done(((bf16[3072,640]{1,0:T(8,128)(2,1)}), bf16[384,640]{1,0:T(8,128)(2,1)}) %reduce-scatter.19.cloned.1.call-update) | async-done | bytes 491536 | tf_op jit(solution)/shard_map/reduce_scatter | solution.py:230
  637.0 1.3 broadcast_in_dim.11
  638.3 7.5 %dynamic_update_slice.3 = f32[3,128,1024]{2,1,0:T(8,128)} dynamic-update-slice(f32[3,128,1024]{2,1,0:T(8,128)} %broadcast_in_dim.11, f32[3,128,640]{2,1,0:T(8,128)S(1)} %convert.20, s32[]{:T(128)} %constant.52.clone.1, s32[]{:T(128)} %constant.52.clone.1, s32[]{:T(128)S(6)} %min.4) | dynamic-update-slice | bytes 1966084 | tf_op jit(solution)/shard_map/dynamic_update_slice | solution.py:243
  (139 shorter events, 17.1 us)
Async XLA Ops:
  7.2 167.3 %copy-start = (bf16[768,768]{1,0:T(8,128)(2,1)S(1)}, bf16[768,768]{1,0:T(8,128)(2,1)}, u32[]{:S(2)}) copy-start(bf16[768,768]{1,0:T(8,128)(2,1)} %param.34) | copy-start | bytes 3538948
  7.2 3.1 copy-start.2
  7.2 5.1 copy-start.31
  7.2 5.1 copy-start.34
  7.2 5.1 copy-start.28
  7.2 36.4 %copy-start.15 = (bf16[3,768,192]{1,2,0:T(8,128)(2,1)S(1)}, bf16[3,768,192]{1,2,0:T(8,128)(2,1)}, u32[]{:S(2)}) copy-start(bf16[3,768,192]{1,2,0:T(8,128)(2,1)} %param.24) | copy-start | bytes 2654212
  7.3 36.4 %all-gather.5.cloned.1.call-start = ((), (), s32[]{:S(2)}) async-start(), calls=%async_computation.8 | async-start | bytes 3932160 | tf_op jit(solution)/shard_map/all_gather | solution.py:259
  10.3 37.4 %copy-start.22 = (f32[512]{0:T(512)}, f32[512]{0:T(512)S(1)}, u32[]{:S(2)}) copy-start(f32[512]{0:T(512)S(1)} %add_rsqrt_fusion.1) | copy-start | bytes 6148
  12.3 98.2 %reduce-scatter.11.cloned.1.call-start = ((), (), s32[]{:S(2)}) async-start(), calls=%async_computation.9 | async-start | bytes 3932160 | tf_op jit(solution)/shard_map/reduce_scatter | solution.py:234
  43.7 4.0 copy-start.35
  51.7 16.8 %copy-start.17 = (bf16[192,768]{1,0:T(8,128)(2,1)S(1)}, bf16[192,768]{1,0:T(8,128)(2,1)}, u32[]{:S(2)}) copy-start(bf16[192,768]{1,0:T(8,128)(2,1)} %param.27) | copy-start | bytes 884740
  72.4 38.1 %copy-start.19 = (f32[768]{0:T(1024)S(1)}, f32[768]{0:T(1024)}, u32[]{:S(2)}) copy-start(f32[768]{0:T(1024)} %param.29) | copy-start | bytes 9220
  72.4 71.5 %all-gather.7.cloned.1.call-start = ((), (), s32[]{:S(2)}) async-start(), calls=%async_computation.10 | async-start | bytes 3932160 | tf_op jit(solution)/shard_map/all_gather | solution.py:269
  110.5 1.6 copy-start.3
  112.1 3.3 copy-start.10
  115.3 59.2 %all-gather.9.cloned.1.call-start = ((), (), s32[]{:S(2)}) async-start(), calls=%async_computation.12 | async-start | bytes 3932160 | tf_op jit(solution)/shard_map/all_gather | solution.py:261
  117.7 111.5 %reduce-scatter.15.cloned.1.call-start = ((), (), s32[]{:S(2)}) async-start(), calls=%async_computation.13 | async-start | bytes 3932160 | tf_op jit(solution)/shard_map/reduce_scatter | solution.py:234
  174.5 12.6 %copy-start.37 = (bf16[768,768]{1,0:T(8,128)(2,1)S(1)}, bf16[768,768]{1,0:T(8,128)(2,1)}, u32[]{:S(2)}) copy-start(bf16[768,768]{1,0:T(8,128)(2,1)} %param.32) | copy-start | bytes 3538948
  185.4 1.7 copy-start.38
  191.1 78.3 %reduce-scatter.13.cloned.1.call-start = ((), (), s32[]{:S(2)}) async-start(), calls=%async_computation.11 | async-start | bytes 3932160 | tf_op jit(solution)/shard_map/reduce_scatter | solution.py:234
  199.7 29.4 %copy-start.20 = (f32[768]{0:T(1024)S(1)}, f32[768]{0:T(1024)}, u32[]{:S(2)}) copy-start(f32[768]{0:T(1024)} %param.30) | copy-start | bytes 9220
  199.7 29.4 %copy-start.25 = (f32[512]{0:T(512)S(1)}, f32[512]{0:T(512)}, u32[]{:S(2)}) copy-start(f32[512]{0:T(512)} %copy-done.24) | copy-start | bytes 6148
  199.7 69.7 %copy-start.27 = (f32[768]{0:T(1024)S(1)}, f32[768]{0:T(1024)}, u32[]{:S(2)}) copy-start(f32[768]{0:T(1024)} %param.36) | copy-start | bytes 9220
  199.8 103.8 %all-gather.11.cloned.1.call-start = ((), (), s32[]{:S(2)}) async-start(), calls=%async_computation.14 | async-start | bytes 3932160 | tf_op jit(solution)/shard_map/all_gather | solution.py:289
  229.2 40.3 %copy-start.12 = (bf16[512,768]{1,0:T(8,128)(2,1)S(1)}, bf16[512,768]{1,0:T(8,128)(2,1)}, u32[]{:S(2)}) copy-start(bf16[512,768]{1,0:T(8,128)(2,1)} %reduce-scatter.15.cloned.1.call-done) | copy-start | bytes 2359300
  272.7 1.1 copy-start.4
  274.9 6.7 %copy-start.30 = (f32[768]{0:T(1024)S(1)}, f32[768]{0:T(1024)}, u32[]{:S(2)}) copy-start(f32[768]{0:T(1024)} %convert_element_type.119) | copy-start | bytes 9220
  275.0 96.8 %reduce-scatter.21.cloned.1.call-start = ((), (), s32[]{:S(2)}) async-start(), calls=%async_computation.17 | async-start | bytes 1327104 | tf_op jit(solution)/shard_map/reduce_scatter | solution.py:230
  281.6 22.0 %copy-start.18 = (bf16[192,768]{1,0:T(8,128)(2,1)S(1)}, bf16[192,768]{1,0:T(8,128)(2,1)}, u32[]{:S(2)}) copy-start(bf16[192,768]{1,0:T(8,128)(2,1)} %param.27) | copy-start | bytes 884740
  281.6 157.4 %reduce-scatter.23.cloned.1.call-start = ((), (), s32[]{:S(2)}) async-start(), calls=%async_computation.18 | async-start | bytes 1327104 | tf_op jit(solution)/shard_map/reduce_scatter | solution.py:230
  290.0 216.6 %reduce-scatter.25.cloned.1.call-start = ((), (), s32[]{:S(2)}) async-start(), calls=%async_computation.19 | async-start | bytes 1327104
  308.0 32.0 %copy-start.9 = (bf16[2048,192]{1,0:T(8,128)(2,1)S(1)}, bf16[2048,192]{1,0:T(8,128)(2,1)}, u32[]{:S(2)}) copy-start(bf16[2048,192]{1,0:T(8,128)(2,1)} %get-tuple-element.23) | copy-start | bytes 2359300
  340.0 2.9 copy-start.13
  340.0 3.2 copy-start.36
  343.2 1.2 copy-start.6
  344.4 1.2 copy-start.7
  348.1 198.1 %reduce-scatter.17.cloned.1.call-start = ((), (), s32[]{:S(2)}) async-start(), calls=%async_computation.15 | async-start | bytes 3932160 | tf_op jit(solution)/shard_map/reduce_scatter | solution.py:234
  348.1 2.1 copy-start.14
  348.1 2.1 copy-start.16
  350.2 1.2 copy-start.8
  354.3 0.7 copy-start.26
  354.3 281.5 %reduce-scatter.19.cloned.1.call-start = ((), (), s32[]{:S(2)}) async-start(), calls=%async_computation.16 | async-start | bytes 4423680 | tf_op jit(solution)/shard_map/reduce_scatter | solution.py:230
  354.8 86.4 %copy-start.29 = (f32[768]{0:T(1024)S(1)}, f32[768]{0:T(1024)}, u32[]{:S(2)}) copy-start(f32[768]{0:T(1024)} %get-tuple-element.47) | copy-start | bytes 9220
  440.7 105.5 %copy-start.21 = (f32[768]{0:T(1024)S(1)}, f32[768]{0:T(1024)}, u32[]{:S(2)}) copy-start(f32[768]{0:T(1024)} %param.22) | copy-start | bytes 9220
  440.7 105.5 %copy-start.23 = (f32[512]{0:T(512)S(1)}, f32[512]{0:T(512)}, u32[]{:S(2)}) copy-start(f32[512]{0:T(512)} %copy-done.22) | copy-start | bytes 6148
  441.3 149.5 %copy-start.5 = (f32[512,768]{1,0:T(8,128)S(1)}, f32[512,768]{1,0:T(8,128)}, u32[]{:S(2)}) copy-start(f32[512,768]{1,0:T(8,128)} %copy-done.4) | copy-start | bytes 4718596
  546.1 44.6 %copy-start.11 = (bf16[512,768]{1,0:T(8,128)(2,1)S(1)}, bf16[512,768]{1,0:T(8,128)(2,1)}, u32[]{:S(2)}) copy-start(bf16[512,768]{1,0:T(8,128)(2,1)} %reduce-scatter.17.cloned.1.call-done) | copy-start | bytes 2359300
  635.8 10.0 %copy-start.1 = (bf16[768,768]{1,0:T(8,128)(2,1)S(1)}, bf16[768,768]{1,0:T(8,128)(2,1)}, u32[]{:S(2)}) copy-start(bf16[768,768]{1,0:T(8,128)(2,1)} %param.34) | copy-start | bytes 3538948
  (3 other events, 2.0 us)
Sparse Core Ops, SparseCore 0:
  12.4 31.2 all-gather.4
  72.5 37.8 reduce-scatter.10
  115.4 28.4 all-gather.6
  145.9 28.4 all-gather.8
  191.2 37.8 reduce-scatter.14
  231.6 37.8 reduce-scatter.12
  275.1 28.5 all-gather.10
  307.0 64.6 reduce-scatter.20
  375.1 63.8 reduce-scatter.22
  442.8 63.8 reduce-scatter.24
  509.2 36.8 reduce-scatter.16
  549.7 86.0 reduce-scatter.18

commit v2 on v1

--- a/solution.py
+++ b/solution.py
@@ -50,11 +50,6 @@
         - normed * jnp.mean(scaled * normed, axis=-1, keepdims=True)
     )
     return (inv_std * inner, jnp.sum(grad_out * normed, axis=0), jnp.sum(grad_out, axis=0))
-
-
-def gelu_back(pre_act, grad):
-    _, pullback = jax.vjp(partial(jax.nn.gelu, approximate=True), pre_act)
-    return pullback(grad)[0]
 
 
 def window(index, length):
@@ -226,6 +221,407 @@
     )(q, k, v, g, lse, table, ids)
 
 
+CHUNKS = 4
+
+
+def loop(count, body):
+    lax.fori_loop(0, count, lambda i, _: (body(i), 0)[1], 0)
+
+
+def neighbours():
+    me = lax.axis_index("mp")
+    partner = me + 1 - 2 * lax.rem(me, 2)
+    return me, partner, lax.rem(me + 2, 4), lax.rem(partner + 2, 4)
+
+
+def greet(peers):
+    barrier = pltpu.get_barrier_semaphore()
+    for peer in peers:
+        pl.semaphore_signal(barrier, inc=1, device_id=peer, device_id_type=MESH)
+    pl.semaphore_wait(barrier, len(peers))
+
+
+def greet_mp():
+    _, partner, cross, _ = neighbours()
+    greet(({"mp": partner}, {"mp": cross}))
+
+
+class Gather:
+    def __init__(self, buffer, send, recv):
+        self.buffer, self.send, self.recv = buffer, send, recv
+        self.size = buffer.shape[0] // 4 // CHUNKS
+        self.me, self.partner, self.cross, self.diag = neighbours()
+
+    def rows(self, block, chunk):
+        return pl.ds(pl.multiple_of((block * CHUNKS + chunk) * self.size, self.size), self.size)
+
+    def copy(self, kind, block, chunk):
+        part = self.buffer.at[self.rows(block, chunk), :]
+        return pltpu.make_async_remote_copy(
+            src_ref=part, dst_ref=part, send_sem=self.send.at[kind, chunk], recv_sem=self.recv.at[kind, chunk],
+            device_id={"mp": self.cross if kind == 0 else self.partner}, device_id_type=MESH,
+        )
+
+    def send_own(self, chunk):
+        self.copy(0, self.me, chunk).start()
+        self.copy(1, self.me, chunk).start()
+
+    def wait_partner(self, chunk):
+        self.copy(1, self.partner, chunk).wait_recv()
+
+    def relay(self, chunk):
+        self.copy(0, self.cross, chunk).wait_recv()
+        self.copy(2, self.cross, chunk).start()
+
+    def wait_diag(self, chunk):
+        self.copy(2, self.diag, chunk).wait_recv()
+
+    def drain(self, chunk):
+        self.copy(0, self.me, chunk).wait_send()
+        self.copy(1, self.me, chunk).wait_send()
+        self.copy(2, self.cross, chunk).wait_send()
+
+
+class Scatter:
+    def __init__(self, out, inn, send, recv):
+        self.out, self.inn, self.send, self.recv = out, inn, send, recv
+        self.size = out.shape[1] // CHUNKS
+        self.me, self.partner, self.cross, self.diag = neighbours()
+
+    def rows(self, chunk):
+        return pl.ds(pl.multiple_of(chunk * self.size, self.size), self.size)
+
+    def copy(self, kind, chunk):
+        return pltpu.make_async_remote_copy(
+            src_ref=self.out.at[kind, self.rows(chunk), :], dst_ref=self.inn.at[kind, self.rows(chunk), :],
+            send_sem=self.send.at[kind, chunk], recv_sem=self.recv.at[kind, chunk],
+            device_id={"mp": self.cross if kind == 1 else self.partner}, device_id_type=MESH,
+        )
+
+    def put(self, kind, chunk, value):
+        self.out[kind, self.rows(chunk), :] = value.astype(BF)
+        self.copy(kind, chunk).start()
+
+    def take(self, kind, chunk):
+        self.copy(kind, chunk).wait_recv()
+        return self.inn[kind, self.rows(chunk), :].astype(F32)
+
+    def drain(self, chunk):
+        for kind in range(3):
+            self.copy(kind, chunk).wait_send()
+
+
+def moves():
+    return [pltpu.SemaphoreType.DMA((3, CHUNKS)), pltpu.SemaphoreType.DMA((3, CHUNKS))]
+
+
+def halves(rows, cols):
+    return [pltpu.VMEM((3, rows, cols), BF), pltpu.VMEM((3, rows, cols), BF)] + moves()
+
+
+def call(kernel, name, number, outs, scratch, *args):
+    return pl.pallas_call(
+        kernel,
+        out_shape=tuple(jax.ShapeDtypeStruct(shape, dtype) for shape, dtype in outs),
+        in_specs=[vmem()] * len(args),
+        out_specs=tuple(vmem() for _ in outs),
+        scratch_shapes=scratch,
+        compiler_params=pltpu.CompilerParams(
+            vmem_limit_bytes=VMEM_MOST, collective_id=number, has_side_effects=True
+        ),
+        name=name,
+    )(*args)
+
+
+def gather_qkv_kernel(x_ref, gain_ref, shift_ref, w_ref, bias_ref, rows_ref, q_ref, k_ref, v_ref, send, recv):
+    net = Gather(rows_ref, send, recv)
+    greet_mp()
+
+    def own(chunk):
+        part = x_ref[pl.ds(pl.multiple_of(chunk * net.size, net.size), net.size), :].astype(F32)
+        rows_ref[net.rows(net.me, chunk), :] = norm_rows(part, gain_ref[...], shift_ref[...])[0].astype(BF)
+        net.send_own(chunk)
+
+    loop(CHUNKS, own)
+    tall = 2 * net.size
+
+    def project(block):
+        def part(i):
+            at = pl.ds(pl.multiple_of(block * CHUNKS * net.size + i * tall, tall), tall)
+            rows = rows_ref[at, :]
+            query = dot(rows, w_ref[0]) + bias_ref[0:1, :].astype(F32)
+            q_ref[at, :] = (query.astype(BF).astype(F32) * 0.125).astype(BF)
+            k_ref[at, :] = dot(rows, w_ref[1]).astype(BF)
+            v_ref[at, :] = (dot(rows, w_ref[2]) + bias_ref[1:2, :].astype(F32)).astype(BF)
+
+        loop(CHUNKS // 2, part)
+
+    project(net.me)
+    loop(CHUNKS, net.wait_partner)
+    project(net.partner)
+    loop(CHUNKS, net.relay)
+    project(net.cross)
+    loop(CHUNKS, net.wait_diag)
+    project(net.diag)
+    loop(CHUNKS, net.drain)
+
+
+def gather_qkv(patches, gain, shift, weight, bias):
+    rows, width = patches.shape
+    cols = weight.shape[2]
+    one = ((4 * rows, cols), BF)
+    return call(
+        gather_qkv_kernel, "gather_qkv", 1, [((4 * rows, width), BF), one, one, one], moves(),
+        patches, gain[None], shift[None], weight, bias,
+    )
+
+
+def project_kernel(
+    ctx_ref, w_ref, bias_ref, x_ref, scale_ref, gain_ref, shift_ref, attn_ref, mid_ref, norm_ref, out, inn, send, recv
+):
+    net = Scatter(out, inn, send, recv)
+    greet_mp()
+
+    def share(block, chunk):
+        at = pl.ds(pl.multiple_of((block * CHUNKS + chunk) * net.size, net.size), net.size)
+        return dot(ctx_ref[at, :], w_ref[...])
+
+    loop(CHUNKS, lambda c: net.put(0, c, share(net.diag, c)))
+    loop(CHUNKS, lambda c: net.put(1, c, share(net.cross, c) + net.take(0, c)))
+    loop(CHUNKS, lambda c: net.put(2, c, share(net.partner, c)))
+
+    def own(chunk):
+        attn_ref[net.rows(chunk), :] = share(net.me, chunk) + net.take(2, chunk) + bias_ref[...].astype(F32)
+
+    loop(CHUNKS, own)
+
+    def last(chunk):
+        at = net.rows(chunk)
+        attn = attn_ref[at, :] + net.take(1, chunk)
+        middle = x_ref[at, :].astype(F32) + scale_ref[...] * attn
+        attn_ref[at, :] = attn
+        mid_ref[at, :] = middle
+        norm_ref[at, :] = norm_rows(middle, gain_ref[...], shift_ref[...])[0].astype(BF)
+
+    loop(CHUNKS, last)
+    loop(CHUNKS, net.drain)
+
+
+def project(context, weight, bias, patches, scale, gain, shift):
+    rows, width = patches.shape
+    return call(
+        project_kernel, "project", 2, [((rows, width), F32), ((rows, width), F32), ((rows, width), BF)],
+        halves(rows, width), context, weight, bias[None], patches, scale[None], gain[None], shift[None],
+    )
+
+
+def gelu_both(u):
+    inner = 0.7978845608028654 * (u + 0.044715 * (u * u * u))
+    t = jnp.tanh(inner)
+    half = 0.5 * (1.0 + t)
+    slope = half + (0.5 * u) * (1.0 - t * t) * (0.7978845608028654 * (1.0 + 0.134145 * (u * u)))
+    return u * half, slope
+
+
+def mlp_kernel(
+    norm_ref, grad_ref, up_ref, bias_ref, down_ref, mid_ref, attn_ref, cot_ref, gain_ref, scale_ref,
+    gmid_ref, gattn_ref, share_ref, upg_ref, downg_ref, sums_ref,
+    rows_ref, hid_ref, pre_ref, own_ref, far_ref, gsend, grecv, out, inn, send, recv,
+):
+    gat = Gather(rows_ref, gsend, grecv)
+    net = Scatter(out, inn, send, recv)
+    size = gat.size
+    greet_mp()
+    sums_ref[...] = jnp.zeros_like(sums_ref)
+
+    def own(chunk):
+        rows_ref[gat.rows(gat.me, chunk), :] = norm_ref[net.rows(chunk), :]
+        gat.send_own(chunk)
+
+    loop(CHUNKS, own)
+
+    def two(first, second, chunk):
+        at, by = gat.rows(first, chunk), gat.rows(second, chunk)
+        both = lambda ref: jnp.concatenate([ref[at, :], ref[by, :]], axis=0)
+        value, slope = gelu_both(dot(both(rows_ref), up_ref[...]) + bias_ref[...].astype(F32))
+        hidden = value.astype(BF)
+        hid_ref[at, :], hid_ref[by, :] = hidden[:size], hidden[size:]
+        grad_pre = (dot_nt(both(grad_ref), down_ref[...]) * slope).astype(BF)
+        pre_ref[at, :], pre_ref[by, :] = grad_pre[:size], grad_pre[size:]
+        sums_ref[0:1, :] += jnp.sum(grad_pre.astype(F32), axis=0, keepdims=True)
+        part = dot(hidden, down_ref[...]).astype(BF)
+        share_ref[at, :], share_ref[by, :] = part[:size], part[size:]
+        back = dot_nt(grad_pre, up_ref[...])
+        return back[:size], back[size:]
+
+    def near(chunk):
+        gat.wait_partner(chunk)
+        theirs, mine = two(gat.partner, gat.me, chunk)
+        net.put(2, chunk, theirs)
+        own_ref[net.rows(chunk), :] = mine
+
+    loop(CHUNKS, near)
+
+    def across(chunk):
+        net.put(1, chunk, far_ref[net.rows(chunk), :] + net.take(0, chunk))
+
+    def far(chunk):
+        gat.relay(chunk)
+        gat.wait_diag(chunk)
+        theirs, mine = two(gat.diag, gat.cross, chunk)
+        net.put(0, chunk, theirs)
+        far_ref[net.rows(chunk), :] = mine
+
+        @pl.when(chunk > 0)
+        def _():
+            across(chunk - 1)
+
+    loop(CHUNKS, far)
+    across(CHUNKS - 1)
+    tile = 256
+
+    def weights(i):
+        at = pl.ds(pl.multiple_of(i * tile, tile), tile)
+        upg_ref[at, :] = dot_tn(rows_ref[:, at], pre_ref[...]).astype(BF)
+        downg_ref[at, :] = dot_tn(grad_ref[:, at], hid_ref[...]).astype(BF)
+
+    loop(rows_ref.shape[1] // tile, weights)
+
+    def last(chunk):
+        at = net.rows(chunk)
+        grad = own_ref[at, :] + net.take(2, chunk) + net.take(1, chunk)
+        normed, inv = norm_rows(mid_ref[at, :], 1.0, 0.0)[1:]
+        back, gain_sum, shift_sum = norm_back(grad, normed, inv, gain_ref[...])
+        middle = cot_ref[at, :].astype(F32) + back
+        gattn = (middle * scale_ref[...]).astype(BF)
+        gmid_ref[at, :] = middle
+        gattn_ref[at, :] = gattn
+        sums_ref[1:2, :] += gain_sum[None]
+        sums_ref[2:3, :] += shift_sum[None]
+        sums_ref[3:4, :] += jnp.sum(middle * attn_ref[at, :], axis=0, keepdims=True)
+        sums_ref[4:5, :] += jnp.sum(gattn.astype(F32), axis=0, keepdims=True)
+
+    loop(CHUNKS, last)
+    loop(CHUNKS, gat.drain)
+    loop(CHUNKS, net.drain)
+
+
+def mlp(normed, grad_rows, up, bias, down, middle, attn, cotangent, gain, scale):
+    rows, width = normed.shape
+    ff = up.shape[1]
+    return call(
+        mlp_kernel, "mlp", 3,
+        [
+            ((rows, width), F32), ((rows, width), BF), ((4 * rows, width), BF), ((width, ff), BF), ((width, ff), BF),
+            ((8, width), F32),
+        ],
+        [
+            pltpu.VMEM((4 * rows, width), BF), pltpu.VMEM((4 * rows, ff), BF), pltpu.VMEM((4 * rows, ff), BF),
+            pltpu.VMEM((rows, width), F32), pltpu.VMEM((rows, width), F32),
+        ] + moves() + halves(rows, width),
+        normed, grad_rows, up, bias[None], down, middle, attn, cotangent, gain[None], scale[None],
+    )
+
+
+def gather_back_kernel(g_ref, w_ref, ctx_ref, back_ref, proj_ref, rows_ref, send, recv):
+    net = Gather(rows_ref, send, recv)
+    greet_mp()
+
+    def own(chunk):
+        at = pl.ds(pl.multiple_of(chunk * net.size, net.size), net.size)
+        rows_ref[net.rows(net.me, chunk), :] = g_ref[at, :]
+        net.send_own(chunk)
+
+    loop(CHUNKS, own)
+
+    def block(number):
+        size = CHUNKS * net.size
+        at = pl.ds(pl.multiple_of(number * size, size), size)
+        back_ref[at, :] = dot_nt(rows_ref[at, :], w_ref[...]).astype(BF)
+
+    block(net.me)
+    loop(CHUNKS, net.wait_partner)
+    block(net.partner)
+    loop(CHUNKS, net.relay)
+    block(net.cross)
+    loop(CHUNKS, net.wait_diag)
+    block(net.diag)
+    tile = 256
+
+    def weights(i):
+        at = pl.ds(pl.multiple_of(i * tile, tile), tile)
+        proj_ref[at, :] = dot_tn(rows_ref[:, at], ctx_ref[...]).astype(BF)
+
+    loop(rows_ref.shape[1] // tile, weights)
+    loop(CHUNKS, net.drain)
+
+
+def gather_back(grad, weight, context):
+    rows, width = grad.shape
+    cols = weight.shape[0]
+    return call(
+        gather_back_kernel, "gather_back", 4, [((4 * rows, cols), BF), ((width, cols), BF)],
+        [pltpu.VMEM((4 * rows, width), BF)] + moves(), grad, weight, context,
+    )
+
+
+def tail_kernel(
+    dq_ref, dk_ref, dv_ref, w_ref, rows_ref, x_ref, gmid_ref, gain_ref,
+    grad_ref, qkv_ref, sums_ref, bias_ref, own_ref, out, inn, send, recv,
+):
+    net = Scatter(out, inn, send, recv)
+    cols = dq_ref.shape[1]
+    greet_mp()
+
+    def share(block, chunk):
+        at = pl.ds(pl.multiple_of((block * CHUNKS + chunk) * net.size, net.size), net.size)
+        return dot_nt(dq_ref[at, :], w_ref[0]) + dot_nt(dk_ref[at, :], w_ref[1]) + dot_nt(dv_ref[at, :], w_ref[2])
+
+    loop(CHUNKS, lambda c: net.put(0, c, share(net.diag, c)))
+    loop(CHUNKS, lambda c: net.put(1, c, share(net.cross, c) + net.take(0, c)))
+    loop(CHUNKS, lambda c: net.put(2, c, share(net.partner, c)))
+    tile = 256
+
+    def weights(i):
+        at = pl.ds(pl.multiple_of(i * tile, tile), tile)
+        rows = rows_ref[:, at]
+        for number, ref in enumerate((dq_ref, dk_ref, dv_ref)):
+            qkv_ref[at, number * cols : (number + 1) * cols] = dot_tn(rows, ref[...]).astype(BF)
+
+    loop(rows_ref.shape[1] // tile, weights)
+    bias_ref[0:1, :] = jnp.sum(dq_ref[...].astype(F32), axis=0, keepdims=True)
+    bias_ref[1:2, :] = jnp.sum(dv_ref[...].astype(F32), axis=0, keepdims=True)
+
+    def own(chunk):
+        own_ref[net.rows(chunk), :] = share(net.me, chunk) + net.take(2, chunk)
+
+    loop(CHUNKS, own)
+    sums_ref[...] = jnp.zeros_like(sums_ref)
+
+    def last(chunk):
+        at = net.rows(chunk)
+        grad = own_ref[at, :] + net.take(1, chunk)
+        normed, inv = norm_rows(x_ref[at, :].astype(F32), 1.0, 0.0)[1:]
+        back, gain_sum, shift_sum = norm_back(grad, normed, inv, gain_ref[...])
+        grad_ref[at, :] = gmid_ref[at, :] + back
+        sums_ref[0:1, :] += gain_sum[None]
+        sums_ref[1:2, :] += shift_sum[None]
+
+    loop(CHUNKS, last)
+    loop(CHUNKS, net.drain)
+
+
+def tail(dq, dk, dv, weight, rows_one, patches, grad_middle, gain):
+    rows, width = patches.shape
+    cols = dq.shape[1]
+    return call(
+        tail_kernel, "tail", 5,
+        [((rows, width), F32), ((width, 3 * cols), BF), ((8, width), F32), ((2, cols), F32)],
+        [pltpu.VMEM((rows, width), F32)] + halves(rows, width),
+        dq, dk, dv, weight, rows_one, patches, grad_middle, gain[None],
+    )
+
+
 def scatter_dp(x):
     return lax.psum_scatter(x, "dp", scatter_dimension=0, tiled=True).astype(F32)
 
@@ -253,65 +649,40 @@
     heads = cols // HEAD_DIM
     places = jnp.arange(length, dtype=jnp.int32)[None]
     ids = jnp.where(places < fill_counts[:, None], segment_ids, -1 - places).astype(F32)
-    inputs = patches.astype(F32)
     grad_top = cotangent.astype(F32)
-    normed_one, hat_one, inv_one = norm_rows(inputs, attn_gain, attn_shift)
-    rows_one = lax.all_gather(normed_one.astype(BF), "mp", axis=0, tiled=True)
     grad_mlp = (grad_top * mlp_scale).astype(BF)
     grad_rows = lax.all_gather(grad_mlp, "mp", axis=0, tiled=True)
-    queries = ((dot(rows_one, qkv_weight[0]) + qv_bias[0].astype(F32)).astype(BF) * 0.125).astype(BF)
-    keys = dot(rows_one, qkv_weight[1]).astype(BF)
-    values = (dot(rows_one, qkv_weight[2]) + qv_bias[1].astype(F32)).astype(BF)
+    rows_one, queries, keys, values = gather_qkv(patches, attn_gain, attn_shift, qkv_weight, qv_bias)
     context, lse = attend(queries, keys, values, rel_table, ids)
-    attn_out = scatter_mp(dot(context, proj_weight)) + proj_bias.astype(F32)
-    middle = inputs + attn_scale * attn_out
-    normed_two, hat_two, inv_two = norm_rows(middle, mlp_gain, mlp_shift)
-    rows_two = lax.all_gather(normed_two.astype(BF), "mp", axis=0, tiled=True)
-    pre_act = dot(rows_two, up_weight) + up_bias.astype(F32)
-    hidden = jax.nn.gelu(pre_act, approximate=True).astype(BF)
-    grad_hidden = dot_nt(grad_rows, down_weight)
-    grad_pre = gelu_back(pre_act, grad_hidden).astype(BF)
-    grad_norm_two = scatter_mp(dot_nt(grad_pre, up_weight))
-    mlp_out = scatter_mp(dot(hidden, down_weight)) + down_bias.astype(F32)
+    attn_out, middle, normed_two = project(context, proj_weight, proj_bias, patches, attn_scale, mlp_gain, mlp_shift)
+    grad_middle, grad_attn, mlp_share, up_local, down_local, sums_two = mlp(
+        normed_two, grad_rows, up_weight, up_bias, down_weight, middle, attn_out, cotangent, mlp_gain, attn_scale
+    )
+    mlp_out = scatter_mp(mlp_share) + down_bias.astype(F32)
     layer_out = (middle + mlp_scale * mlp_out).astype(BF)
-    up_local = dot_tn(rows_two, grad_pre).astype(BF)
-    down_local = dot_tn(grad_rows, hidden).astype(BF)
+    scale_two_grad = jnp.sum(grad_top * mlp_out, axis=0)
+    down_bias_grad = jnp.sum(grad_mlp.astype(F32), axis=0)
     up_grad = scatter_dp(up_local)
     down_grad = scatter_dp(down_local).T
-    up_bias_local = jnp.sum(grad_pre.astype(F32), axis=0)
-    scale_two_grad = jnp.sum(grad_top * mlp_out, axis=0)
-    down_bias_grad = jnp.sum(grad_mlp.astype(F32), axis=0)
-    back_two, gain_two_grad, shift_two_grad = norm_back(grad_norm_two, hat_two, inv_two, mlp_gain)
-    grad_middle = grad_top + back_two
-    grad_attn = (grad_middle * attn_scale).astype(BF)
-    scale_one_grad = jnp.sum(grad_middle * attn_out, axis=0)
-    proj_bias_grad = jnp.sum(grad_attn.astype(F32), axis=0)
-    attn_grad_rows = lax.all_gather(grad_attn, "mp", axis=0, tiled=True)
-    grad_context = dot_nt(attn_grad_rows, proj_weight).astype(BF)
+    grad_context, proj_local = gather_back(grad_attn, proj_weight, context)
     grad_q, grad_k, grad_v, band = attend_back(queries, keys, values, grad_context, lse, rel_table, ids)
-    total = dot_nt(grad_q, qkv_weight[0]) + dot_nt(grad_k, qkv_weight[1]) + dot_nt(grad_v, qkv_weight[2])
-    grad_norm_one = scatter_mp(total)
+    patch_grad, qkv_local, sums_one, qv_bias_local = tail(
+        grad_q, grad_k, grad_v, qkv_weight, rows_one, patches, grad_middle, attn_gain
+    )
     table_grad = reduce_table(band, length, n_dp)
-    mixed = jnp.concatenate(
-        [dot_tn(rows_one, grad_q), dot_tn(rows_one, grad_k), dot_tn(rows_one, grad_v), dot_tn(attn_grad_rows, context)],
-        axis=1,
-    ).astype(BF)
-    mixed = scatter_dp(mixed)
+    mixed = scatter_dp(jnp.concatenate([qkv_local, proj_local], axis=1))
     qkv_grad = mixed[:, : 3 * cols].reshape(-1, 3, cols).swapaxes(0, 1)
     proj_grad = mixed[:, 3 * cols :].T
-    qv_bias_local = jnp.stack([jnp.sum(grad_q.astype(F32), axis=0), jnp.sum(grad_v.astype(F32), axis=0)])
-    back_one, gain_one_grad, shift_one_grad = norm_back(grad_norm_one, hat_one, inv_one, attn_gain)
-    patch_grad = grad_middle + back_one
     small = lax.psum(
         jnp.stack(
             [
-                gain_one_grad, shift_one_grad, proj_bias_grad, scale_one_grad,
-                gain_two_grad, shift_two_grad, down_bias_grad, scale_two_grad,
+                sums_one[0], sums_one[1], sums_two[4], sums_two[3], sums_two[1], sums_two[2], down_bias_grad,
+                scale_two_grad,
             ]
         ),
         ("dp", "mp"),
     )
-    qv_bias_grad, up_bias_grad = lax.psum((qv_bias_local, up_bias_local), "dp")
+    qv_bias_grad, up_bias_grad = lax.psum((qv_bias_local, sums_two[0]), "dp")
     return (
         layer_out, patch_grad, small[0], small[1], qkv_grad, qv_bias_grad, table_grad, proj_grad, small[2], small[3],
         small[4], small[5], up_grad, up_bias_grad, down_grad, small[6], small[7],

time: 660 us -> 583 us (0.88)
  Pallas kernels: 48.8 us -> 217 us
  waiting for transfers between devices: 404 us -> 253 us
  matrix products: 72.1 us -> 0 us
  other arithmetic: 28.8 us -> 13.1 us
    pallas_call x0 -> x5, Pallas kernels: none -> 168 us  [call(): pl.pallas_call(kernel, out_shape=tuple((jax.ShapeDtypeStruct(shape, dtype...]
    reduce_scatter x4 -> x1, waiting for transfers between devices: 141 us -> 37.7 us  [scatter_mp(): lax.psum_scatter(x.astype(BF), 'mp', scatter_dimension=0, tiled=True)]
    reduce_scatter x3 -> x4, waiting for transfers between devices: 126 us -> 213 us  [scatter_dp(): lax.psum_scatter(x, 'dp', scatter_dimension=0, tiled=True).astype(F32)]
    dot_general x18 -> x0, matrix products: 72.1 us -> none  [the longest x6 28 us: dot(): return jnp.dot(a, b, preferred_element_type=F32)]
    all_gather x3 -> x0, waiting for transfers between devices: 68.6 us -> none  [the longest x1 30.6 us: local(): rows_one = lax.all_gather(normed_one.astype(BF), 'mp', axis=0, tiled=True)]
    unnamed x13 -> x6, waiting for transfers between devices: 45.7 us -> 2.26 us
    all_gather x1, waiting for transfers between devices: 23 us -> 0.02 us  [local(): grad_rows = lax.all_gather(grad_mlp, 'mp', axis=0, tiled=True)]
    reduce_sum x10 -> x1, other arithmetic: 14.1 us -> 2.4 us  [local(): scale_two_grad = jnp.sum(grad_top * mlp_out, axis=0)]
  transfers between devices with their start and end apart: 12 -> 6, of which waited for: 12 -> 5; matrix products, arithmetic and copies ran while one was open for 10% -> 3% of each run, Pallas kernels for 5% -> 15%
where the time goes in v2:
time: 583 us; the launch traced here: 582 us
  waiting for transfers between devices  253 us (43%)
  Pallas kernels  217 us (37%)
  blocking collectives  64.5 us (11%)
  local copies, waits for them, and re-layouts  19.9 us (3%)
  between operations  14.4 us (2%)
  other arithmetic  13.1 us (2%)
    reduce_scatter x4, waiting for transfers between devices, scatter_dp(): lax.psum_scatter(x, 'dp', scatter_dimension=0, tiled=True).astype(F32)  213 us
    pallas_call x5, Pallas kernels, call(): pl.pallas_call(kernel, out_shape=tuple((jax.ShapeDtypeStruct(shape, dtype...  168 us
    psum x1, blocking collectives, local(): lax.psum(jnp.stack([sums_one[0], sums_one[1], sums_two[4], sums_two[3], s...  42 us
    reduce_scatter x1, waiting for transfers between devices, scatter_mp(): lax.psum_scatter(x.astype(BF), 'mp', scatter_dimension=0, tiled=True)  37.7 us
    pallas_call x1, Pallas kernels, attend_back(): pl.pallas_call(partial(attend_back_kernel, seqs, length, heads), out_shap...  32.2 us
    psum x1, blocking collectives, local(): qv_bias_grad, up_bias_grad = lax.psum((qv_bias_local, sums_two[0]), 'dp')  22.5 us
    pallas_call x1, Pallas kernels, attend(): pl.pallas_call(partial(attend_kernel, seqs, length, heads), out_shape=(ja...  16.7 us
  transfers between devices with their start and end apart: 6, of which 5 were waited for; matrix products, arithmetic and copies ran while one was open for 3% of the time, Pallas kernels for 15%

profile of v2, /device:TPU:0, one launch (start us, length us, event | category | flops | bytes accessed | tf_op | source)
XLA Modules:
  0.0 582.3 jit_solution(14654689319856464970)
XLA Ops:
  7.3 2.3 convert_reduce_fusion
  9.6 0.0 reduce-scatter.8.cloned.1.call-start
  9.7 0.6 broadcast_in_dim.40.gain_ref
  10.2 0.6 broadcast_in_dim.41.shift_ref
  10.8 1.4 copy.40.w_ref
  12.2 0.6 broadcast_in_dim.43.bias_ref
  12.8 0.6 broadcast_in_dim.44.scale_ref
  13.4 0.6 broadcast_in_dim.45.gain_ref
  14.0 0.6 broadcast_in_dim.46.shift_ref
  14.6 0.6 broadcast_in_dim.47.bias_ref
  15.2 43.1 %gather_qkv.1 = (bf16[2048,768]{1,0:T(8,128)(2,1)}, bf16[2048,192]{1,0:T(8,128)(2,1)}, bf16[2048,192]{1,0:T(8,128)(2,1)}, bf16[2048,192]{1,0:T(8,128)(2,1)}) custom-call(bf16[512,768]{1,0:T(8,128)(2,1)} %x_ref.5, f32[1,768]{1,0:T(1,128)} %broadcast_in_dim.40.gain_ref, f32[1,768]{1,0:T(1,128)} %broadcast_in_dim.41.shift_ref, ...), custom_call_target="tpu_custom_call" | custom-call | tf_op jit(solution)/shard_map/gather_qkv/pallas_call | solution.py:323
  58.3 0.7 fusion.2.ids_ref
  59.0 16.7 %attend.1 = (bf16[2048,192]{1,0:T(8,128)(2,1)}, f32[2048,128]{1,0:T(8,128)}) custom-call(bf16[2048,192]{1,0:T(8,128)(2,1)} %get-tuple-element.42.q_ref, bf16[2048,192]{1,0:T(8,128)(2,1)} %get-tuple-element.43.k_ref, bf16[2048,192]{1,0:T(8,128)(2,1)} %get-tuple-element.44.v_ref, bf16[3,1024,1024]{2,1,0:T(8,128)(2,1)} %table_ref.3, f32[2,1024]{1,0:T(2,128)} %fusion.2.ids_ref), custom_call_target="tpu_custom_call" | custom-call | tf_op jit(solution)/shard_map/attend/pallas_call | solution.py:121
  75.7 26.6 %project.1 = (f32[512,768]{1,0:T(8,128)}, f32[512,768]{1,0:T(8,128)}, bf16[512,768]{1,0:T(8,128)(2,1)}) custom-call(bf16[2048,192]{1,0:T(8,128)(2,1)} %get-tuple-element.45.ctx_ref, bf16[192,768]{1,0:T(8,128)(2,1)} %w_ref.5, bf16[1,768]{1,0:T(2,128)(2,1)} %broadcast_in_dim.43.bias_ref, bf16[512,768]{1,0:T(8,128)(2,1)} %x_ref.5, ...), custom_call_target="tpu_custom_call" | custom-call | tf_op jit(solution)/shard_map/project/pallas_call | solution.py:323
  102.4 44.8 %mlp.1 = (f32[512,768]{1,0:T(8,128)}, bf16[512,768]{1,0:T(8,128)(2,1)}, bf16[2048,768]{1,0:T(8,128)(2,1)}, bf16[768,768]{1,0:T(8,128)(2,1)}, bf16[768,768]{1,0:T(8,128)(2,1)}, /*index=5*/f32[8,768]{1,0:T(8,128)}) custom-call(bf16[512,768]{1,0:T(8,128)(2,1)} %get-tuple-element.47.norm_ref, bf16[2048,768]{1,0:T(8,128)(2,1)} %all-gather.2.cloned.1.call-done.grad_ref, ...), custom_call_target="tpu_custom_call" | custom-call | tf_op jit(solution)/shard_map/mlp/pallas_call | solution.py:323
  147.1 24.8 %gather_back.1 = (bf16[2048,192]{1,0:T(8,128)(2,1)}, bf16[768,192]{1,0:T(8,128)(2,1)}) custom-call(bf16[512,768]{1,0:T(8,128)(2,1)} %get-tuple-element.50.g_ref, bf16[192,768]{1,0:T(8,128)(2,1)} %w_ref.5, bf16[2048,192]{1,0:T(8,128)(2,1)} %get-tuple-element.45.ctx_ref), custom_call_target="tpu_custom_call" | custom-call | tf_op jit(solution)/shard_map/gather_back/pallas_call | solution.py:323
  171.9 32.2 %attend_back.1 = (bf16[2048,192]{1,0:T(8,128)(2,1)}, bf16[2048,192]{1,0:T(8,128)(2,1)}, bf16[2048,192]{1,0:T(8,128)(2,1)}, bf16[8,3,128,640]{3,2,1,0:T(8,128)(2,1)}) custom-call(bf16[2048,192]{1,0:T(8,128)(2,1)} %get-tuple-element.42.q_ref, bf16[2048,192]{1,0:T(8,128)(2,1)} %get-tuple-element.43.k_ref, bf16[2048,192]{1,0:T(8,128)(2,1)} %get-tuple-element.44.v_ref, ...), custom_call_target="tpu_custom_call" | custom-call | tf_op jit(solution)/shard_map/attend_back/pallas_call | solution.py:206
  204.2 29.2 %tail.1 = (f32[512,768]{1,0:T(8,128)}, bf16[768,576]{1,0:T(8,128)(2,1)}, f32[8,768]{1,0:T(8,128)}, f32[2,192]{1,0:T(2,128)}) custom-call(bf16[2048,192]{1,0:T(8,128)(2,1)} %get-tuple-element.53.dq_ref, bf16[2048,192]{1,0:T(8,128)(2,1)} %get-tuple-element.54.dk_ref, bf16[2048,192]{1,0:T(8,128)(2,1)} %get-tuple-element.55.dv_ref, ...), custom_call_target="tpu_custom_call" | custom-call | tf_op jit(solution)/shard_map/tail/pallas_call | solution.py:323
  233.3 2.4 pad_maximum_fusion
  235.8 0.0 reduce-scatter.12.cloned.1.call-start
  235.8 0.7 reduce-scatter.12.cloned.1.call-update
  236.6 0.5 reduce-scatter.14.cloned.1.call-update
  237.1 0.5 reduce-scatter.6.cloned.1.call-update
  237.7 0.0 reduce-scatter.10.cloned.1.call-start
  237.8 0.5 reduce-scatter.10.cloned.1.call-update
  238.3 0.1 copy-done.13
  238.4 0.7 slice.49
  239.2 22.5 %all-reduce = (f32[2,192]{1,0:T(2,128)}, f32[768]{0:T(1024)}) all-reduce(f32[2,192]{1,0:T(2,128)S(1)} %copy-done.14, f32[768]{0:T(1024)S(1)} %get-tuple-element.115), channel_id=1, replica_groups=mesh['dp'=8,'mp'=4] {'dp'}, use_global_device_ids=true, to_apply=%region_5.6 | all-reduce | flops 1152 | bytes 9216 | tf_op jit(solution)/shard_map/psum | solution.py:685
  261.8 39.6 %reduce-scatter.8.cloned.1.call-done = bf16[96,768]{1,0:T(8,128)(2,1)} async-done(((bf16[768,768]{1,0:T(8,128)(2,1)}), bf16[96,768]{1,0:T(8,128)(2,1)}) %reduce-scatter.8.cloned.1.call-update) | async-done | bytes 147472 | tf_op jit(solution)/shard_map/reduce_scatter | solution.py:626
  301.4 0.9 slice.66
  302.3 0.1 copy.42
  302.4 0.9 copy.43
  303.3 0.9 convert_element_type.36
  304.3 0.1 slice_bitcast_fusion
  304.3 0.7 copy.44
  305.1 63.4 %reduce-scatter.12.cloned.1.call-done = bf16[96,768]{1,0:T(8,128)(2,1)} async-done(((bf16[768,768]{1,0:T(8,128)(2,1)}), bf16[96,768]{1,0:T(8,128)(2,1)}) %reduce-scatter.12.cloned.1.call-update) | async-done | bytes 147472 | tf_op jit(solution)/shard_map/reduce_scatter | solution.py:626
  368.5 1.6 convert_element_type.37
  370.1 65.3 %reduce-scatter.14.cloned.1.call-done = bf16[96,768]{1,0:T(8,128)(2,1)} async-done(((bf16[768,768]{1,0:T(8,128)(2,1)}), bf16[96,768]{1,0:T(8,128)(2,1)}) %reduce-scatter.14.cloned.1.call-update) | async-done | bytes 147472 | tf_op jit(solution)/shard_map/reduce_scatter | solution.py:626
  435.4 1.6 convert_bitcast_fusion
  437.1 37.7 %reduce-scatter.6.cloned.1.call-done = bf16[512,768]{1,0:T(8,128)(2,1)} async-done(((bf16[2048,768]{1,0:T(8,128)(2,1)}), bf16[512,768]{1,0:T(8,128)(2,1)}) %reduce-scatter.6.cloned.1.call-update) | async-done | bytes 786448 | tf_op jit(solution)/shard_map/reduce_scatter | solution.py:630
  474.7 2.4 fusion.1
  477.2 42.0 %psum.21 = f32[8,768]{1,0:T(8,128)S(1)} all-reduce(f32[8,768]{1,0:T(8,128)S(1)} %stack.12), channel_id=1, replica_groups=mesh['dp'=8,'mp'=4] {'dp','mp'}, use_global_device_ids=true, to_apply=%region_3.4 | all-reduce | flops 6144 | bytes 49152 | tf_op jit(solution)/shard_map/psum | solution.py:676
  519.2 0.7 slice_reduce_fusion
  519.9 44.5 %reduce-scatter.10.cloned.1.call-done = bf16[384,640]{1,0:T(8,128)(2,1)} async-done(((bf16[3072,640]{1,0:T(8,128)(2,1)}), bf16[384,640]{1,0:T(8,128)(2,1)}) %reduce-scatter.10.cloned.1.call-update) | async-done | bytes 491536 | tf_op jit(solution)/shard_map/reduce_scatter | solution.py:626
  564.4 1.1 convert.2
  565.5 1.3 broadcast_in_dim.48
  566.8 7.5 %dynamic_update_slice.3 = f32[3,128,1024]{2,1,0:T(8,128)} dynamic-update-slice(f32[3,128,1024]{2,1,0:T(8,128)} %broadcast_in_dim.48, f32[3,128,640]{2,1,0:T(8,128)S(1)} %convert.2, s32[]{:T(128)} %constant.26.clone.1, s32[]{:T(128)} %constant.26.clone.1, s32[]{:T(128)S(6)} %min.4) | dynamic-update-slice | bytes 1966084 | tf_op jit(solution)/shard_map/dynamic_update_slice | solution.py:639
  574.3 1.1 copy.47
  (48 shorter events, 0.3 us)
Async XLA Ops:
  7.2 2.5 copy-start.8
  7.2 3.0 copy-start.9
  7.2 3.6 copy-start.3
  7.2 95.1 %all-gather.2.cloned.1.call-start = ((), (), s32[]{:S(2)}) async-start(), calls=%async_computation.5 | async-start | bytes 3932160 | tf_op jit(solution)/shard_map/all_gather | solution.py:654
  9.5 2.7 copy-start.15
  9.5 3.3 copy-start.10
  9.6 3.9 copy-start.11
  9.6 4.4 copy-start.12
  9.6 5.0 copy-start.16
  9.6 291.8 %reduce-scatter.8.cloned.1.call-start = ((), (), s32[]{:S(2)}) async-start(), calls=%async_computation.7 | async-start | bytes 1327104 | tf_op jit(solution)/shard_map/reduce_scatter | solution.py:626
  10.8 47.5 %copy-start.7 = (s32[2,1024]{1,0:T(2,128)S(1)}, s32[2,1024]{1,0:T(2,128)}, u32[]{:S(2)}) copy-start(s32[2,1024]{1,0:T(2,128)} %param.20) | copy-start | bytes 24580
  10.8 47.5 %copy-start.17 = (s32[2]{0:T(128)S(1)}, s32[2]{0:T(128)}, u32[]{:S(2)}) copy-start(s32[2]{0:T(128)} %param.21) | copy-start | bytes 28
  204.1 29.2 %copy-start.4 = (bf16[768,192]{1,0:T(8,128)(2,1)S(1)}, bf16[768,192]{1,0:T(8,128)(2,1)}, u32[]{:S(2)}) copy-start(bf16[768,192]{1,0:T(8,128)(2,1)} %get-tuple-element.62) | copy-start | bytes 884740
  235.8 132.7 %reduce-scatter.12.cloned.1.call-start = ((), (), s32[]{:S(2)}) async-start(), calls=%async_computation.9 | async-start | bytes 1327104 | tf_op jit(solution)/shard_map/reduce_scatter | solution.py:626
  236.5 198.9 %reduce-scatter.14.cloned.1.call-start = ((), (), s32[]{:S(2)}) async-start(), calls=%async_computation.10 | async-start | bytes 1327104 | tf_op jit(solution)/shard_map/reduce_scatter | solution.py:626
  237.1 237.6 %reduce-scatter.6.cloned.1.call-start = ((), (), s32[]{:S(2)}) async-start(), calls=%async_computation.6 | async-start | bytes 3932160 | tf_op jit(solution)/shard_map/reduce_scatter | solution.py:630
  237.7 326.7 %reduce-scatter.10.cloned.1.call-start = ((), (), s32[]{:S(2)}) async-start(), calls=%async_computation.8 | async-start | bytes 4423680 | tf_op jit(solution)/shard_map/reduce_scatter | solution.py:626
  237.7 0.7 copy-start.13
  237.8 1.4 copy-start.6
  237.8 1.4 copy-start.14
  261.7 213.0 %copy-start = (bf16[512,768]{1,0:T(8,128)(2,1)S(1)}, bf16[512,768]{1,0:T(8,128)(2,1)}, u32[]{:S(2)}) copy-start(bf16[512,768]{1,0:T(8,128)(2,1)} %cot_ref.1) | copy-start | bytes 2359300
  261.7 213.0 %copy-start.1 = (f32[512,768]{1,0:T(8,128)S(1)}, f32[512,768]{1,0:T(8,128)}, u32[]{:S(2)}) copy-start(f32[512,768]{1,0:T(8,128)} %get-tuple-element.46.mid_ref) | copy-start | bytes 4718596
  261.7 213.0 %copy-start.5 = (f32[768]{0:T(1024)S(1)}, f32[768]{0:T(1024)}, u32[]{:S(2)}) copy-start(f32[768]{0:T(1024)} %param.36) | copy-start | bytes 9220
  565.5 8.8 %copy-start.2 = (f32[512,768]{1,0:T(8,128)S(1)}, f32[512,768]{1,0:T(8,128)}, u32[]{:S(2)}) copy-start(f32[512,768]{1,0:T(8,128)} %get-tuple-element.136) | copy-start | bytes 4718596
Sparse Core Ops, SparseCore 0:
  10.2 46.3 all-gather.1
  235.9 65.4 reduce-scatter.7
  304.8 63.6 reduce-scatter.11
  371.7 63.6 reduce-scatter.13
  437.8 36.8 reduce-scatter.5
  478.3 86.0 reduce-scatter.9

commit v3 on v2

v3 whole, which is shorter than its diff:
```python
from functools import partial

import jax
import jax.numpy as jnp
from jax import lax
from jax.experimental import pallas as pl
from jax.experimental.pallas import tpu as pltpu
from jax.sharding import PartitionSpec as P

HEAD_DIM = 64
BLOCK = 256
GROUP = 128
CHUNKS = 4
SLOTS = 8
PARTS = 2
PAGE_MOST = 256
BF = jnp.bfloat16
F32 = jnp.float32
MESH = pl.DeviceIdType.MESH
VMEM_MOST = 61 * 1024 * 1024
NT = (((1,), (1,)), ((), ()))
TN = (((0,), (0,)), ((), ()))


def vmem():
    return pl.BlockSpec(memory_space=pltpu.VMEM)


def dot(a, b):
    return jnp.dot(a, b, preferred_element_type=F32)


def dot_nt(a, b):
    return lax.dot_general(a, b, NT, preferred_element_type=F32)


def dot_tn(a, b):
    return lax.dot_general(a, b, TN, preferred_element_type=F32)


def norm_rows(rows, gain, shift):
    centre = rows - jnp.mean(rows, axis=-1, keepdims=True)
    inv_std = lax.rsqrt(jnp.mean(centre * centre, axis=-1, keepdims=True) + 1e-06)
    normed = centre * inv_std
    return (normed * gain + shift, normed, inv_std)


def norm_back(grad_out, normed, inv_std, gain):
    scaled = grad_out * gain
    inner = (
        scaled
        - jnp.mean(scaled, axis=-1, keepdims=True)
        - normed * jnp.mean(scaled * normed, axis=-1, keepdims=True)
    )
    return (inv_std * inner, jnp.sum(grad_out * normed, axis=0), jnp.sum(grad_out, axis=0))


def window(index, length):
    width = min(length, BLOCK + 2 * PAGE_MOST)
    start = jnp.clip(index * BLOCK - PAGE_MOST, 0, length - width)
    return pl.multiple_of(start, 128), width


def band_window(group, length):
    wide = min(length, GROUP + 2 * PAGE_MOST)
    start = jnp.clip(group * GROUP - PAGE_MOST, 0, length - wide)
    return pl.multiple_of(start, 128), wide


def head_lanes(head, cols):
    return lax.broadcasted_iota(jnp.int32, (1, cols), 1) // HEAD_DIM == head


def id_columns(ids_ref, cols_ref, seqs, length):
    for s in range(seqs):
        wide = jnp.broadcast_to(ids_ref[s : s + 1, :], (128, length))
        cols_ref[s * length : (s + 1) * length, :] = wide.T


def loop(count, body):
    lax.fori_loop(0, count, lambda i, _: (body(i), 0)[1], 0)


def neighbours():
    me = lax.axis_index("mp")
    partner = me + 1 - 2 * lax.rem(me, 2)
    return me, partner, lax.rem(me + 2, 4), lax.rem(partner + 2, 4)


def greet(peers):
    barrier = pltpu.get_barrier_semaphore()
    for peer in peers:
        pl.semaphore_signal(barrier, inc=1, device_id=peer, device_id_type=MESH)
    pl.semaphore_wait(barrier, len(peers))


def greet_mp():
    _, partner, cross, _ = neighbours()
    greet(({"mp": partner}, {"mp": cross}))


class Gather:
    def __init__(self, buffer, send, recv):
        self.buffer, self.send, self.recv = buffer, send, recv
        self.size = buffer.shape[0] // 4 // CHUNKS
        self.me, self.partner, self.cross, self.diag = neighbours()

    def rows(self, block, chunk):
        return pl.ds(pl.multiple_of((block * CHUNKS + chunk) * self.size, self.size), self.size)

    def copy(self, kind, block, chunk):
        part = self.buffer.at[self.rows(block, chunk), :]
        return pltpu.make_async_remote_copy(
            src_ref=part, dst_ref=part, send_sem=self.send.at[kind, chunk], recv_sem=self.recv.at[kind, chunk],
            device_id={"mp": self.cross if kind == 0 else self.partner}, device_id_type=MESH,
        )

    def send_own(self, chunk):
        self.copy(0, self.me, chunk).start()
        self.copy(1, self.me, chunk).start()

    def wait_partner(self, chunk):
        self.copy(1, self.partner, chunk).wait_recv()

    def relay(self, chunk):
        self.copy(0, self.cross, chunk).wait_recv()
        self.copy(2, self.cross, chunk).start()

    def wait_diag(self, chunk):
        self.copy(2, self.diag, chunk).wait_recv()

    def drain(self, chunk):
        self.copy(0, self.me, chunk).wait_send()
        self.copy(1, self.me, chunk).wait_send()
        self.copy(2, self.cross, chunk).wait_send()


class Scatter:
    def __init__(self, out, inn, send, recv):
        self.out, self.inn, self.send, self.recv = out, inn, send, recv
        self.size = out.shape[1] // CHUNKS
        self.me, self.partner, self.cross, self.diag = neighbours()

    def rows(self, chunk):
        return pl.ds(pl.multiple_of(chunk * self.size, self.size), self.size)

    def copy(self, kind, chunk):
        return pltpu.make_async_remote_copy(
            src_ref=self.out.at[kind, self.rows(chunk), :], dst_ref=self.inn.at[kind, self.rows(chunk), :],
            send_sem=self.send.at[kind, chunk], recv_sem=self.recv.at[kind, chunk],
            device_id={"mp": self.cross if kind == 1 else self.partner}, device_id_type=MESH,
        )

    def put(self, kind, chunk, value):
        self.out[kind, self.rows(chunk), :] = value.astype(BF)
        self.copy(kind, chunk).start()

    def take(self, kind, chunk):
        self.copy(kind, chunk).wait_recv()
        return self.inn[kind, self.rows(chunk), :].astype(F32)

    def drain(self, chunk, kinds=(0, 1, 2)):
        for kind in kinds:
            self.copy(kind, chunk).wait_send()


def slot_of(place):
    return 4 * lax.rem(place, 2) + 2 * lax.rem(place // 2, 2) + place // 4


def half_of(ref, i):
    size = ref.shape[1] // 2
    return pl.ds(pl.multiple_of(i * size, size), size)


def pack(ref, half, value, at=0):
    size = ref.shape[1]
    for j in range(SLOTS // 2):
        ref[4 * (j % 2) + 2 * (j // 2) + half, :, at : at + value.shape[1]] = value[j * size : (j + 1) * size].astype(BF)


def moves():
    return [pltpu.SemaphoreType.DMA((3, CHUNKS)), pltpu.SemaphoreType.DMA((3, CHUNKS))]


def halves(rows, cols):
    return [pltpu.VMEM((3, rows, cols), BF), pltpu.VMEM((3, rows, cols), BF)] + moves()


def call(kernel, name, number, outs, scratch, *args, far=0):
    return pl.pallas_call(
        kernel,
        out_shape=tuple(jax.ShapeDtypeStruct(shape, dtype) for shape, dtype in outs),
        in_specs=[vmem()] * (len(args) - far) + [pl.BlockSpec(memory_space=pl.ANY)] * far,
        out_specs=tuple(vmem() for _ in outs),
        scratch_shapes=scratch,
        compiler_params=pltpu.CompilerParams(
            vmem_limit_bytes=VMEM_MOST, collective_id=number, has_side_effects=True
        ),
        name=name,
    )(*args)


def attend_block(q_ref, k_ref, v_ref, table_ref, ids_ref, cols_ref, ctx_ref, lse_ref, seq, index):
    cols = q_ref.shape[1]
    length = ids_ref.shape[1]
    base = seq * length
    start, width = window(index, length)
    here = pl.ds(pl.multiple_of(index * BLOCK, BLOCK), BLOCK)
    rows = pl.ds(pl.multiple_of(base + index * BLOCK, BLOCK), BLOCK)
    keys_at = pl.ds(pl.multiple_of(base + start, 128), width)
    query = q_ref[rows, :]
    keys = k_ref[keys_at, :]
    values = v_ref[keys_at, :]
    same = cols_ref[rows, 0:1] == ids_ref[pl.ds(seq, 1), pl.ds(start, width)]
    context = jnp.zeros((BLOCK, cols), F32)
    sums = jnp.zeros((BLOCK, 128), F32)
    lane = lax.broadcasted_iota(jnp.int32, (1, 128), 1)
    for head in range(cols // HEAD_DIM):
        mine = head_lanes(head, cols)
        scores = dot_nt(jnp.where(mine, query, 0), keys)
        scores = jnp.where(same, scores + table_ref[head, here, pl.ds(start, width)].astype(F32), -1e30)
        peak = jnp.max(scores, axis=-1, keepdims=True)
        expo = jnp.exp(scores - peak)
        total = jnp.sum(expo, axis=-1, keepdims=True)
        part = dot(expo.astype(BF), values) * (1.0 / total)
        context = jnp.where(mine, part, context)
        sums = jnp.where(lane == head, peak + jnp.log(total), sums)
    ctx_ref[rows, :] = context.astype(BF)
    lse_ref[rows, :] = sums


def front_kernel(
    x_ref, gain_ref, shift_ref, w_ref, bias_ref, cot_ref, scale_ref, ids_ref, table_hbm,
    rows_ref, grad_ref, q_ref, k_ref, v_ref, ctx_ref, lse_ref,
    table_ref, cols_ref, load, send, recv, gsend, grecv,
):
    net = Gather(rows_ref, send, recv)
    top = Gather(grad_ref, gsend, grecv)
    seqs, length = ids_ref.shape
    fetch = pltpu.make_async_copy(table_hbm, table_ref, load)
    fetch.start()
    greet_mp()

    def own(chunk):
        part = x_ref[pl.ds(pl.multiple_of(chunk * net.size, net.size), net.size), :].astype(F32)
        rows_ref[net.rows(net.me, chunk), :] = norm_rows(part, gain_ref[...], shift_ref[...])[0].astype(BF)
        net.send_own(chunk)

    loop(CHUNKS, own)

    def top_own(chunk):
        part = cot_ref[pl.ds(pl.multiple_of(chunk * net.size, net.size), net.size), :].astype(F32)
        grad_ref[net.rows(net.me, chunk), :] = (part * scale_ref[...]).astype(BF)

    loop(CHUNKS, top_own)
    id_columns(ids_ref, cols_ref, seqs, length)
    tall = 2 * net.size

    def project(block):
        def part(i):
            at = pl.ds(pl.multiple_of(block * CHUNKS * net.size + i * tall, tall), tall)
            rows = rows_ref[at, :]
            query = dot(rows, w_ref[0]) + bias_ref[0:1, :].astype(F32)
            q_ref[at, :] = (query.astype(BF).astype(F32) * 0.125).astype(BF)
            k_ref[at, :] = dot(rows, w_ref[1]).astype(BF)
            v_ref[at, :] = (dot(rows, w_ref[2]) + bias_ref[1:2, :].astype(F32)).astype(BF)

        loop(CHUNKS // 2, part)

    def attend(seq, index):
        attend_block(q_ref, k_ref, v_ref, table_ref, ids_ref, cols_ref, ctx_ref, lse_ref, seq, index)

    project(net.me)
    loop(CHUNKS, net.wait_partner)
    project(net.partner)
    fetch.wait()
    mine = net.me // 2
    steps = length // BLOCK

    def near(i):
        attend(mine, i)
        net.relay(i)
        top.send_own(i)

    loop(steps, near)
    project(net.cross)
    loop(CHUNKS, net.wait_diag)
    project(net.diag)

    def far(i):
        attend(1 - mine, i)
        top.relay(i)
        net.drain(i)

    loop(steps, far)
    for wait in (top.wait_partner, top.wait_diag, top.drain):
        loop(CHUNKS, wait)


def front(patches, gain, shift, weight, bias, cotangent, scale, ids, table):
    rows, width = patches.shape
    cols = weight.shape[2]
    one, wide = ((4 * rows, cols), BF), ((4 * rows, width), BF)
    return call(
        front_kernel, "front", 1, [wide, wide, one, one, one, one, ((4 * rows, 128), F32)],
        [pltpu.VMEM(table.shape, BF), pltpu.VMEM((4 * rows, 128), F32), pltpu.SemaphoreType.DMA] + moves() + moves(),
        patches, gain[None], shift[None], weight, bias, cotangent, scale[None], ids, table, far=1,
    )


def project_kernel(
    ctx_ref, w_ref, bias_ref, x_ref, scale_ref, gain_ref, shift_ref, attn_ref, mid_ref, norm_ref, out, inn, send, recv
):
    net = Scatter(out, inn, send, recv)
    greet_mp()

    def share(block, chunk):
        at = pl.ds(pl.multiple_of((block * CHUNKS + chunk) * net.size, net.size), net.size)
        return dot(ctx_ref[at, :], w_ref[...])

    loop(CHUNKS, lambda c: net.put(0, c, share(net.diag, c)))
    loop(CHUNKS, lambda c: net.put(1, c, share(net.cross, c) + net.take(0, c)))
    loop(CHUNKS, lambda c: net.put(2, c, share(net.partner, c)))

    def own(chunk):
        attn_ref[net.rows(chunk), :] = share(net.me, chunk) + net.take(2, chunk) + bias_ref[...].astype(F32)

    loop(CHUNKS, own)

    def last(chunk):
        at = net.rows(chunk)
        attn = attn_ref[at, :] + net.take(1, chunk)
        middle = x_ref[at, :].astype(F32) + scale_ref[...] * attn
        attn_ref[at, :] = attn
        mid_ref[at, :] = middle
        norm_ref[at, :] = norm_rows(middle, gain_ref[...], shift_ref[...])[0].astype(BF)

    loop(CHUNKS, last)
    loop(CHUNKS, net.drain)


def project(context, weight, bias, patches, scale, gain, shift):
    rows, width = patches.shape
    return call(
        project_kernel, "project", 2, [((rows, width), F32), ((rows, width), F32), ((rows, width), BF)],
        halves(rows, width), context, weight, bias[None], patches, scale[None], gain[None], shift[None],
    )


def gelu_both(u):
    inner = 0.7978845608028654 * (u + 0.044715 * (u * u * u))
    t = jnp.tanh(inner)
    half = 0.5 * (1.0 + t)
    slope = half + (0.5 * u) * (1.0 - t * t) * (0.7978845608028654 * (1.0 + 0.134145 * (u * u)))
    return u * half, slope


def mlp_kernel(
    norm_ref, grad_ref, up_ref, bias_ref, down_ref, mid_ref, attn_ref, cot_ref, gain_ref, scale_ref,
    gmid_ref, gattn_ref, cross_ref, here_ref, upg_ref, downg_ref, sums_ref,
    rows_ref, hid_ref, pre_ref, own_ref, far_ref, mfar_ref, gsend, grecv, out, inn, send, recv,
    mout, minn, msend, mrecv,
):
    gat = Gather(rows_ref, gsend, grecv)
    net = Scatter(out, inn, send, recv)
    top = Scatter(mout, minn, msend, mrecv)
    size = gat.size
    greet_mp()
    sums_ref[...] = jnp.zeros_like(sums_ref)

    def own(chunk):
        rows_ref[gat.rows(gat.me, chunk), :] = norm_ref[net.rows(chunk), :]
        gat.send_own(chunk)

    loop(CHUNKS, own)

    def two(first, second, chunk):
        at, by = gat.rows(first, chunk), gat.rows(second, chunk)
        both = lambda ref: jnp.concatenate([ref[at, :], ref[by, :]], axis=0)
        value, slope = gelu_both(dot(both(rows_ref), up_ref[...]) + bias_ref[...].astype(F32))
        hidden = value.astype(BF)
        hid_ref[at, :], hid_ref[by, :] = hidden[:size], hidden[size:]
        grad_pre = (dot_nt(both(grad_ref), down_ref[...]) * slope).astype(BF)
        pre_ref[at, :], pre_ref[by, :] = grad_pre[:size], grad_pre[size:]
        sums_ref[0:1, :] += jnp.sum(grad_pre.astype(F32), axis=0, keepdims=True)
        back = dot_nt(grad_pre, up_ref[...])
        part = dot(hidden, down_ref[...])
        return back[:size], back[size:], part[:size], part[size:]

    def near(chunk):
        gat.wait_partner(chunk)
        theirs, mine, share, kept = two(gat.partner, gat.me, chunk)
        net.put(2, chunk, theirs)
        top.put(2, chunk, share)
        own_ref[net.rows(chunk), :] = mine
        here_ref[net.rows(chunk), :] = kept

    loop(CHUNKS, near)

    def across(chunk):
        net.put(1, chunk, far_ref[net.rows(chunk), :] + net.take(0, chunk))

    def far(chunk):
        gat.relay(chunk)
        gat.wait_diag(chunk)
        theirs, mine, share, kept = two(gat.diag, gat.cross, chunk)
        net.put(0, chunk, theirs)
        top.put(0, chunk, share)
        far_ref[net.rows(chunk), :] = mine
        mfar_ref[net.rows(chunk), :] = kept

        @pl.when(chunk > 0)
        def _():
            across(chunk - 1)

    loop(CHUNKS, far)
    across(CHUNKS - 1)

    def weights(i):
        pack(upg_ref, i, dot_tn(rows_ref[:, half_of(rows_ref, i)], pre_ref[...]))
        pack(downg_ref, i, dot_tn(grad_ref[:, half_of(grad_ref, i)], hid_ref[...]))

    loop(2, weights)

    def outs(chunk):
        at = net.rows(chunk)
        here_ref[at, :] += top.take(2, chunk)
        cross_ref[at, :] = (mfar_ref[at, :] + top.take(0, chunk)).astype(BF)

    loop(CHUNKS, outs)

    def last(chunk):
        at = net.rows(chunk)
        grad = own_ref[at, :] + net.take(2, chunk) + net.take(1, chunk)
        normed, inv = norm_rows(mid_ref[at, :], 1.0, 0.0)[1:]
        back, gain_sum, shift_sum = norm_back(grad, normed, inv, gain_ref[...])
        middle = cot_ref[at, :].astype(F32) + back
        gattn = (middle * scale_ref[...]).astype(BF)
        gmid_ref[at, :] = middle
        gattn_ref[at, :] = gattn
        sums_ref[1:2, :] += gain_sum[None]
        sums_ref[2:3, :] += shift_sum[None]
        sums_ref[3:4, :] += jnp.sum(middle * attn_ref[at, :], axis=0, keepdims=True)
        sums_ref[4:5, :] += jnp.sum(gattn.astype(F32), axis=0, keepdims=True)

    loop(CHUNKS, last)
    loop(CHUNKS, gat.drain)
    loop(CHUNKS, net.drain)
    loop(CHUNKS, lambda chunk: top.drain(chunk, (0, 2)))


def mlp(normed, grad_rows, up, bias, down, middle, attn, cotangent, gain, scale):
    rows, width = normed.shape
    ff = up.shape[1]
    one = pltpu.VMEM((rows, width), F32)
    packed = ((SLOTS, width // SLOTS, ff), BF)
    return call(
        mlp_kernel, "mlp", 3,
        [((rows, width), F32), ((rows, width), BF), ((rows, width), BF), ((rows, width), F32), packed, packed, ((8, width), F32)],
        [pltpu.VMEM((4 * rows, width), BF), pltpu.VMEM((4 * rows, ff), BF), pltpu.VMEM((4 * rows, ff), BF), one, one, one]
        + moves() + halves(rows, width) + halves(rows, width),
        normed, grad_rows, up, bias[None], down, middle, attn, cotangent, gain[None], scale[None],
    )


class Fold:
    def __init__(self, src, inn, send, recv):
        self.src, self.inn, self.send, self.recv = src, inn, send, recv
        self.size = src.shape[1] // PARTS
        place = lax.axis_index("dp")
        x, lo, hi = lax.rem(place, 2), lax.rem(place // 2, 2), place // 4
        self.peers = (place + 1 - 2 * x, place + 2 - 4 * lo, place + 4 - 8 * hi)
        self.theirs = (4 * (1 - x), 2 * (1 - lo), 4 + 1 - hi)
        self.mine = (4 * x, 2 * lo, 4 + hi)

    def copy(self, stage, part):
        count, offset = (4, 2, 1)[stage], (0, 4, 6)[stage]
        rows = pl.ds(part * self.size, self.size)
        src = self.src if stage == 0 else self.inn
        return pltpu.make_async_remote_copy(
            src_ref=src.at[pl.ds(self.theirs[stage], count), rows, :],
            dst_ref=self.inn.at[pl.ds(offset, count), rows, :],
            send_sem=self.send.at[stage, part], recv_sem=self.recv.at[stage, part],
            device_id={"dp": self.peers[stage]}, device_id_type=MESH,
        )

    def start(self):
        for part in range(PARTS):
            self.copy(0, part).start()

    def advance(self, stage):
        count, offset = (4, 2)[stage], (0, 4)[stage]
        src = self.src if stage == 0 else self.inn
        for part in range(PARTS):
            rows = pl.ds(part * self.size, self.size)
            self.copy(stage, part).wait_recv()
            for i in range(count):
                self.inn[offset + i, rows, :] = self.inn[offset + i, rows, :] + src[self.mine[stage] + i, rows, :]
            self.copy(stage + 1, part).start()

    def finish(self, put):
        for part in range(PARTS):
            rows = pl.ds(part * self.size, self.size)
            self.copy(2, part).wait_recv()
            put(rows, self.inn[self.mine[2], rows, :].astype(F32) + self.inn[6, rows, :].astype(F32))

    def drain(self):
        for stage in range(3):
            for part in range(PARTS):
                self.copy(stage, part).wait_send()


class Total:
    def __init__(self, acc, inn, send, recv):
        self.acc, self.inn, self.send, self.recv = acc, inn, send, recv
        place = lax.axis_index("dp")
        x, lo, hi = lax.rem(place, 2), lax.rem(place // 2, 2), place // 4
        _, partner, cross, _ = neighbours()
        self.peers = (
            {"dp": place + 1 - 2 * x}, {"dp": place + 2 - 4 * lo}, {"dp": place + 4 - 8 * hi}, {"mp": partner}, {"mp": cross},
        )

    def copy(self, stage):
        return pltpu.make_async_remote_copy(
            src_ref=self.acc.at[stage], dst_ref=self.inn.at[stage], send_sem=self.send.at[stage],
            recv_sem=self.recv.at[stage], device_id=self.peers[stage], device_id_type=MESH,
        )

    def start(self, stage):
        self.copy(stage).start()

    def finish(self, stage):
        self.copy(stage).wait_recv()
        self.acc[stage + 1] = self.acc[stage] + self.inn[stage]

    def drain(self):
        for stage in range(5):
            self.copy(stage).wait_send()


def back_kernel(
    fold,
    pw_ref, ctx_ref, q_ref, k_ref, v_ref, lse_ref, ids_ref, w_ref, x_ref, gmid_ref, gain_ref,
    cot_ref, mid_ref, cross_ref, here_ref, dbias_ref, mscale_ref, upg_ref, downg_ref, two_ref, gattn_hbm, rows_hbm, table_hbm,
    *refs,
):
    if fold:
        layer_ref, grad_ref, tab_ref, upo_ref, downo_ref, mixo_ref, sums_ref, *refs = refs
        band_ref, mix_ref, acc_ref, *refs = refs
        winn, wsend, wrecv, tinn, tsend, trecv, ainn, asend, arecv, *refs = refs
    else:
        layer_ref, grad_ref, band_ref, mix_ref, sums_ref, *refs = refs
        acc_ref = None
    (
        table_ref, cols_ref, rowsg_ref, g_ref, qt_ref, gt_ref, dkt_ref, dvt_ref, total_ref, dq_ref, dv_ref,
        far_ref, load, fsend, frecv, gsend, grecv, out, inn, send, recv,
    ) = refs
    dk_ref = g_ref
    own_ref = grad_ref
    gat = Gather(rowsg_ref, gsend, grecv)
    net = Scatter(out, inn, send, recv)
    seqs, length = ids_ref.shape
    rows_all, cols = q_ref.shape
    blocks = length // BLOCK
    heads = cols // HEAD_DIM
    small_ref = acc_ref.at[0] if fold else sums_ref
    me, partner, cross, _ = neighbours()
    whole = CHUNKS * gat.size
    mine_at = pl.ds(pl.multiple_of(me * whole, whole), whole)
    first = pltpu.make_async_copy(gattn_hbm, rowsg_ref.at[mine_at, :], load.at[0])
    first.start()

    def fetch(head):
        at = pl.ds(pl.multiple_of(lax.rem(head, 2) * length, length), length)
        return pltpu.make_async_copy(table_hbm.at[head], table_ref.at[at, :], load.at[1 + head])

    fetch(0).start()
    fetch(1).start()
    far = pltpu.make_async_remote_copy(
        src_ref=cross_ref, dst_ref=far_ref, send_sem=fsend, recv_sem=frecv, device_id={"mp": cross}, device_id_type=MESH
    )
    if fold:
        up = Fold(upg_ref, winn.at[0], wsend.at[0], wrecv.at[0])
        down = Fold(downg_ref, winn.at[1], wsend.at[1], wrecv.at[1])
        mix = Fold(mix_ref, winn.at[2], wsend.at[2], wrecv.at[2])
        tab = lambda head: Fold(band_ref.at[head], tinn.at[head], tsend.at[head], trecv.at[head])
        small = Total(acc_ref, ainn, asend, arecv)
        greet(({"mp": partner}, {"mp": cross}) + tuple({"dp": peer} for peer in up.peers))
    else:
        greet_mp()

    first.wait()
    loop(CHUNKS, gat.send_own)
    if fold:
        up.start()
        down.start()
    id_columns(ids_ref, cols_ref, seqs, length)

    def block(number):
        at = pl.ds(pl.multiple_of(number * whole, whole), whole)
        g_ref[at, :] = dot_nt(rowsg_ref[at, :], pw_ref[...]).astype(BF)

    def tall(i):
        return pl.ds(pl.multiple_of(i * BLOCK, BLOCK), BLOCK)

    def flip_q(i):
        qt_ref[:, tall(i)] = q_ref[tall(i), :].T

    def flip_g(i):
        gt_ref[:, tall(i)] = g_ref[tall(i), :].T

    block(gat.me)
    loop(CHUNKS, gat.wait_partner)
    block(gat.partner)
    loop(rows_all // BLOCK, flip_q)
    dkt_ref[...] = jnp.zeros_like(dkt_ref)
    dvt_ref[...] = jnp.zeros_like(dvt_ref)
    dq_ref[...] = jnp.zeros_like(dq_ref)
    small_ref[...] = jnp.zeros_like(small_ref)
    if fold:
        tab_ref[...] = jnp.zeros_like(tab_ref)
    loop(CHUNKS, gat.relay)
    block(gat.cross)
    loop(CHUNKS, gat.wait_diag)
    block(gat.diag)
    far.start()
    loop(rows_all // BLOCK, flip_g)
    if fold:
        up.advance(0)
    lane = lax.broadcasted_iota(jnp.int32, (1, 128), 1)

    def step(head, index):
        start, width = window(index, length)
        mine = head_lanes(head, cols)
        feats = pl.ds(pl.multiple_of(head * HEAD_DIM, HEAD_DIM), HEAD_DIM)
        bias = table_ref[tall(lax.rem(head, 2) * blocks + index), pl.ds(start, width)].astype(F32)
        for seq in range(seqs):
            base = seq * length
            rows = pl.ds(pl.multiple_of(base + index * BLOCK, BLOCK), BLOCK)
            keys_at = pl.ds(pl.multiple_of(base + start, 128), width)
            keys = k_ref[keys_at, :]
            same = cols_ref[rows, 0:1] == ids_ref[seq : seq + 1, pl.ds(start, width)]
            sums = jnp.sum(jnp.where(lane == head, lse_ref[rows, :], 0.0), axis=-1, keepdims=True)
            scores = dot_nt(jnp.where(mine, q_ref[rows, :], 0), keys) + bias
            probs = jnp.where(same, jnp.exp(scores - sums), 0.0)
            grad_probs = dot_nt(jnp.where(mine, g_ref[rows, :], 0), v_ref[keys_at, :])
            centre = jnp.sum(grad_probs * probs, axis=-1, keepdims=True)
            grad_scores = (probs * (grad_probs - centre)).astype(BF)
            dvt_ref[feats, keys_at] += dot(gt_ref[feats, rows], probs.astype(BF))
            dkt_ref[feats, keys_at] += dot(qt_ref[feats, rows], grad_scores)
            grad_q = (dot(grad_scores, keys) * 0.125).astype(BF)
            dq_ref[rows, :] = jnp.where(mine, grad_q, dq_ref[rows, :])
            if seq == 0:
                total_ref[:, 0:width] = grad_scores.astype(F32)
            else:
                total_ref[:, 0:width] += grad_scores.astype(F32)
        for part in range(BLOCK // GROUP):
            group = index * (BLOCK // GROUP) + part
            first, wide = band_window(group, length)
            offset = pl.multiple_of(first - start, 128)
            value = total_ref[part * GROUP : (part + 1) * GROUP, pl.ds(offset, wide)]
            band_ref[head, slot_of(group), :, :] = value.astype(BF)

    def one_head(head):
        fetch(head).wait()
        loop(blocks, lambda index: step(head, index))

        @pl.when(head + 2 < heads)
        def _():
            fetch(head + 2).start()

        if fold:
            tab(head).start()

            @pl.when(head == 0)
            def _():
                down.advance(0)
                up.advance(1)

            @pl.when(head == 1)
            def _():
                down.advance(1)

            @pl.when(head == 2)
            def _():
                tab(0).advance(0)

    loop(heads, one_head)
    rows_ref = table_ref.at[:, 0 : rowsg_ref.shape[1]]
    again = pltpu.make_async_copy(rows_hbm, rows_ref, load.at[0])
    again.start()

    def unflip(i):
        dk_ref[tall(i), :] = dkt_ref[:, tall(i)].T.astype(BF)
        dv_ref[tall(i), :] = dvt_ref[:, tall(i)].T.astype(BF)

    loop(rows_all // BLOCK, unflip)

    again.wait()

    def weights(i):
        rows = table_ref[:, half_of(rowsg_ref, i)]
        for number, ref in enumerate((dq_ref, dk_ref, dv_ref)):
            pack(mix_ref, i, dot_tn(rows, ref[...]), number * cols)
        pack(mix_ref, i, dot_tn(rowsg_ref[:, half_of(rowsg_ref, i)], ctx_ref[...]), 3 * cols)

    loop(2, weights)

    def put_table(head):
        def put(rows, value):
            first = band_window(lax.axis_index("dp"), length)[0]
            tab_ref[head, rows, pl.ds(first, value.shape[1])] = value
        return put

    def put_to(ref):
        def put(rows, value):
            ref[rows, :] = value
        return put

    if fold:
        mix.start()

    def share(number, chunk):
        at = gat.rows(number, chunk)
        return dot_nt(dq_ref[at, :], w_ref[0]) + dot_nt(dk_ref[at, :], w_ref[1]) + dot_nt(dv_ref[at, :], w_ref[2])

    loop(CHUNKS, lambda c: net.put(0, c, share(net.diag, c)))
    loop(CHUNKS, lambda c: net.put(1, c, share(net.cross, c) + net.take(0, c)))
    if fold:
        up.finish(put_to(upo_ref))
        down.finish(put_to(downo_ref))
        tab(0).advance(1)
        tab(1).advance(0)
    loop(CHUNKS, lambda c: net.put(2, c, share(net.partner, c)))

    def keep(chunk):
        own_ref[net.rows(chunk), :] = share(net.me, chunk) + net.take(2, chunk)

    loop(CHUNKS, keep)
    far.wait_recv()

    def layer(chunk):
        at = net.rows(chunk)
        mlp_out = here_ref[at, :] + far_ref[at, :].astype(F32) + dbias_ref[...].astype(F32)
        layer_ref[at, :] = (mid_ref[at, :] + mscale_ref[...] * mlp_out).astype(BF)
        top = cot_ref[at, :].astype(F32)
        small_ref[7:8, :] += jnp.sum(top * mlp_out, axis=0, keepdims=True)
        low = (top * mscale_ref[...]).astype(BF).astype(F32)
        small_ref[6:7, :] += jnp.sum(low, axis=0, keepdims=True)

    loop(CHUNKS, layer)
    for row, source in ((2, 4), (3, 3), (4, 1), (5, 2), (8, 0)):
        small_ref[row : row + 1, :] = two_ref[source : source + 1, :]
    small_ref[9:10, 0:cols] = jnp.sum(dq_ref[...].astype(F32), axis=0, keepdims=True)
    small_ref[10:11, 0:cols] = jnp.sum(dv_ref[...].astype(F32), axis=0, keepdims=True)
    if fold:
        tab(2).advance(0)
        tab(1).advance(1)
        tab(0).finish(put_table(0))

    def last(chunk):
        at = net.rows(chunk)
        grad = own_ref[at, :] + net.take(1, chunk)
        normed, inv = norm_rows(x_ref[at, :].astype(F32), 1.0, 0.0)[1:]
        back, gain_sum, shift_sum = norm_back(grad, normed, inv, gain_ref[...])
        grad_ref[at, :] = gmid_ref[at, :] + back
        small_ref[0:1, :] += gain_sum[None]
        small_ref[1:2, :] += shift_sum[None]

    loop(CHUNKS, last)
    if fold:
        small.start(0)
        mix.advance(0)
        small.finish(0)
        small.start(1)
        tab(2).advance(1)
        tab(1).finish(put_table(1))
        small.finish(1)
        small.start(2)
        mix.advance(1)
        small.finish(2)
        small.start(3)
        tab(2).finish(put_table(2))
        small.finish(3)
        small.start(4)
        mix.finish(put_to(mixo_ref))
        small.finish(4)
        sums_ref[0:8, :] = acc_ref[5, 0:8, :]
        sums_ref[8:16, :] = acc_ref[3, 8:16, :]
        for piece in (up, down, mix, tab(0), tab(1), tab(2), small):
            piece.drain()
    far.wait_send()
    loop(CHUNKS, gat.drain)
    loop(CHUNKS, net.drain)


def back(fold, length, gattn, rows_one, table, proj, ctx, q, k, v, lse, ids, qkv, patches, gmid, gain, *rest):
    rows, width = patches.shape
    cols = q.shape[1]
    heads = cols // HEAD_DIM
    piece, wide = width // SLOTS, band_window(0, length)[1]
    strip = min(length, BLOCK + 2 * PAGE_MOST)
    band, mix = ((heads, SLOTS, GROUP, wide), BF), ((SLOTS, piece, width), BF)
    outs = [((rows, width), BF), ((rows, width), F32)]
    scratch = []
    if fold:
        sem = pltpu.SemaphoreType.DMA((3, 3, PARTS))
        outs += [((heads, GROUP, length), F32)] + [((piece, width), F32)] * 3
        scratch += [pltpu.VMEM(*band), pltpu.VMEM(*mix), pltpu.VMEM((6, 16, width), F32)]
        scratch += [pltpu.VMEM((3, 7, piece, width), BF), sem, sem, pltpu.VMEM((heads, 7, GROUP, wide), BF), sem, sem]
        scratch += [pltpu.VMEM((5, 16, width), F32), pltpu.SemaphoreType.DMA((5,)), pltpu.SemaphoreType.DMA((5,))]
    else:
        outs += [band, mix]
    outs += [((16, width), F32)]
    one, flat = pltpu.VMEM((4 * rows, cols), BF), pltpu.VMEM((cols, 4 * rows), BF)
    total = pltpu.VMEM((cols, 4 * rows), F32)
    scratch += [
        pltpu.VMEM((2 * length, length), BF), pltpu.VMEM((4 * rows, 128), F32), pltpu.VMEM((4 * rows, width), BF), one,
        flat, flat, total, total, pltpu.VMEM((BLOCK, strip), F32), one, one,
        pltpu.VMEM((rows, width), BF),
        pltpu.SemaphoreType.DMA((1 + heads,)), pltpu.SemaphoreType.DMA, pltpu.SemaphoreType.DMA,
    ] + moves() + halves(rows, width)
    return call(
        partial(back_kernel, fold), "back", 4, outs, scratch,
        proj, ctx, q, k, v, lse, ids, qkv, patches, gmid, gain, *rest, gattn, rows_one, table, far=3,
    )


def scatter_dp(x):
    return lax.psum_scatter(x, "dp", scatter_dimension=0, tiled=True).astype(F32)


def in_order(packed):
    _, rows, cols = packed.shape
    return packed.reshape(2, 2, 2, rows, cols).transpose(2, 1, 0, 3, 4).reshape(SLOTS * rows, cols)


def reduce_table(band, length, n_dp):
    groups, heads, _, wide = band.shape
    shard = length // n_dp
    send = band.reshape(groups, heads, GROUP // shard, shard, wide).swapaxes(1, 2)
    part = scatter_dp(send.reshape(n_dp * heads * shard, wide)).reshape(heads, shard, wide)
    first = band_window(lax.axis_index("dp") * shard // GROUP, length)[0]
    return lax.dynamic_update_slice(jnp.zeros((heads, shard, length), F32), part, (0, 0, first))


def local(
    patches, segment_ids, fill_counts, attn_gain, attn_shift, qkv_weight, qv_bias, rel_table, proj_weight,
    proj_bias, attn_scale, mlp_gain, mlp_shift, up_weight, up_bias, down_weight, down_bias, mlp_scale, cotangent,
):
    n_dp = lax.axis_size("dp")
    seqs, length = segment_ids.shape
    cols = qkv_weight.shape[2]
    places = jnp.arange(length, dtype=jnp.int32)[None]
    ids = jnp.where(places < fill_counts[:, None], segment_ids, -1 - places).astype(F32)
    fold = n_dp == SLOTS and length == SLOTS * GROUP
    rows_one, grad_rows, queries, keys, values, context, lse = front(
        patches, attn_gain, attn_shift, qkv_weight, qv_bias, cotangent, mlp_scale, ids, rel_table
    )
    attn_out, middle, normed_two = project(context, proj_weight, proj_bias, patches, attn_scale, mlp_gain, mlp_shift)
    grad_middle, grad_attn, cross, here, up_local, down_local, sums_two = mlp(
        normed_two, grad_rows, up_weight, up_bias, down_weight, middle, attn_out, cotangent, mlp_gain, attn_scale
    )
    layer_out, patch_grad, *more, sums = back(
        fold, length, grad_attn, rows_one, rel_table, proj_weight, context, queries, keys, values, lse, ids, qkv_weight,
        patches, grad_middle, attn_gain[None], cotangent, middle, cross, here, down_bias[None], mlp_scale[None],
        up_local, down_local, sums_two,
    )
    if fold:
        table_grad, up_grad, down_grad, mixed = more
    else:
        band, mixed = more
        order = [4 * (d % 2) + 2 * (d // 2 % 2) + d // 4 for d in range(SLOTS)]
        table_grad = reduce_table(jnp.stack([band[:, slot] for slot in order]), length, n_dp)
        up_grad, down_grad, mixed = [scatter_dp(in_order(piece)) for piece in (up_local, down_local, mixed)]
        sums = jnp.concatenate([lax.psum(sums[:8], ("dp", "mp")), lax.psum(sums[8:], "dp")])
    qkv_grad = mixed[:, : 3 * cols].reshape(-1, 3, cols).swapaxes(0, 1)
    return (
        layer_out, patch_grad, sums[0], sums[1], qkv_grad, sums[9:11, :cols], table_grad, mixed[:, 3 * cols :].T,
        sums[2], sums[3], sums[4], sums[5], up_grad, sums[8], down_grad.T, sums[6], sums[7],
    )


def solution(mesh):
    rows, split = P(("dp", "mp"), None), P("mp", None)
    placed = (
        rows, P("dp", None), P("dp"), P(), P(), P(None, None, "mp"), P(None, "mp"), P("mp", None, None), split,
        P(), P(), P(), P(), P(None, "mp"), P("mp"), split, P(), P(), rows,
    )
    given = (
        rows, rows, P(), P(), P(None, "dp", "mp"), P(None, "mp"), P("mp", "dp", None), P("mp", "dp"), P(), P(),
        P(), P(), P("dp", "mp"), P("mp"), P("mp", "dp"), P(), P(),
    )
    return jax.shard_map(local, mesh=mesh, in_specs=placed, out_specs=given, check_vma=False)
```

time: 583 us -> 252 us (0.43)
  waiting for transfers between devices: 253 us -> 0 us
  blocking collectives: 64.5 us -> 0 us
  Pallas kernels: 217 us -> 232 us
  between operations: 14.4 us -> 0.82 us
  other arithmetic: 13.1 us -> 0.68 us
    reduce_scatter x5 -> x0, waiting for transfers between devices: 251 us -> none  [the longest x4 213 us: scatter_dp(): lax.psum_scatter(x, 'dp', scatter_dimension=0, tiled=True).astype(F32)]
    psum x2 -> x0, blocking collectives: 64.5 us -> none  [the longest x1 42 us: local(): lax.psum(jnp.stack([sums_one[0], sums_one[1], sums_two[4], sums_two[3], s...]
    pallas_call x5 -> x4, Pallas kernels: 168 us -> 232 us  [call(): pl.pallas_call(kernel, out_shape=tuple((jax.ShapeDtypeStruct(shape, dtype...]
    pallas_call x2 -> x0, Pallas kernels: 48.9 us -> none  [the longest x1 32.2 us: attend_back(): pl.pallas_call(partial(attend_back_kernel, seqs, length, heads), out_shap...]
    dynamic_update_slice x1 -> x0, local copies, waits for them, and re-layouts: 7.45 us -> none  [reduce_table(): lax.dynamic_update_slice(jnp.zeros((heads, shard, length), F32), part, (0...]
  transfers between devices with their start and end apart: 6 -> 0, of which waited for: 5 -> 0; matrix products, arithmetic and copies ran while one was open for 3% -> 0% of each run, Pallas kernels for 15% -> 0%
where the time goes in v3:
time: 252 us
  Pallas kernels  232 us (92%)
  local copies, waits for them, and re-layouts  18.1 us (7%)
    pallas_call x4, Pallas kernels, call(): pl.pallas_call(kernel, out_shape=tuple((jax.ShapeDtypeStruct(shape, dtype...  232 us
    unnamed x42, local copies, waits for them, and re-layouts  9.46 us

profile of v3, /device:TPU:0, one launch (start us, length us, event | category | flops | bytes accessed | tf_op | source)
XLA Modules:
  0.0 251.6 jit_solution(7127284882135666764)
XLA Ops:
  0.7 0.0 copy-start.6
  0.7 0.0 copy-start.16
  0.7 0.0 copy-start.7
  0.7 0.0 copy-start.8
  0.7 0.0 copy-start.9
  0.7 2.3 copy.40.w_ref
  3.1 0.0 copy-done.6
  3.1 0.0 copy-done.16
  3.1 0.7 fusion.ids_ref
  3.7 0.0 copy-done.7
  3.7 0.6 broadcast_in_dim.41.gain_ref
  4.3 0.0 copy-done.8
  4.3 0.6 broadcast_in_dim.43.scale_ref.mscale_ref
  4.9 0.0 copy-done.9
  4.9 0.6 broadcast_in_dim.42.shift_ref
  5.5 45.8 %front.1 = (bf16[2048,768]{1,0:T(8,128)(2,1)}, bf16[2048,768]{1,0:T(8,128)(2,1)}, bf16[2048,192]{1,0:T(8,128)(2,1)}, bf16[2048,192]{1,0:T(8,128)(2,1)}, bf16[204...) custom-call(bf16[512,768]{1,0:T(8,128)(2,1)} %x_ref.5, f32[1,768]{1,0:T(1,128)} %broadcast_in_dim.41.gain_ref, ...), custom_call_target="tpu_custom_call" | custom-call | tf_op jit(solution)/shard_map/front/pallas_call | solution.py:191
  51.3 0.0 copy-start.14
  51.4 0.0 copy-done.10
  51.4 0.6 broadcast_in_dim.46.scale_ref
  51.9 0.0 copy-done.11
  51.9 0.6 broadcast_in_dim.47.gain_ref
  52.5 0.0 copy-done.13
  52.5 0.6 broadcast_in_dim.45.bias_ref
  53.1 0.0 copy-done.12
  53.1 0.6 broadcast_in_dim.48.shift_ref
  53.7 25.6 %project.1 = (f32[512,768]{1,0:T(8,128)}, f32[512,768]{1,0:T(8,128)}, bf16[512,768]{1,0:T(8,128)(2,1)}) custom-call(bf16[2048,192]{1,0:T(8,128)(2,1)} %get-tuple-element.41.ctx_ref, bf16[192,768]{1,0:T(8,128)(2,1)} %pw_ref.1, bf16[1,768]{1,0:T(2,128)(2,1)} %broadcast_in_dim.45.bias_ref, bf16[512,768]{1,0:T(8,128)(2,1)} %x_ref.5, ...), custom_call_target="tpu_custom_call" | custom-call | tf_op jit(solution)/shard_map/project/pallas_call | solution.py:191
  79.3 0.0 copy-done.14
  79.3 0.6 broadcast_in_dim.49.bias_ref
  79.9 44.2 %mlp.1 = (f32[512,768]{1,0:T(8,128)}, bf16[512,768]{1,0:T(8,128)(2,1)}, bf16[512,768]{1,0:T(8,128)(2,1)}, f32[512,768]{1,0:T(8,128)}, bf16[8,96,768]{2,1,0:T(8,1...) custom-call(bf16[512,768]{1,0:T(8,128)(2,1)} %get-tuple-element.46.norm_ref, ...), custom_call_target="tpu_custom_call" | custom-call | tf_op jit(solution)/shard_map/mlp/pallas_call | solution.py:191
  124.1 0.0 copy-done.15
  124.1 0.6 broadcast_in_dim.50.dbias_ref
  124.7 116.4 %back.1 = (bf16[512,768]{1,0:T(8,128)(2,1)}, f32[512,768]{1,0:T(8,128)}, f32[3,128,1024]{2,1,0:T(8,128)}, f32[96,768]{1,0:T(8,128)}, f32[96,768]{1,0:T(8,128)}, /*index=5*/f32[96,768]{1,0:T(8,128)}, f32[16,768]{1,0:T(8,128)}) custom-call(bf16[192,768]{1,0:T(8,128)(2,1)} %pw_ref.1, bf16[2048,192]{1,0:T(8,128)(2,1)} %get-tuple-element.41.ctx_ref, ...), custom_call_target="tpu_custom_call" | custom-call | tf_op jit(solution)/shard_map/back/pallas_call | solution.py:191
  241.1 0.0 copy-start.5
  241.1 0.0 copy-start.2
  241.1 1.0 slice.38
  242.2 0.0 copy-start.1
  242.2 0.1 copy.42
  242.3 0.9 copy.43
  243.2 1.0 slice_bitcast_fusion
  244.2 0.7 copy.44
  244.9 0.7 slice_reduce_fusion
  245.6 0.6 slice.39
  246.2 0.9 copy.50
  247.1 1.1 copy.51
  248.2 0.8 copy-done
  249.0 1.1 copy.52
  250.2 0.7 copy.53
  250.9 0.7 copy.54
  (14 shorter events, 0.0 us)
Async XLA Ops:
  0.7 2.4 copy-start.6
  0.7 2.4 copy-start.16
  0.7 3.1 %copy-start.7 = (f32[768]{0:T(1024)S(1)}, f32[768]{0:T(1024)}, u32[]{:S(2)}) copy-start(f32[768]{0:T(1024)} %param.22) | copy-start | bytes 9220
  0.7 3.6 %copy-start.8 = (f32[768]{0:T(1024)S(1)}, f32[768]{0:T(1024)}, u32[]{:S(2)}) copy-start(f32[768]{0:T(1024)} %param.36) | copy-start | bytes 9220
  0.7 4.2 %copy-start.9 = (f32[768]{0:T(1024)S(1)}, f32[768]{0:T(1024)}, u32[]{:S(2)}) copy-start(f32[768]{0:T(1024)} %param.23) | copy-start | bytes 9220
  5.5 45.9 %copy-start.10 = (f32[768]{0:T(1024)S(1)}, f32[768]{0:T(1024)}, u32[]{:S(2)}) copy-start(f32[768]{0:T(1024)} %param.29) | copy-start | bytes 9220
  5.5 46.5 %copy-start.11 = (f32[768]{0:T(1024)S(1)}, f32[768]{0:T(1024)}, u32[]{:S(2)}) copy-start(f32[768]{0:T(1024)} %param.30) | copy-start | bytes 9220
  5.5 47.0 %copy-start.13 = (bf16[768]{0:T(1024)(128)(2,1)S(1)}, bf16[768]{0:T(1024)(128)(2,1)}, u32[]{:S(2)}) copy-start(bf16[768]{0:T(1024)(128)(2,1)} %param.28) | copy-start | bytes 4612
  5.5 47.6 %copy-start.12 = (f32[768]{0:T(1024)S(1)}, f32[768]{0:T(1024)}, u32[]{:S(2)}) copy-start(f32[768]{0:T(1024)} %param.31) | copy-start | bytes 9220
  51.3 27.9 %copy-start.14 = (bf16[768]{0:T(1024)(128)(2,1)S(1)}, bf16[768]{0:T(1024)(128)(2,1)}, u32[]{:S(2)}) copy-start(bf16[768]{0:T(1024)(128)(2,1)} %param.33) | copy-start | bytes 4612
  79.9 44.2 %copy-start.15 = (bf16[768]{0:T(1024)(128)(2,1)S(1)}, bf16[768]{0:T(1024)(128)(2,1)}, u32[]{:S(2)}) copy-start(bf16[768]{0:T(1024)(128)(2,1)} %param.35) | copy-start | bytes 4612
  241.1 3.8 %copy-start.5 = (f32[16,768]{1,0:T(8,128)S(1)}, f32[16,768]{1,0:T(8,128)}, u32[]{:S(2)}) copy-start(f32[16,768]{1,0:T(8,128)} %get-tuple-element.60) | copy-start | bytes 147460
  241.1 5.1 %copy-start.2 = (bf16[512,768]{1,0:T(8,128)(2,1)S(1)}, bf16[512,768]{1,0:T(8,128)(2,1)}, u32[]{:S(2)}) copy-start(bf16[512,768]{1,0:T(8,128)(2,1)} %get-tuple-element.125) | copy-start | bytes 2359300
  242.2 4.9 %copy-start.1 = (f32[512,768]{1,0:T(8,128)S(1)}, f32[512,768]{1,0:T(8,128)}, u32[]{:S(2)}) copy-start(f32[512,768]{1,0:T(8,128)} %get-tuple-element.126) | copy-start | bytes 4718596
  247.1 2.0 copy-start
  249.0 1.1 copy-start.4
  249.0 1.9 copy-start.3

commit v4 on v3

--- a/solution.py
+++ b/solution.py
@@ -10,9 +10,12 @@
 HEAD_DIM = 64
 BLOCK = 256
 GROUP = 128
+ATTN_GAIN, ATTN_SHIFT, PROJ_BIAS, ATTN_SCALE, MLP_GAIN, MLP_SHIFT, UP_BIAS, DOWN_BIAS, MLP_SCALE = range(9)
 CHUNKS = 4
 SLOTS = 8
 PARTS = 2
+EARLY = 15
+MIX_ORDER = (1, 2, 0)
 PAGE_MOST = 256
 BF = jnp.bfloat16
 F32 = jnp.float32
@@ -173,10 +176,12 @@
     return pl.ds(pl.multiple_of(i * size, size), size)
 
 
-def pack(ref, half, value, at=0):
+def pack(ref, half, value, at=0, order=(0, 1, 2)):
     size = ref.shape[1]
     for j in range(SLOTS // 2):
-        ref[4 * (j % 2) + 2 * (j // 2) + half, :, at : at + value.shape[1]] = value[j * size : (j + 1) * size].astype(BF)
+        bits = (j % 2, j // 2, half)
+        slot = 4 * bits[order[0]] + 2 * bits[order[1]] + bits[order[2]]
+        ref[slot, :, at : at + value.shape[1]] = value[j * size : (j + 1) * size].astype(BF)
 
 
 def moves():
@@ -187,12 +192,34 @@
     return [pltpu.VMEM((3, rows, cols), BF), pltpu.VMEM((3, rows, cols), BF)] + moves()
 
 
-def call(kernel, name, number, outs, scratch, *args, far=0):
+class Moves:
+    def __init__(self, sem, pairs):
+        self.copies = [pltpu.make_async_copy(src, dst, sem.at[i]) for i, (src, dst) in enumerate(pairs)]
+
+    def start(self, *which):
+        for i in which:
+            self.copies[i].start()
+
+    def wait(self, *which):
+        for i in which:
+            self.copies[i].wait()
+
+
+def row(ref, number):
+    return ref[number : number + 1, :]
+
+
+def like(*arrays):
+    return [pltpu.VMEM(a.shape, a.dtype) for a in arrays]
+
+
+def call(kernel, name, number, outs, scratch, *args, far=0, far_out=0):
+    anywhere = pl.BlockSpec(memory_space=pl.ANY)
     return pl.pallas_call(
         kernel,
         out_shape=tuple(jax.ShapeDtypeStruct(shape, dtype) for shape, dtype in outs),
-        in_specs=[vmem()] * (len(args) - far) + [pl.BlockSpec(memory_space=pl.ANY)] * far,
-        out_specs=tuple(vmem() for _ in outs),
+        in_specs=[vmem()] * (len(args) - far) + [anywhere] * far,
+        out_specs=tuple([vmem()] * (len(outs) - far_out) + [anywhere] * far_out),
         scratch_shapes=scratch,
         compiler_params=pltpu.CompilerParams(
             vmem_limit_bytes=VMEM_MOST, collective_id=number, has_side_effects=True
@@ -231,27 +258,30 @@
 
 
 def front_kernel(
-    x_ref, gain_ref, shift_ref, w_ref, bias_ref, cot_ref, scale_ref, ids_ref, table_hbm,
-    rows_ref, grad_ref, q_ref, k_ref, v_ref, ctx_ref, lse_ref,
-    table_ref, cols_ref, load, send, recv, gsend, grecv,
+    x_ref, par_ref, w_ref, bias_ref, cot_ref, ids_ref, table_hbm,
+    ctx_ref, lse_ref, rows_hbm, grad_hbm, q_hbm, k_hbm, v_hbm,
+    table_ref, cols_ref, rows_ref, grad_ref, q_ref, k_ref, v_ref, load, send, recv, gsend, grecv,
 ):
     net = Gather(rows_ref, send, recv)
     top = Gather(grad_ref, gsend, grecv)
     seqs, length = ids_ref.shape
-    fetch = pltpu.make_async_copy(table_hbm, table_ref, load)
-    fetch.start()
+    moves = Moves(
+        load,
+        ((table_hbm, table_ref), (rows_ref, rows_hbm), (grad_ref, grad_hbm), (q_ref, q_hbm), (k_ref, k_hbm), (v_ref, v_hbm)),
+    )
+    moves.start(0)
     greet_mp()
 
     def own(chunk):
         part = x_ref[pl.ds(pl.multiple_of(chunk * net.size, net.size), net.size), :].astype(F32)
-        rows_ref[net.rows(net.me, chunk), :] = norm_rows(part, gain_ref[...], shift_ref[...])[0].astype(BF)
+        rows_ref[net.rows(net.me, chunk), :] = norm_rows(part, row(par_ref, ATTN_GAIN), row(par_ref, ATTN_SHIFT))[0].astype(BF)
         net.send_own(chunk)
 
     loop(CHUNKS, own)
 
     def top_own(chunk):
         part = cot_ref[pl.ds(pl.multiple_of(chunk * net.size, net.size), net.size), :].astype(F32)
-        grad_ref[net.rows(net.me, chunk), :] = (part * scale_ref[...]).astype(BF)
+        grad_ref[net.rows(net.me, chunk), :] = (part * row(par_ref, MLP_SCALE)).astype(BF)
 
     loop(CHUNKS, top_own)
     id_columns(ids_ref, cols_ref, seqs, length)
@@ -261,10 +291,10 @@
         def part(i):
             at = pl.ds(pl.multiple_of(block * CHUNKS * net.size + i * tall, tall), tall)
             rows = rows_ref[at, :]
-            query = dot(rows, w_ref[0]) + bias_ref[0:1, :].astype(F32)
+            query = dot_nt(rows, w_ref[0]) + bias_ref[0:1, :].astype(F32)
             q_ref[at, :] = (query.astype(BF).astype(F32) * 0.125).astype(BF)
-            k_ref[at, :] = dot(rows, w_ref[1]).astype(BF)
-            v_ref[at, :] = (dot(rows, w_ref[2]) + bias_ref[1:2, :].astype(F32)).astype(BF)
+            k_ref[at, :] = dot_nt(rows, w_ref[1]).astype(BF)
+            v_ref[at, :] = (dot_nt(rows, w_ref[2]) + bias_ref[1:2, :].astype(F32)).astype(BF)
 
         loop(CHUNKS // 2, part)
 
@@ -274,7 +304,7 @@
     project(net.me)
     loop(CHUNKS, net.wait_partner)
     project(net.partner)
-    fetch.wait()
+    moves.wait(0)
     mine = net.me // 2
     steps = length // BLOCK
 
@@ -287,6 +317,7 @@
     project(net.cross)
     loop(CHUNKS, net.wait_diag)
     project(net.diag)
+    moves.start(1, 3, 4, 5)
 
     def far(i):
         attend(1 - mine, i)
@@ -294,23 +325,28 @@
         net.drain(i)
 
     loop(steps, far)
-    for wait in (top.wait_partner, top.wait_diag, top.drain):
+    for wait in (top.wait_partner, top.wait_diag):
         loop(CHUNKS, wait)
-
-
-def front(patches, gain, shift, weight, bias, cotangent, scale, ids, table):
+    moves.start(2)
+    loop(CHUNKS, top.drain)
+    moves.wait(1, 2, 3, 4, 5)
+
+
+def front(patches, params, weight, bias, cotangent, ids, table):
     rows, width = patches.shape
-    cols = weight.shape[2]
+    cols = weight.shape[1]
     one, wide = ((4 * rows, cols), BF), ((4 * rows, width), BF)
     return call(
-        front_kernel, "front", 1, [wide, wide, one, one, one, one, ((4 * rows, 128), F32)],
-        [pltpu.VMEM(table.shape, BF), pltpu.VMEM((4 * rows, 128), F32), pltpu.SemaphoreType.DMA] + moves() + moves(),
-        patches, gain[None], shift[None], weight, bias, cotangent, scale[None], ids, table, far=1,
+        front_kernel, "front", 1, [one, ((4 * rows, 128), F32), wide, wide, one, one, one],
+        [pltpu.VMEM(table.shape, BF), pltpu.VMEM((4 * rows, 128), F32)]
+        + [pltpu.VMEM(*shape) for shape in (wide, wide, one, one, one)]
+        + [pltpu.SemaphoreType.DMA((6,))] + moves() + moves(),
+        patches, params, weight, bias, cotangent, ids, table, far=1, far_out=5,
     )
 
 
 def project_kernel(
-    ctx_ref, w_ref, bias_ref, x_ref, scale_ref, gain_ref, shift_ref, attn_ref, mid_ref, norm_ref, out, inn, send, recv
+    ctx_ref, w_ref, x_ref, par_ref, attn_ref, mid_ref, norm_ref, out, inn, send, recv
 ):
     net = Scatter(out, inn, send, recv)
     greet_mp()
@@ -324,27 +360,27 @@
     loop(CHUNKS, lambda c: net.put(2, c, share(net.partner, c)))
 
     def own(chunk):
-        attn_ref[net.rows(chunk), :] = share(net.me, chunk) + net.take(2, chunk) + bias_ref[...].astype(F32)
+        attn_ref[net.rows(chunk), :] = share(net.me, chunk) + net.take(2, chunk) + row(par_ref, PROJ_BIAS)
 
     loop(CHUNKS, own)
 
     def last(chunk):
         at = net.rows(chunk)
         attn = attn_ref[at, :] + net.take(1, chunk)
-        middle = x_ref[at, :].astype(F32) + scale_ref[...] * attn
+        middle = x_ref[at, :].astype(F32) + row(par_ref, ATTN_SCALE) * attn
         attn_ref[at, :] = attn
         mid_ref[at, :] = middle
-        norm_ref[at, :] = norm_rows(middle, gain_ref[...], shift_ref[...])[0].astype(BF)
+        norm_ref[at, :] = norm_rows(middle, row(par_ref, MLP_GAIN), row(par_ref, MLP_SHIFT))[0].astype(BF)
 
     loop(CHUNKS, last)
     loop(CHUNKS, net.drain)
 
 
-def project(context, weight, bias, patches, scale, gain, shift):
+def project(context, weight, patches, params):
     rows, width = patches.shape
     return call(
         project_kernel, "project", 2, [((rows, width), F32), ((rows, width), F32), ((rows, width), BF)],
-        halves(rows, width), context, weight, bias[None], patches, scale[None], gain[None], shift[None],
+        halves(rows, width), context, weight, patches, params,
     )
 
 
@@ -357,8 +393,9 @@
 
 
 def mlp_kernel(
-    norm_ref, grad_ref, up_ref, bias_ref, down_ref, mid_ref, attn_ref, cot_ref, gain_ref, scale_ref,
-    gmid_ref, gattn_ref, cross_ref, here_ref, upg_ref, downg_ref, sums_ref,
+    norm_ref, par_ref, up_hbm, down_hbm, grad_hbm, mid_hbm, attn_hbm, cot_hbm,
+    gmid_ref, gattn_ref, sums_ref, cross_hbm, here_hbm, upg_hbm, downg_hbm,
+    up_ref, down_ref, grad_ref, mid_ref, attn_ref, cot_ref, cross_ref, here_ref, upg_ref, downg_ref, load,
     rows_ref, hid_ref, pre_ref, own_ref, far_ref, mfar_ref, gsend, grecv, out, inn, send, recv,
     mout, minn, msend, mrecv,
 ):
@@ -366,6 +403,14 @@
     net = Scatter(out, inn, send, recv)
     top = Scatter(mout, minn, msend, mrecv)
     size = gat.size
+    moves = Moves(
+        load,
+        (
+            (up_hbm, up_ref), (down_hbm, down_ref), (grad_hbm, grad_ref), (mid_hbm, mid_ref), (attn_hbm, attn_ref),
+            (cot_hbm, cot_ref), (cross_ref, cross_hbm), (here_ref, here_hbm), (upg_ref, upg_hbm), (downg_ref, downg_hbm),
+        ),
+    )
+    moves.start(0, 1, 2, 3, 4, 5)
     greet_mp()
     sums_ref[...] = jnp.zeros_like(sums_ref)
 
@@ -375,10 +420,12 @@
 
     loop(CHUNKS, own)
 
+    moves.wait(0, 1, 2)
+
     def two(first, second, chunk):
         at, by = gat.rows(first, chunk), gat.rows(second, chunk)
         both = lambda ref: jnp.concatenate([ref[at, :], ref[by, :]], axis=0)
-        value, slope = gelu_both(dot(both(rows_ref), up_ref[...]) + bias_ref[...].astype(F32))
+        value, slope = gelu_both(dot(both(rows_ref), up_ref[...]) + row(par_ref, UP_BIAS))
         hidden = value.astype(BF)
         hid_ref[at, :], hid_ref[by, :] = hidden[:size], hidden[size:]
         grad_pre = (dot_nt(both(grad_ref), down_ref[...]) * slope).astype(BF)
@@ -429,14 +476,16 @@
         cross_ref[at, :] = (mfar_ref[at, :] + top.take(0, chunk)).astype(BF)
 
     loop(CHUNKS, outs)
+    moves.start(6, 7, 8, 9)
+    moves.wait(3, 4, 5)
 
     def last(chunk):
         at = net.rows(chunk)
         grad = own_ref[at, :] + net.take(2, chunk) + net.take(1, chunk)
         normed, inv = norm_rows(mid_ref[at, :], 1.0, 0.0)[1:]
-        back, gain_sum, shift_sum = norm_back(grad, normed, inv, gain_ref[...])
+        back, gain_sum, shift_sum = norm_back(grad, normed, inv, row(par_ref, MLP_GAIN))
         middle = cot_ref[at, :].astype(F32) + back
-        gattn = (middle * scale_ref[...]).astype(BF)
+        gattn = (middle * row(par_ref, ATTN_SCALE)).astype(BF)
         gmid_ref[at, :] = middle
         gattn_ref[at, :] = gattn
         sums_ref[1:2, :] += gain_sum[None]
@@ -448,31 +497,36 @@
     loop(CHUNKS, gat.drain)
     loop(CHUNKS, net.drain)
     loop(CHUNKS, lambda chunk: top.drain(chunk, (0, 2)))
-
-
-def mlp(normed, grad_rows, up, bias, down, middle, attn, cotangent, gain, scale):
+    moves.wait(6, 7, 8, 9)
+
+
+def mlp(normed, params, up, down, grad_rows, middle, attn, cotangent):
     rows, width = normed.shape
     ff = up.shape[1]
     one = pltpu.VMEM((rows, width), F32)
     packed = ((SLOTS, width // SLOTS, ff), BF)
+    late = [((rows, width), BF), ((rows, width), F32), packed, packed]
     return call(
         mlp_kernel, "mlp", 3,
-        [((rows, width), F32), ((rows, width), BF), ((rows, width), BF), ((rows, width), F32), packed, packed, ((8, width), F32)],
-        [pltpu.VMEM((4 * rows, width), BF), pltpu.VMEM((4 * rows, ff), BF), pltpu.VMEM((4 * rows, ff), BF), one, one, one]
+        [((rows, width), F32), ((rows, width), BF), ((8, width), F32)] + late,
+        like(up, down, grad_rows, middle, attn, cotangent) + [pltpu.VMEM(*shape) for shape in late]
+        + [pltpu.SemaphoreType.DMA((10,))]
+        + [pltpu.VMEM((4 * rows, width), BF), pltpu.VMEM((4 * rows, ff), BF), pltpu.VMEM((4 * rows, ff), BF), one, one, one]
         + moves() + halves(rows, width) + halves(rows, width),
-        normed, grad_rows, up, bias[None], down, middle, attn, cotangent, gain[None], scale[None],
+        normed, params, up, down, grad_rows, middle, attn, cotangent, far=6, far_out=4,
     )
 
 
 class Fold:
-    def __init__(self, src, inn, send, recv):
+    def __init__(self, src, inn, send, recv, order=(0, 1, 2)):
         self.src, self.inn, self.send, self.recv = src, inn, send, recv
         self.size = src.shape[1] // PARTS
         place = lax.axis_index("dp")
-        x, lo, hi = lax.rem(place, 2), lax.rem(place // 2, 2), place // 4
-        self.peers = (place + 1 - 2 * x, place + 2 - 4 * lo, place + 4 - 8 * hi)
-        self.theirs = (4 * (1 - x), 2 * (1 - lo), 4 + 1 - hi)
-        self.mine = (4 * x, 2 * lo, 4 + hi)
+        bits = (lax.rem(place, 2), lax.rem(place // 2, 2), place // 4)
+        a, b, c = [bits[i] for i in order]
+        self.peers = [place + (1 << i) - (2 << i) * bits[i] for i in order]
+        self.theirs = (4 * (1 - a), 2 * (1 - b), 4 + 1 - c)
+        self.mine = (4 * a, 2 * b, 4 + c)
 
     def copy(self, stage, part):
         count, offset = (4, 2, 1)[stage], (0, 4, 6)[stage]
@@ -541,10 +595,9 @@
 
 def back_kernel(
     fold,
-    pw_ref, ctx_ref, q_ref, k_ref, v_ref, lse_ref, ids_ref, w_ref, x_ref, gmid_ref, gain_ref,
-    cot_ref, mid_ref, cross_ref, here_ref, dbias_ref, mscale_ref, upg_ref, downg_ref, two_ref, gattn_hbm, rows_hbm, table_hbm,
-    *refs,
+    pw_ref, ids_ref, par_ref, two_ref, rows_hbm, table_hbm, *refs,
 ):
+    early, refs = refs[:EARLY], refs[EARLY:]
     if fold:
         layer_ref, grad_ref, tab_ref, upo_ref, downo_ref, mixo_ref, sums_ref, *refs = refs
         band_ref, mix_ref, acc_ref, *refs = refs
@@ -552,9 +605,11 @@
     else:
         layer_ref, grad_ref, band_ref, mix_ref, sums_ref, *refs = refs
         acc_ref = None
+    held, refs = refs[: EARLY - 1], refs[EARLY - 1 :]
+    upg_ref, downg_ref, q_ref, k_ref, v_ref, lse_ref, cross_ref, ctx_ref, w_ref, here_ref, mid_ref, cot_ref, x_ref, gmid_ref = held
     (
-        table_ref, cols_ref, rowsg_ref, g_ref, qt_ref, gt_ref, dkt_ref, dvt_ref, total_ref, dq_ref, dv_ref,
-        far_ref, load, fsend, frecv, gsend, grecv, out, inn, send, recv,
+        table_ref, cols_ref, rowsg_ref, g_ref, qt_ref, gt_ref, dkt_ref, dvt_ref, strip_ref, dq_ref, dv_ref,
+        far_ref, load, hold, fsend, frecv, gsend, grecv, out, inn, send, recv,
     ) = refs
     dk_ref = g_ref
     own_ref = grad_ref
@@ -568,8 +623,8 @@
     me, partner, cross, _ = neighbours()
     whole = CHUNKS * gat.size
     mine_at = pl.ds(pl.multiple_of(me * whole, whole), whole)
-    first = pltpu.make_async_copy(gattn_hbm, rowsg_ref.at[mine_at, :], load.at[0])
-    first.start()
+    moves = Moves(hold, [(early[0], rowsg_ref.at[mine_at, :])] + list(zip(early[1:], held)))
+    moves.start(*range(7))
 
     def fetch(head):
         at = pl.ds(pl.multiple_of(lax.rem(head, 2) * length, length), length)
@@ -577,21 +632,23 @@
 
     fetch(0).start()
     fetch(1).start()
+    moves.start(*range(7, EARLY))
     far = pltpu.make_async_remote_copy(
         src_ref=cross_ref, dst_ref=far_ref, send_sem=fsend, recv_sem=frecv, device_id={"mp": cross}, device_id_type=MESH
     )
     if fold:
         up = Fold(upg_ref, winn.at[0], wsend.at[0], wrecv.at[0])
         down = Fold(downg_ref, winn.at[1], wsend.at[1], wrecv.at[1])
-        mix = Fold(mix_ref, winn.at[2], wsend.at[2], wrecv.at[2])
+        mix = Fold(mix_ref, winn.at[2], wsend.at[2], wrecv.at[2], MIX_ORDER)
         tab = lambda head: Fold(band_ref.at[head], tinn.at[head], tsend.at[head], trecv.at[head])
         small = Total(acc_ref, ainn, asend, arecv)
         greet(({"mp": partner}, {"mp": cross}) + tuple({"dp": peer} for peer in up.peers))
     else:
         greet_mp()
 
-    first.wait()
+    moves.wait(0)
     loop(CHUNKS, gat.send_own)
+    moves.wait(1, 2)
     if fold:
         up.start()
         down.start()
@@ -610,66 +667,75 @@
     def flip_g(i):
         gt_ref[:, tall(i)] = g_ref[tall(i), :].T
 
+    per = rows_all // BLOCK // seqs
+    near_seq = gat.me // 2
     block(gat.me)
-    loop(CHUNKS, gat.wait_partner)
-    block(gat.partner)
-    loop(rows_all // BLOCK, flip_q)
     dkt_ref[...] = jnp.zeros_like(dkt_ref)
     dvt_ref[...] = jnp.zeros_like(dvt_ref)
     dq_ref[...] = jnp.zeros_like(dq_ref)
     small_ref[...] = jnp.zeros_like(small_ref)
     if fold:
         tab_ref[...] = jnp.zeros_like(tab_ref)
-    loop(CHUNKS, gat.relay)
-    block(gat.cross)
-    loop(CHUNKS, gat.wait_diag)
-    block(gat.diag)
-    far.start()
-    loop(rows_all // BLOCK, flip_g)
-    if fold:
-        up.advance(0)
+    moves.wait(3, 4, 5, 6)
+    loop(rows_all // BLOCK, flip_q)
+    loop(CHUNKS, gat.wait_partner)
+    block(gat.partner)
+    loop(per, lambda i: flip_g(near_seq * per + i))
     lane = lax.broadcasted_iota(jnp.int32, (1, 128), 1)
 
-    def step(head, index):
+    def step(head, index, seq, first):
         start, width = window(index, length)
         mine = head_lanes(head, cols)
         feats = pl.ds(pl.multiple_of(head * HEAD_DIM, HEAD_DIM), HEAD_DIM)
+        rows = tall(seq * blocks + index)
+        keys_at = pl.ds(pl.multiple_of(seq * length + start, 128), width)
+        keys = k_ref[keys_at, :]
+        same = cols_ref[rows, 0:1] == ids_ref[pl.ds(seq, 1), pl.ds(start, width)]
+        sums = jnp.sum(jnp.where(lane == head, lse_ref[rows, :], 0.0), axis=-1, keepdims=True)
         bias = table_ref[tall(lax.rem(head, 2) * blocks + index), pl.ds(start, width)].astype(F32)
-        for seq in range(seqs):
-            base = seq * length
-            rows = pl.ds(pl.multiple_of(base + index * BLOCK, BLOCK), BLOCK)
-            keys_at = pl.ds(pl.multiple_of(base + start, 128), width)
-            keys = k_ref[keys_at, :]
-            same = cols_ref[rows, 0:1] == ids_ref[seq : seq + 1, pl.ds(start, width)]
-            sums = jnp.sum(jnp.where(lane == head, lse_ref[rows, :], 0.0), axis=-1, keepdims=True)
-            scores = dot_nt(jnp.where(mine, q_ref[rows, :], 0), keys) + bias
-            probs = jnp.where(same, jnp.exp(scores - sums), 0.0)
-            grad_probs = dot_nt(jnp.where(mine, g_ref[rows, :], 0), v_ref[keys_at, :])
-            centre = jnp.sum(grad_probs * probs, axis=-1, keepdims=True)
-            grad_scores = (probs * (grad_probs - centre)).astype(BF)
-            dvt_ref[feats, keys_at] += dot(gt_ref[feats, rows], probs.astype(BF))
-            dkt_ref[feats, keys_at] += dot(qt_ref[feats, rows], grad_scores)
-            grad_q = (dot(grad_scores, keys) * 0.125).astype(BF)
-            dq_ref[rows, :] = jnp.where(mine, grad_q, dq_ref[rows, :])
-            if seq == 0:
-                total_ref[:, 0:width] = grad_scores.astype(F32)
-            else:
-                total_ref[:, 0:width] += grad_scores.astype(F32)
+        scores = dot_nt(jnp.where(mine, q_ref[rows, :], 0), keys) + bias
+        probs = jnp.where(same, jnp.exp(scores - sums), 0.0)
+        grad_probs = dot_nt(jnp.where(mine, g_ref[rows, :], 0), v_ref[keys_at, :])
+        centre = jnp.sum(grad_probs * probs, axis=-1, keepdims=True)
+        grad_scores = (probs * (grad_probs - centre)).astype(BF)
+        strip_ref[:, 0:width] = grad_scores
+        dvt_ref[feats, keys_at] += dot(gt_ref[feats, rows], probs.astype(BF))
+        dkt_ref[feats, keys_at] += dot(qt_ref[feats, rows], grad_scores)
+        grad_q = (dot(grad_scores, keys) * 0.125).astype(BF)
+        dq_ref[rows, :] = jnp.where(mine, grad_q, dq_ref[rows, :])
         for part in range(BLOCK // GROUP):
             group = index * (BLOCK // GROUP) + part
-            first, wide = band_window(group, length)
-            offset = pl.multiple_of(first - start, 128)
-            value = total_ref[part * GROUP : (part + 1) * GROUP, pl.ds(offset, wide)]
-            band_ref[head, slot_of(group), :, :] = value.astype(BF)
-
-    def one_head(head):
+            begin, wide = band_window(group, length)
+            offset = pl.multiple_of(begin - start, 128)
+            value = strip_ref[part * GROUP : (part + 1) * GROUP, pl.ds(offset, wide)]
+            slot = slot_of(group)
+            if not first:
+                value = (value.astype(F32) + band_ref[head, slot, :, :].astype(F32)).astype(BF)
+            band_ref[head, slot, :, :] = value
+
+    def one_head(head, seq, first):
         fetch(head).wait()
-        loop(blocks, lambda index: step(head, index))
+
+        def inner(index):
+            step(head, index, seq, first)
+            if first:
+                i = head * blocks + index
+
+                @pl.when(lax.rem(i, heads) == heads - 1)
+                def _():
+                    gat.relay(i // heads)
+
+        loop(blocks, inner)
 
         @pl.when(head + 2 < heads)
         def _():
             fetch(head + 2).start()
 
+    def near_head(head):
+        one_head(head, near_seq, True)
+
+    def far_head(head):
+        one_head(head, 1 - near_seq, False)
         if fold:
             tab(head).start()
 
@@ -686,7 +752,19 @@
             def _():
                 tab(0).advance(0)
 
-    loop(heads, one_head)
+    loop(heads, near_head)
+    fetch(0).start()
+    fetch(1).start()
+    block(gat.cross)
+    loop(CHUNKS, gat.wait_diag)
+    block(gat.diag)
+    moves.wait(7)
+    far.start()
+    loop(per, lambda i: flip_g((1 - near_seq) * per + i))
+    if fold:
+        up.advance(0)
+    loop(heads, far_head)
+    moves.wait(*range(8, EARLY))
     rows_ref = table_ref.at[:, 0 : rowsg_ref.shape[1]]
     again = pltpu.make_async_copy(rows_hbm, rows_ref, load.at[0])
     again.start()
@@ -699,11 +777,13 @@
 
     again.wait()
 
+    order = MIX_ORDER if fold else (0, 1, 2)
+
     def weights(i):
         rows = table_ref[:, half_of(rowsg_ref, i)]
         for number, ref in enumerate((dq_ref, dk_ref, dv_ref)):
-            pack(mix_ref, i, dot_tn(rows, ref[...]), number * cols)
-        pack(mix_ref, i, dot_tn(rowsg_ref[:, half_of(rowsg_ref, i)], ctx_ref[...]), 3 * cols)
+            pack(mix_ref, i, dot_tn(rows, ref[...]), number * cols, order)
+        pack(mix_ref, i, dot_tn(rowsg_ref[:, half_of(rowsg_ref, i)], ctx_ref[...]), 3 * cols, order)
 
     loop(2, weights)
 
@@ -723,7 +803,7 @@
 
     def share(number, chunk):
         at = gat.rows(number, chunk)
-        return dot_nt(dq_ref[at, :], w_ref[0]) + dot_nt(dk_ref[at, :], w_ref[1]) + dot_nt(dv_ref[at, :], w_ref[2])
+        return dot(dq_ref[at, :], w_ref[0]) + dot(dk_ref[at, :], w_ref[1]) + dot(dv_ref[at, :], w_ref[2])
 
     loop(CHUNKS, lambda c: net.put(0, c, share(net.diag, c)))
     loop(CHUNKS, lambda c: net.put(1, c, share(net.cross, c) + net.take(0, c)))
@@ -742,16 +822,16 @@
 
     def layer(chunk):
         at = net.rows(chunk)
-        mlp_out = here_ref[at, :] + far_ref[at, :].astype(F32) + dbias_ref[...].astype(F32)
-        layer_ref[at, :] = (mid_ref[at, :] + mscale_ref[...] * mlp_out).astype(BF)
+        mlp_out = here_ref[at, :] + far_ref[at, :].astype(F32) + row(par_ref, DOWN_BIAS)
+        layer_ref[at, :] = (mid_ref[at, :] + row(par_ref, MLP_SCALE) * mlp_out).astype(BF)
         top = cot_ref[at, :].astype(F32)
         small_ref[7:8, :] += jnp.sum(top * mlp_out, axis=0, keepdims=True)
-        low = (top * mscale_ref[...]).astype(BF).astype(F32)
+        low = (top * row(par_ref, MLP_SCALE)).astype(BF).astype(F32)
         small_ref[6:7, :] += jnp.sum(low, axis=0, keepdims=True)
 
     loop(CHUNKS, layer)
-    for row, source in ((2, 4), (3, 3), (4, 1), (5, 2), (8, 0)):
-        small_ref[row : row + 1, :] = two_ref[source : source + 1, :]
+    for put, source in ((2, 4), (3, 3), (4, 1), (5, 2), (8, 0)):
+        small_ref[put : put + 1, :] = two_ref[source : source + 1, :]
     small_ref[9:10, 0:cols] = jnp.sum(dq_ref[...].astype(F32), axis=0, keepdims=True)
     small_ref[10:11, 0:cols] = jnp.sum(dv_ref[...].astype(F32), axis=0, keepdims=True)
     if fold:
@@ -763,7 +843,7 @@
         at = net.rows(chunk)
         grad = own_ref[at, :] + net.take(1, chunk)
         normed, inv = norm_rows(x_ref[at, :].astype(F32), 1.0, 0.0)[1:]
-        back, gain_sum, shift_sum = norm_back(grad, normed, inv, gain_ref[...])
+        back, gain_sum, shift_sum = norm_back(grad, normed, inv, row(par_ref, ATTN_GAIN))
         grad_ref[at, :] = gmid_ref[at, :] + back
         small_ref[0:1, :] += gain_sum[None]
         small_ref[1:2, :] += shift_sum[None]
@@ -795,9 +875,9 @@
     loop(CHUNKS, net.drain)
 
 
-def back(fold, length, gattn, rows_one, table, proj, ctx, q, k, v, lse, ids, qkv, patches, gmid, gain, *rest):
-    rows, width = patches.shape
-    cols = q.shape[1]
+def back(fold, length, proj, ids, params, two, rows_one, table, *early):
+    rows, width = early[0].shape
+    cols = proj.shape[0]
     heads = cols // HEAD_DIM
     piece, wide = width // SLOTS, band_window(0, length)[1]
     strip = min(length, BLOCK + 2 * PAGE_MOST)
@@ -815,15 +895,14 @@
     outs += [((16, width), F32)]
     one, flat = pltpu.VMEM((4 * rows, cols), BF), pltpu.VMEM((cols, 4 * rows), BF)
     total = pltpu.VMEM((cols, 4 * rows), F32)
-    scratch += [
+    scratch += like(*early[1:]) + [
         pltpu.VMEM((2 * length, length), BF), pltpu.VMEM((4 * rows, 128), F32), pltpu.VMEM((4 * rows, width), BF), one,
-        flat, flat, total, total, pltpu.VMEM((BLOCK, strip), F32), one, one,
-        pltpu.VMEM((rows, width), BF),
-        pltpu.SemaphoreType.DMA((1 + heads,)), pltpu.SemaphoreType.DMA, pltpu.SemaphoreType.DMA,
+        flat, flat, total, total, pltpu.VMEM((BLOCK, strip), BF), one, one, pltpu.VMEM((rows, width), BF),
+        pltpu.SemaphoreType.DMA((1 + heads,)), pltpu.SemaphoreType.DMA((EARLY,)),
+        pltpu.SemaphoreType.DMA, pltpu.SemaphoreType.DMA,
     ] + moves() + halves(rows, width)
     return call(
-        partial(back_kernel, fold), "back", 4, outs, scratch,
-        proj, ctx, q, k, v, lse, ids, qkv, patches, gmid, gain, *rest, gattn, rows_one, table, far=3,
+        partial(back_kernel, fold), "back", 4, outs, scratch, proj, ids, params, two, rows_one, table, *early, far=2 + EARLY
     )
 
 
@@ -855,17 +934,20 @@
     places = jnp.arange(length, dtype=jnp.int32)[None]
     ids = jnp.where(places < fill_counts[:, None], segment_ids, -1 - places).astype(F32)
     fold = n_dp == SLOTS and length == SLOTS * GROUP
-    rows_one, grad_rows, queries, keys, values, context, lse = front(
-        patches, attn_gain, attn_shift, qkv_weight, qv_bias, cotangent, mlp_scale, ids, rel_table
-    )
-    attn_out, middle, normed_two = project(context, proj_weight, proj_bias, patches, attn_scale, mlp_gain, mlp_shift)
-    grad_middle, grad_attn, cross, here, up_local, down_local, sums_two = mlp(
-        normed_two, grad_rows, up_weight, up_bias, down_weight, middle, attn_out, cotangent, mlp_gain, attn_scale
+    vectors = (attn_gain, attn_shift, proj_bias, attn_scale, mlp_gain, mlp_shift, up_bias, down_bias, mlp_scale)
+    params = jnp.concatenate([v.astype(F32) for v in vectors]).reshape(len(vectors), -1)
+    turned = qkv_weight.swapaxes(1, 2)
+    context, lse, rows_one, grad_rows, queries, keys, values = front(
+        patches, params, turned, qv_bias, cotangent, ids, rel_table
+    )
+    attn_out, middle, normed_two = project(context, proj_weight, patches, params)
+    grad_middle, grad_attn, sums_two, cross, here, up_local, down_local = mlp(
+        normed_two, params, up_weight, down_weight, grad_rows, middle, attn_out, cotangent
     )
     layer_out, patch_grad, *more, sums = back(
-        fold, length, grad_attn, rows_one, rel_table, proj_weight, context, queries, keys, values, lse, ids, qkv_weight,
-        patches, grad_middle, attn_gain[None], cotangent, middle, cross, here, down_bias[None], mlp_scale[None],
-        up_local, down_local, sums_two,
+        fold, length, proj_weight, ids, params, sums_two, rows_one, rel_table,
+        grad_attn, up_local, down_local, queries, keys, values, lse, cross, context, turned, here, middle, cotangent,
+        patches, grad_middle,
     )
     if fold:
         table_grad, up_grad, down_grad, mixed = more

time: 252 us -> 247 us (0.980)
  Pallas kernels: 232 us -> 225 us
  other arithmetic: 0.68 us -> 3.44 us
    pallas_call x4, Pallas kernels: 232 us -> 225 us  [call(): pl.pallas_call(kernel, out_shape=tuple((jax.ShapeDtypeStruct(shape, dtype...]
    broadcast_in_dim x9 -> x0, local copies, waits for them, and re-layouts: 5.23 us -> none  [the longest x1 0.58 us: local(): down_bias[None]]
    unnamed x42 -> x22, local copies, waits for them, and re-layouts: 9.46 us -> 10.5 us
where the time goes in v4:
time: 247 us; the launch traced here: 246 us
  Pallas kernels  225 us (91%)
  local copies, waits for them, and re-layouts  17 us (7%)
  other arithmetic  3.44 us (1%)
    pallas_call x4, Pallas kernels, call(): pl.pallas_call(kernel, out_shape=tuple((jax.ShapeDtypeStruct(shape, dtype...  225 us
    unnamed x22, local copies, waits for them, and re-layouts  10.5 us

profile of v4, /device:TPU:0, one launch (start us, length us, event | category | flops | bytes accessed | tf_op | source)
XLA Modules:
  0.0 246.4 jit_solution(3618619230917230727)
XLA Ops:
  0.7 1.4 fusion.ids_ref
  2.0 0.7 constant_dynamic-update-slice_fusion.8
  2.7 0.7 constant_dynamic-update-slice_fusion.7
  3.4 0.7 constant_dynamic-update-slice_fusion.6
  4.1 0.7 constant_dynamic-update-slice_fusion.5
  4.8 0.7 constant_dynamic-update-slice_fusion.4
  5.5 0.7 constant_dynamic-update-slice_fusion.3
  6.2 0.7 constant_dynamic-update-slice_fusion.2
  6.9 0.7 constant_dynamic-update-slice_fusion.1
  7.6 0.7 constant_dynamic-update-slice_fusion
  8.3 0.6 reshape.46.par_ref
  8.9 44.3 %front.1 = (bf16[2048,192]{1,0:T(8,128)(2,1)}, f32[2048,128]{1,0:T(8,128)}, bf16[2048,768]{1,0:T(8,128)(2,1)}, bf16[2048,768]{1,0:T(8,128)(2,1)}, bf16[2048,192]...) custom-call(bf16[512,768]{1,0:T(8,128)(2,1)} %refs_13_.1, f32[9,768]{1,0:T(8,128)} %reshape.46.par_ref, ...), custom_call_target="tpu_custom_call" | custom-call | tf_op jit(solution)/shard_map/front/pallas_call | solution.py:218
  53.2 25.6 %project.1 = (f32[512,768]{1,0:T(8,128)}, f32[512,768]{1,0:T(8,128)}, bf16[512,768]{1,0:T(8,128)(2,1)}) custom-call(bf16[2048,192]{1,0:T(8,128)(2,1)} %get-tuple-element.41.ctx_ref.refs_8_, bf16[192,768]{1,0:T(8,128)(2,1)} %pw_ref.1, bf16[512,768]{1,0:T(8,128)(2,1)} %refs_13_.1, f32[9,768]{1,0:T(8,128)} %reshape.46.par_ref), custom_call_target="tpu_custom_call" | custom-call | tf_op jit(solution)/shard_map/project/pallas_call | solution.py:218
  78.8 39.9 %mlp.1 = (f32[512,768]{1,0:T(8,128)}, bf16[512,768]{1,0:T(8,128)(2,1)}, f32[8,768]{1,0:T(8,128)}, bf16[512,768]{1,0:T(8,128)(2,1)}, f32[512,768]{1,0:T(8,128)}, ...) custom-call(bf16[512,768]{1,0:T(8,128)(2,1)} %get-tuple-element.42.norm_ref, f32[9,768]{1,0:T(8,128)} %reshape.46.par_ref, ...), custom_call_target="tpu_custom_call" | custom-call | tf_op jit(solution)/shard_map/mlp/pallas_call | solution.py:218
  118.7 115.4 %back.1 = (bf16[512,768]{1,0:T(8,128)(2,1)}, f32[512,768]{1,0:T(8,128)}, f32[3,128,1024]{2,1,0:T(8,128)}, f32[96,768]{1,0:T(8,128)}, f32[96,768]{1,0:T(8,128)}, /*index=5*/f32[96,768]{1,0:T(8,128)}, f32[16,768]{1,0:T(8,128)}) custom-call(bf16[192,768]{1,0:T(8,128)(2,1)} %pw_ref.1, f32[2,1024]{1,0:T(2,128)} %fusion.ids_ref, f32[9,768]{1,0:T(8,128)} %reshape.46.par_ref, ...), custom_call_target="tpu_custom_call" | custom-call | tf_op jit(solution)/shard_map/back/pallas_call | solution.py:218
  234.1 0.0 copy-start.2
  234.1 1.3 slice.39
  235.5 1.7 slice_reduce_fusion
  237.2 1.0 slice_bitcast_fusion
  238.2 1.0 slice.38
  239.1 0.0 copy-start.1
  239.1 0.7 copy.40
  239.9 0.1 copy.38
  240.0 0.9 copy.39
  240.9 0.0 copy-done.2
  240.9 0.9 copy.55
  241.8 0.0 copy-done.1
  241.8 0.0 copy-start
  241.8 1.1 copy.56
  242.9 0.8 copy-done
  243.8 0.0 copy-start.4
  243.8 0.0 copy-start.3
  243.8 1.1 copy.57
  244.9 0.0 copy-done.4
  244.9 0.7 copy.58
  245.6 0.0 copy-done.3
  245.6 0.7 copy.59
  (2 shorter events, 0.0 us)
Async XLA Ops:
  234.1 6.8 %copy-start.2 = (bf16[512,768]{1,0:T(8,128)(2,1)S(1)}, bf16[512,768]{1,0:T(8,128)(2,1)}, u32[]{:S(2)}) copy-start(bf16[512,768]{1,0:T(8,128)(2,1)} %get-tuple-element.125) | copy-start | bytes 2359300
  239.1 2.7 %copy-start.1 = (f32[512,768]{1,0:T(8,128)S(1)}, f32[512,768]{1,0:T(8,128)}, u32[]{:S(2)}) copy-start(f32[512,768]{1,0:T(8,128)} %get-tuple-element.126) | copy-start | bytes 4718596
  241.8 2.0 copy-start
  243.8 1.1 copy-start.4
  243.8 1.9 copy-start.3

commit v5 on v4

--- a/solution.py
+++ b/solution.py
@@ -10,13 +10,15 @@
 HEAD_DIM = 64
 BLOCK = 256
 GROUP = 128
+
 ATTN_GAIN, ATTN_SHIFT, PROJ_BIAS, ATTN_SCALE, MLP_GAIN, MLP_SHIFT, UP_BIAS, DOWN_BIAS, MLP_SCALE = range(9)
 CHUNKS = 4
 SLOTS = 8
 PARTS = 2
 EARLY = 15
-MIX_ORDER = (1, 2, 0)
+MIX_ORDER = (0, 1, 2)
 PAGE_MOST = 256
+TILES = 2 * PAGE_MOST // GROUP
 BF = jnp.bfloat16
 F32 = jnp.float32
 MESH = pl.DeviceIdType.MESH
@@ -64,10 +66,10 @@
     return pl.multiple_of(start, 128), width
 
 
-def band_window(group, length):
-    wide = min(length, GROUP + 2 * PAGE_MOST)
-    start = jnp.clip(group * GROUP - PAGE_MOST, 0, length - wide)
-    return pl.multiple_of(start, 128), wide
+def edge(first_row, rows):
+    place = lax.broadcasted_iota(jnp.int32, (rows, GROUP), 0) + first_row
+    column = lax.broadcasted_iota(jnp.int32, (rows, GROUP), 1)
+    return column > place, column < place
 
 
 def head_lanes(head, cols):
@@ -205,8 +207,12 @@
             self.copies[i].wait()
 
 
-def row(ref, number):
-    return ref[number : number + 1, :]
+def row(vectors, number):
+    return vectors[number][...].astype(F32).reshape(1, -1)
+
+
+def some(vectors, *numbers):
+    return {number: vectors[number] for number in numbers}
 
 
 def like(*arrays):
@@ -218,7 +224,7 @@
     return pl.pallas_call(
         kernel,
         out_shape=tuple(jax.ShapeDtypeStruct(shape, dtype) for shape, dtype in outs),
-        in_specs=[vmem()] * (len(args) - far) + [anywhere] * far,
+        in_specs=[jax.tree.map(lambda _: vmem(), arg) for arg in args[: len(args) - far]] + [anywhere] * far,
         out_specs=tuple([vmem()] * (len(outs) - far_out) + [anywhere] * far_out),
         scratch_shapes=scratch,
         compiler_params=pltpu.CompilerParams(
@@ -341,7 +347,7 @@
         [pltpu.VMEM(table.shape, BF), pltpu.VMEM((4 * rows, 128), F32)]
         + [pltpu.VMEM(*shape) for shape in (wide, wide, one, one, one)]
         + [pltpu.SemaphoreType.DMA((6,))] + moves() + moves(),
-        patches, params, weight, bias, cotangent, ids, table, far=1, far_out=5,
+        patches, some(params, ATTN_GAIN, ATTN_SHIFT, MLP_SCALE), weight, bias, cotangent, ids, table, far=1, far_out=5,
     )
 
 
@@ -380,7 +386,7 @@
     rows, width = patches.shape
     return call(
         project_kernel, "project", 2, [((rows, width), F32), ((rows, width), F32), ((rows, width), BF)],
-        halves(rows, width), context, weight, patches, params,
+        halves(rows, width), context, weight, patches, some(params, PROJ_BIAS, ATTN_SCALE, MLP_GAIN, MLP_SHIFT),
     )
 
 
@@ -513,7 +519,7 @@
         + [pltpu.SemaphoreType.DMA((10,))]
         + [pltpu.VMEM((4 * rows, width), BF), pltpu.VMEM((4 * rows, ff), BF), pltpu.VMEM((4 * rows, ff), BF), one, one, one]
         + moves() + halves(rows, width) + halves(rows, width),
-        normed, params, up, down, grad_rows, middle, attn, cotangent, far=6, far_out=4,
+        normed, some(params, UP_BIAS, MLP_GAIN, ATTN_SCALE), up, down, grad_rows, middle, attn, cotangent, far=6, far_out=4,
     )
 
 
@@ -572,7 +578,7 @@
         x, lo, hi = lax.rem(place, 2), lax.rem(place // 2, 2), place // 4
         _, partner, cross, _ = neighbours()
         self.peers = (
-            {"dp": place + 1 - 2 * x}, {"dp": place + 2 - 4 * lo}, {"dp": place + 4 - 8 * hi}, {"mp": partner}, {"mp": cross},
+            {"mp": partner}, {"mp": cross}, {"dp": place + 1 - 2 * x}, {"dp": place + 2 - 4 * lo}, {"dp": place + 4 - 8 * hi},
         )
 
     def copy(self, stage):
@@ -587,6 +593,8 @@
     def finish(self, stage):
         self.copy(stage).wait_recv()
         self.acc[stage + 1] = self.acc[stage] + self.inn[stage]
+        if stage == 1:
+            self.acc[2, 8:16, :] = self.acc[0, 8:16, :]
 
     def drain(self):
         for stage in range(5):
@@ -705,9 +713,15 @@
         dq_ref[rows, :] = jnp.where(mine, grad_q, dq_ref[rows, :])
         for part in range(BLOCK // GROUP):
             group = index * (BLOCK // GROUP) + part
-            begin, wide = band_window(group, length)
-            offset = pl.multiple_of(begin - start, 128)
-            value = strip_ref[part * GROUP : (part + 1) * GROUP, pl.ds(offset, wide)]
+            tiles = []
+            for t in range(TILES + 1):
+                block = group - TILES // 2 + t
+                there = (block >= 0) & (block < length // GROUP)
+                offset = jnp.clip(block * GROUP - start, 0, width - GROUP)
+                tile = strip_ref[part * GROUP : (part + 1) * GROUP, pl.ds(pl.multiple_of(offset, GROUP), GROUP)]
+                tiles.append(jnp.where(there, tile, 0))
+            tiles[0] += tiles.pop()
+            value = jnp.concatenate(tiles, axis=1)
             slot = slot_of(group)
             if not first:
                 value = (value.astype(F32) + band_ref[head, slot, :, :].astype(F32)).astype(BF)
@@ -747,10 +761,6 @@
             @pl.when(head == 1)
             def _():
                 down.advance(1)
-
-            @pl.when(head == 2)
-            def _():
-                tab(0).advance(0)
 
     loop(heads, near_head)
     fetch(0).start()
@@ -789,8 +799,17 @@
 
     def put_table(head):
         def put(rows, value):
-            first = band_window(lax.axis_index("dp"), length)[0]
-            tab_ref[head, rows, pl.ds(first, value.shape[1])] = value
+            group = lax.axis_index("dp")
+            left, right = edge(rows.start, rows.size)
+            for t in range(TILES + 1):
+                tile = value[:, t % TILES * GROUP : (t % TILES + 1) * GROUP]
+                if t % TILES == 0:
+                    tile = jnp.where(right if t else left, tile, 0.0)
+                block = group - TILES // 2 + t
+
+                @pl.when((block >= 0) & (block < length // GROUP))
+                def _():
+                    tab_ref[head, rows, pl.ds(pl.multiple_of(block * GROUP, GROUP), GROUP)] = tile
         return put
 
     def put_to(ref):
@@ -807,17 +826,16 @@
 
     loop(CHUNKS, lambda c: net.put(0, c, share(net.diag, c)))
     loop(CHUNKS, lambda c: net.put(1, c, share(net.cross, c) + net.take(0, c)))
+    loop(CHUNKS, lambda c: net.put(2, c, share(net.partner, c)))
+
+    def keep(chunk):
+        own_ref[net.rows(chunk), :] = share(net.me, chunk) + net.take(2, chunk)
+
+    loop(CHUNKS, keep)
     if fold:
+        tab(0).advance(0)
         up.finish(put_to(upo_ref))
         down.finish(put_to(downo_ref))
-        tab(0).advance(1)
-        tab(1).advance(0)
-    loop(CHUNKS, lambda c: net.put(2, c, share(net.partner, c)))
-
-    def keep(chunk):
-        own_ref[net.rows(chunk), :] = share(net.me, chunk) + net.take(2, chunk)
-
-    loop(CHUNKS, keep)
     far.wait_recv()
 
     def layer(chunk):
@@ -835,9 +853,8 @@
     small_ref[9:10, 0:cols] = jnp.sum(dq_ref[...].astype(F32), axis=0, keepdims=True)
     small_ref[10:11, 0:cols] = jnp.sum(dv_ref[...].astype(F32), axis=0, keepdims=True)
     if fold:
-        tab(2).advance(0)
-        tab(1).advance(1)
-        tab(0).finish(put_table(0))
+        tab(0).advance(1)
+        tab(1).advance(0)
 
     def last(chunk):
         at = net.rows(chunk)
@@ -851,23 +868,25 @@
     loop(CHUNKS, last)
     if fold:
         small.start(0)
-        mix.advance(0)
+        tab(0).finish(put_table(0))
+        tab(1).advance(1)
         small.finish(0)
         small.start(1)
-        tab(2).advance(1)
-        tab(1).finish(put_table(1))
+        tab(2).advance(0)
         small.finish(1)
         small.start(2)
-        mix.advance(1)
+        tab(1).finish(put_table(1))
         small.finish(2)
         small.start(3)
-        tab(2).finish(put_table(2))
+        tab(2).advance(1)
+        mix.advance(0)
         small.finish(3)
         small.start(4)
+        mix.advance(1)
         mix.finish(put_to(mixo_ref))
+        tab(2).finish(put_table(2))
         small.finish(4)
-        sums_ref[0:8, :] = acc_ref[5, 0:8, :]
-        sums_ref[8:16, :] = acc_ref[3, 8:16, :]
+        sums_ref[...] = acc_ref[5]
         for piece in (up, down, mix, tab(0), tab(1), tab(2), small):
             piece.drain()
     far.wait_send()
@@ -879,7 +898,7 @@
     rows, width = early[0].shape
     cols = proj.shape[0]
     heads = cols // HEAD_DIM
-    piece, wide = width // SLOTS, band_window(0, length)[1]
+    piece, wide = width // SLOTS, TILES * GROUP
     strip = min(length, BLOCK + 2 * PAGE_MOST)
     band, mix = ((heads, SLOTS, GROUP, wide), BF), ((SLOTS, piece, width), BF)
     outs = [((rows, width), BF), ((rows, width), F32)]
@@ -901,6 +920,7 @@
         pltpu.SemaphoreType.DMA((1 + heads,)), pltpu.SemaphoreType.DMA((EARLY,)),
         pltpu.SemaphoreType.DMA, pltpu.SemaphoreType.DMA,
     ] + moves() + halves(rows, width)
+    params = some(params, DOWN_BIAS, MLP_SCALE, ATTN_GAIN)
     return call(
         partial(back_kernel, fold), "back", 4, outs, scratch, proj, ids, params, two, rows_one, table, *early, far=2 + EARLY
     )
@@ -920,8 +940,18 @@
     shard = length // n_dp
     send = band.reshape(groups, heads, GROUP // shard, shard, wide).swapaxes(1, 2)
     part = scatter_dp(send.reshape(n_dp * heads * shard, wide)).reshape(heads, shard, wide)
-    first = band_window(lax.axis_index("dp") * shard // GROUP, length)[0]
-    return lax.dynamic_update_slice(jnp.zeros((heads, shard, length), F32), part, (0, 0, first))
+    place = lax.axis_index("dp") * shard
+    return unfold(part, place // GROUP, place % GROUP, length)
+
+
+def unfold(part, group, first_row, length):
+    heads, shard, _ = part.shape
+    left, right = edge(first_row, shard)
+    end = part[:, :, :GROUP]
+    band = jnp.concatenate([jnp.where(left, end, 0.0), part[:, :, GROUP:], jnp.where(right, end, 0.0)], axis=2)
+    full = jnp.zeros((heads, shard, length + 2 * PAGE_MOST), F32)
+    full = lax.dynamic_update_slice(full, band, (0, 0, group * GROUP))
+    return full[:, :, PAGE_MOST : PAGE_MOST + length]
 
 
 def local(
@@ -935,7 +965,7 @@
     ids = jnp.where(places < fill_counts[:, None], segment_ids, -1 - places).astype(F32)
     fold = n_dp == SLOTS and length == SLOTS * GROUP
     vectors = (attn_gain, attn_shift, proj_bias, attn_scale, mlp_gain, mlp_shift, up_bias, down_bias, mlp_scale)
-    params = jnp.concatenate([v.astype(F32) for v in vectors]).reshape(len(vectors), -1)
+    params = dict(enumerate(vectors))
     turned = qkv_weight.swapaxes(1, 2)
     context, lse, rows_one, grad_rows, queries, keys, values = front(
         patches, params, turned, qv_bias, cotangent, ids, rel_table

time: 247 us -> 230 us (0.931)
  Pallas kernels: 225 us -> 215 us
  local copies, waits for them, and re-layouts: 17 us -> 12.2 us
    pallas_call x4, Pallas kernels: 225 us -> 215 us  [call(): pl.pallas_call(kernel, out_shape=tuple((jax.ShapeDtypeStruct(shape, dtype...]
    unnamed x22 -> x17, local copies, waits for them, and re-layouts: 10.5 us -> 7.06 us
where the time goes in v5:
time: 230 us; the launch traced here: 229 us
  Pallas kernels  215 us (93%)
  local copies, waits for them, and re-layouts  12.2 us (5%)
    pallas_call x4, Pallas kernels, call(): pl.pallas_call(kernel, out_shape=tuple((jax.ShapeDtypeStruct(shape, dtype...  215 us
    unnamed x17, local copies, waits for them, and re-layouts  7.06 us

profile of v5, /device:TPU:0, one launch (start us, length us, event | category | flops | bytes accessed | tf_op | source)
XLA Modules:
  0.0 229.0 jit_solution(4305622301190343958)
XLA Ops:
  0.7 1.4 fusion.ids_ref
  2.0 44.3 %front.1 = (bf16[2048,192]{1,0:T(8,128)(2,1)}, f32[2048,128]{1,0:T(8,128)}, bf16[2048,768]{1,0:T(8,128)(2,1)}, bf16[2048,768]{1,0:T(8,128)(2,1)}, bf16[2048,192]...) custom-call(bf16[512,768]{1,0:T(8,128)(2,1)} %refs_13_.1, f32[768]{0:T(1024)} %par_ref_0_.3, ...), custom_call_target="tpu_custom_call" | custom-call | tf_op jit(solution)/shard_map/front/pallas_call | solution.py:224
  46.4 25.6 %project.1 = (f32[512,768]{1,0:T(8,128)}, f32[512,768]{1,0:T(8,128)}, bf16[512,768]{1,0:T(8,128)(2,1)}) custom-call(bf16[2048,192]{1,0:T(8,128)(2,1)} %get-tuple-element.41.ctx_ref.refs_8_, bf16[192,768]{1,0:T(8,128)(2,1)} %pw_ref.1, bf16[512,768]{1,0:T(8,128)(2,1)} %refs_13_.1, bf16[768]{0:T(1024)(128)(2,1)} %par_ref_2_.1, f32[768]{0:T(1024)} %par_ref_3_.3, ...), custom_call_target="tpu_custom_call" | custom-call | tf_op jit(solution)/shard_map/project/pallas_call | solution.py:224
  72.0 40.0 %mlp.1 = (f32[512,768]{1,0:T(8,128)}, bf16[512,768]{1,0:T(8,128)(2,1)}, f32[8,768]{1,0:T(8,128)}, bf16[512,768]{1,0:T(8,128)(2,1)}, f32[512,768]{1,0:T(8,128)}, ...) custom-call(bf16[512,768]{1,0:T(8,128)(2,1)} %get-tuple-element.42.norm_ref, f32[768]{0:T(1024)} %par_ref_3_.3, ...), custom_call_target="tpu_custom_call" | custom-call | tf_op jit(solution)/shard_map/mlp/pallas_call | solution.py:224
  112.0 104.8 %back.1 = (bf16[512,768]{1,0:T(8,128)(2,1)}, f32[512,768]{1,0:T(8,128)}, f32[3,128,1024]{2,1,0:T(8,128)}, f32[96,768]{1,0:T(8,128)}, f32[96,768]{1,0:T(8,128)}, /*index=5*/f32[96,768]{1,0:T(8,128)}, f32[16,768]{1,0:T(8,128)}) custom-call(bf16[192,768]{1,0:T(8,128)(2,1)} %pw_ref.1, f32[2,1024]{1,0:T(2,128)} %fusion.ids_ref, f32[768]{0:T(1024)} %par_ref_0_.3, ...), custom_call_target="tpu_custom_call" | custom-call | tf_op jit(solution)/shard_map/back/pallas_call | solution.py:224
  216.8 0.0 copy-start.2
  216.8 1.3 slice.39
  218.1 1.7 slice_reduce_fusion
  219.9 1.0 slice_bitcast_fusion
  220.8 1.0 slice.38
  221.8 0.0 copy-start.1
  221.8 0.7 copy.40
  222.6 0.1 copy.38
  222.7 0.9 copy.39
  223.6 0.0 copy-done.2
  223.6 0.9 copy.46
  224.5 0.0 copy-done.1
  224.5 0.0 copy-start
  224.5 1.1 copy.47
  225.6 0.8 copy-done
  226.5 0.0 copy-start.4
  226.5 0.0 copy-start.3
  226.5 1.1 copy.48
  227.6 0.0 copy-done.4
  227.6 0.7 copy.49
  228.3 0.0 copy-done.3
  228.3 0.7 copy.50
  (1 shorter events, 0.0 us)
Async XLA Ops:
  216.8 6.8 %copy-start.2 = (bf16[512,768]{1,0:T(8,128)(2,1)S(1)}, bf16[512,768]{1,0:T(8,128)(2,1)}, u32[]{:S(2)}) copy-start(bf16[512,768]{1,0:T(8,128)(2,1)} %get-tuple-element.125) | copy-start | bytes 2359300
  221.8 2.7 %copy-start.1 = (f32[512,768]{1,0:T(8,128)S(1)}, f32[512,768]{1,0:T(8,128)}, u32[]{:S(2)}) copy-start(f32[512,768]{1,0:T(8,128)} %get-tuple-element.126) | copy-start | bytes 4718596
  224.5 2.0 copy-start
  226.5 1.1 copy-start.4
  226.5 1.9 copy-start.3

commit v6 on v5

--- a/solution.py
+++ b/solution.py
@@ -264,12 +264,14 @@
 
 
 def front_kernel(
-    x_ref, par_ref, w_ref, bias_ref, cot_ref, ids_ref, table_hbm,
-    ctx_ref, lse_ref, rows_hbm, grad_hbm, q_hbm, k_hbm, v_hbm,
+    x_ref, par_ref, w_ref, bias_ref, cot_ref, ids_ref, pw_ref, table_hbm,
+    ctx_ref, lse_ref, attn_ref, mid_ref, norm_ref, rows_hbm, grad_hbm, q_hbm, k_hbm, v_hbm,
     table_ref, cols_ref, rows_ref, grad_ref, q_ref, k_ref, v_ref, load, send, recv, gsend, grecv,
+    out, inn, ssend, srecv,
 ):
     net = Gather(rows_ref, send, recv)
     top = Gather(grad_ref, gsend, grecv)
+    red = Scatter(out, inn, ssend, srecv)
     seqs, length = ids_ref.shape
     moves = Moves(
         load,
@@ -331,62 +333,49 @@
         net.drain(i)
 
     loop(steps, far)
+
+    def share(block, chunk):
+        return dot(ctx_ref[net.rows(block, chunk), :], pw_ref[...])
+
+    loop(CHUNKS, lambda c: red.put(0, c, share(red.diag, c)))
+    loop(CHUNKS, lambda c: red.put(1, c, share(red.cross, c) + red.take(0, c)))
+    loop(CHUNKS, lambda c: red.put(2, c, share(red.partner, c)))
+
+    def keep(chunk):
+        attn_ref[red.rows(chunk), :] = share(red.me, chunk) + red.take(2, chunk) + row(par_ref, PROJ_BIAS)
+
+    loop(CHUNKS, keep)
     for wait in (top.wait_partner, top.wait_diag):
         loop(CHUNKS, wait)
     moves.start(2)
-    loop(CHUNKS, top.drain)
-    moves.wait(1, 2, 3, 4, 5)
-
-
-def front(patches, params, weight, bias, cotangent, ids, table):
-    rows, width = patches.shape
-    cols = weight.shape[1]
-    one, wide = ((4 * rows, cols), BF), ((4 * rows, width), BF)
-    return call(
-        front_kernel, "front", 1, [one, ((4 * rows, 128), F32), wide, wide, one, one, one],
-        [pltpu.VMEM(table.shape, BF), pltpu.VMEM((4 * rows, 128), F32)]
-        + [pltpu.VMEM(*shape) for shape in (wide, wide, one, one, one)]
-        + [pltpu.SemaphoreType.DMA((6,))] + moves() + moves(),
-        patches, some(params, ATTN_GAIN, ATTN_SHIFT, MLP_SCALE), weight, bias, cotangent, ids, table, far=1, far_out=5,
-    )
-
-
-def project_kernel(
-    ctx_ref, w_ref, x_ref, par_ref, attn_ref, mid_ref, norm_ref, out, inn, send, recv
-):
-    net = Scatter(out, inn, send, recv)
-    greet_mp()
-
-    def share(block, chunk):
-        at = pl.ds(pl.multiple_of((block * CHUNKS + chunk) * net.size, net.size), net.size)
-        return dot(ctx_ref[at, :], w_ref[...])
-
-    loop(CHUNKS, lambda c: net.put(0, c, share(net.diag, c)))
-    loop(CHUNKS, lambda c: net.put(1, c, share(net.cross, c) + net.take(0, c)))
-    loop(CHUNKS, lambda c: net.put(2, c, share(net.partner, c)))
-
-    def own(chunk):
-        attn_ref[net.rows(chunk), :] = share(net.me, chunk) + net.take(2, chunk) + row(par_ref, PROJ_BIAS)
-
-    loop(CHUNKS, own)
 
     def last(chunk):
-        at = net.rows(chunk)
-        attn = attn_ref[at, :] + net.take(1, chunk)
+        at = red.rows(chunk)
+        attn = attn_ref[at, :] + red.take(1, chunk)
         middle = x_ref[at, :].astype(F32) + row(par_ref, ATTN_SCALE) * attn
         attn_ref[at, :] = attn
         mid_ref[at, :] = middle
         norm_ref[at, :] = norm_rows(middle, row(par_ref, MLP_GAIN), row(par_ref, MLP_SHIFT))[0].astype(BF)
 
     loop(CHUNKS, last)
-    loop(CHUNKS, net.drain)
-
-
-def project(context, weight, patches, params):
+    loop(CHUNKS, top.drain)
+    loop(CHUNKS, red.drain)
+    moves.wait(1, 2, 3, 4, 5)
+
+
+def front(patches, params, weight, bias, cotangent, ids, proj, table):
     rows, width = patches.shape
+    cols = weight.shape[1]
+    one, wide = ((4 * rows, cols), BF), ((4 * rows, width), BF)
+    own = ((rows, width), F32)
+    params = some(params, ATTN_GAIN, ATTN_SHIFT, MLP_SCALE, PROJ_BIAS, ATTN_SCALE, MLP_GAIN, MLP_SHIFT)
     return call(
-        project_kernel, "project", 2, [((rows, width), F32), ((rows, width), F32), ((rows, width), BF)],
-        halves(rows, width), context, weight, patches, some(params, PROJ_BIAS, ATTN_SCALE, MLP_GAIN, MLP_SHIFT),
+        front_kernel, "front", 1,
+        [one, ((4 * rows, 128), F32), own, own, ((rows, width), BF), wide, wide, one, one, one],
+        [pltpu.VMEM(table.shape, BF), pltpu.VMEM((4 * rows, 128), F32)]
+        + [pltpu.VMEM(*shape) for shape in (wide, wide, one, one, one)]
+        + [pltpu.SemaphoreType.DMA((6,))] + moves() + moves() + halves(rows, width),
+        patches, params, weight, bias, cotangent, ids, proj, table, far=1, far_out=5,
     )
 
 
@@ -926,6 +915,43 @@
     )
 
 
+def finish_kernel(mix_ref, sums_ref, *refs):
+    late, refs = refs[:5], refs[5:]
+    (qkv_ref, proj_ref, qv_ref), refs = refs[:3], refs[3:]
+    vectors, refs = refs[:9], refs[9:]
+    done, held, sem, back_sem = refs[:5], refs[5:10], refs[10], refs[11]
+    inward = Moves(sem, zip(late, held))
+    outward = Moves(back_sem, zip(held, done))
+    inward.start(*range(5))
+    cols = qkv_ref.shape[2]
+    for number in range(3):
+        qkv_ref[number] = mix_ref[:, number * cols : (number + 1) * cols]
+    proj_ref[...] = mix_ref[:, 3 * cols :].T
+    qv_ref[...] = sums_ref[9:11, 0:cols]
+    for number in range(9):
+        vectors[number][...] = sums_ref[number : number + 1, :].reshape(-1)
+    for number in range(5):
+        inward.wait(number)
+        outward.start(number)
+    outward.wait(*range(5))
+
+
+def finish(mixed, sums, cols, *late):
+    piece, width = mixed.shape
+    anywhere = pl.BlockSpec(memory_space=pl.ANY)
+    shapes = [(3, piece, cols), (width - 3 * cols, piece), (2, cols)] + [(width,)] * 9
+    return pl.pallas_call(
+        finish_kernel,
+        out_shape=tuple(jax.ShapeDtypeStruct(shape, F32) for shape in shapes)
+        + tuple(jax.ShapeDtypeStruct(a.shape, a.dtype) for a in late),
+        in_specs=[vmem()] * 2 + [anywhere] * 5,
+        out_specs=tuple([vmem()] * len(shapes) + [anywhere] * 5),
+        scratch_shapes=like(*late) + [pltpu.SemaphoreType.DMA((5,)), pltpu.SemaphoreType.DMA((5,))],
+        compiler_params=pltpu.CompilerParams(vmem_limit_bytes=VMEM_MOST),
+        name="finish",
+    )(mixed, sums, *late)
+
+
 def scatter_dp(x):
     return lax.psum_scatter(x, "dp", scatter_dimension=0, tiled=True).astype(F32)
 
@@ -967,10 +993,9 @@
     vectors = (attn_gain, attn_shift, proj_bias, attn_scale, mlp_gain, mlp_shift, up_bias, down_bias, mlp_scale)
     params = dict(enumerate(vectors))
     turned = qkv_weight.swapaxes(1, 2)
-    context, lse, rows_one, grad_rows, queries, keys, values = front(
-        patches, params, turned, qv_bias, cotangent, ids, rel_table
-    )
-    attn_out, middle, normed_two = project(context, proj_weight, patches, params)
+    context, lse, attn_out, middle, normed_two, rows_one, grad_rows, queries, keys, values = front(
+        patches, params, turned, qv_bias, cotangent, ids, proj_weight, rel_table
+    )
     grad_middle, grad_attn, sums_two, cross, here, up_local, down_local = mlp(
         normed_two, params, up_weight, down_weight, grad_rows, middle, attn_out, cotangent
     )
@@ -981,16 +1006,20 @@
     )
     if fold:
         table_grad, up_grad, down_grad, mixed = more
+        qkv_grad, proj_grad, qv_grad, *vectors, layer_out, patch_grad, table_grad, up_grad, down_grad = finish(
+            mixed, sums, cols, layer_out, patch_grad, table_grad, up_grad, down_grad
+        )
     else:
         band, mixed = more
         order = [4 * (d % 2) + 2 * (d // 2 % 2) + d // 4 for d in range(SLOTS)]
         table_grad = reduce_table(jnp.stack([band[:, slot] for slot in order]), length, n_dp)
         up_grad, down_grad, mixed = [scatter_dp(in_order(piece)) for piece in (up_local, down_local, mixed)]
         sums = jnp.concatenate([lax.psum(sums[:8], ("dp", "mp")), lax.psum(sums[8:], "dp")])
-    qkv_grad = mixed[:, : 3 * cols].reshape(-1, 3, cols).swapaxes(0, 1)
+        qkv_grad = mixed[:, : 3 * cols].reshape(-1, 3, cols).swapaxes(0, 1)
+        proj_grad, qv_grad, vectors = mixed[:, 3 * cols :].T, sums[9:11, :cols], sums[:9]
     return (
-        layer_out, patch_grad, sums[0], sums[1], qkv_grad, sums[9:11, :cols], table_grad, mixed[:, 3 * cols :].T,
-        sums[2], sums[3], sums[4], sums[5], up_grad, sums[8], down_grad.T, sums[6], sums[7],
+        layer_out, patch_grad, vectors[0], vectors[1], qkv_grad, qv_grad, table_grad, proj_grad,
+        vectors[2], vectors[3], vectors[4], vectors[5], up_grad, vectors[8], down_grad.T, vectors[6], vectors[7],
     )
 
 

time: 230 us -> 217 us (0.943)
  local copies, waits for them, and re-layouts: 12.2 us -> 0 us
    unnamed x17 -> x0, local copies, waits for them, and re-layouts: 7.06 us -> none
    pallas_call x0 -> x1, Pallas kernels: none -> 5.4 us  [finish(): pl.pallas_call(finish_kernel, out_shape=tuple((jax.ShapeDtypeStruct(shape...]
    pallas_call x4 -> x3, Pallas kernels: 215 us -> 209 us  [call(): pl.pallas_call(kernel, out_shape=tuple((jax.ShapeDtypeStruct(shape, dtype...]
    slice x4 -> x0, local copies, waits for them, and re-layouts: 4.19 us -> none  [the longest x1 1.73 us: local(): sums[7]]
where the time goes in v6:
time: 217 us
  Pallas kernels  215 us (99%)
    pallas_call x3, Pallas kernels, call(): pl.pallas_call(kernel, out_shape=tuple((jax.ShapeDtypeStruct(shape, dtype...  209 us
    pallas_call x1, Pallas kernels, finish(): pl.pallas_call(finish_kernel, out_shape=tuple((jax.ShapeDtypeStruct(shape...  5.4 us

profile of v6, /device:TPU:0, one launch (start us, length us, event | category | flops | bytes accessed | tf_op | source)
XLA Modules:
  0.0 217.0 jit_solution(17522815774973302307)
XLA Ops:
  0.7 1.4 fusion.ids_ref
  2.0 64.0 %front.1 = (bf16[2048,192]{1,0:T(8,128)(2,1)}, f32[2048,128]{1,0:T(8,128)}, f32[512,768]{1,0:T(8,128)}, f32[512,768]{1,0:T(8,128)}, bf16[512,768]{1,0:T(8,128)(2...) custom-call(bf16[512,768]{1,0:T(8,128)(2,1)} %refs_13_.1, ...), custom_call_target="tpu_custom_call" | custom-call | tf_op jit(solution)/shard_map/front/pallas_call | solution.py:224
  66.1 40.5 %mlp.1 = (f32[512,768]{1,0:T(8,128)}, bf16[512,768]{1,0:T(8,128)(2,1)}, f32[8,768]{1,0:T(8,128)}, bf16[512,768]{1,0:T(8,128)(2,1)}, f32[512,768]{1,0:T(8,128)}, ...) custom-call(bf16[512,768]{1,0:T(8,128)(2,1)} %get-tuple-element.58.norm_ref, f32[768]{0:T(1024)} %par_ref_3_.3, ...), custom_call_target="tpu_custom_call" | custom-call | tf_op jit(solution)/shard_map/mlp/pallas_call | solution.py:224
  106.5 104.9 %back.1 = (bf16[512,768]{1,0:T(8,128)(2,1)}, f32[512,768]{1,0:T(8,128)}, f32[3,128,1024]{2,1,0:T(8,128)}, f32[96,768]{1,0:T(8,128)}, f32[96,768]{1,0:T(8,128)}, /*index=5*/f32[96,768]{1,0:T(8,128)}, f32[16,768]{1,0:T(8,128)}) custom-call(bf16[192,768]{1,0:T(8,128)(2,1)} %pw_ref.3, f32[2,1024]{1,0:T(2,128)} %fusion.ids_ref, f32[768]{0:T(1024)} %par_ref_0_.3, ...), custom_call_target="tpu_custom_call" | custom-call | tf_op jit(solution)/shard_map/back/pallas_call | solution.py:224
  211.4 5.4 %finish.1 = (f32[3,96,192]{2,1,0:T(8,128)}, f32[192,96]{1,0:T(8,128)}, f32[2,192]{1,0:T(2,128)}, f32[768]{0:T(1024)}, f32[768]{0:T(1024)}, /*index=5*/f32[768]{0...) custom-call(f32[96,768]{1,0:T(8,128)} %get-tuple-element.75.mix_ref,, ...), custom_call_target="tpu_custom_call" | custom-call | tf_op jit(solution)/shard_map/finish/pallas_call | solution.py:943
  (1 shorter events, 0.0 us)
